TPU v7x, 32 devices: a whole 2x2x4 slice. The times are simulated.
32 devices in a mesh: model: 4 (over z), data: 8 (over y, x, core).
Axes of the slice: x: 2, y: 2, z: 4, core: 2. Of those that a mesh axis runs over, the one named last changes fastest.
Arguments:
- emb_param: float32 [16384, 768], P('model', 'data')
- head_param: float32 [768, 16384], P('data', 'model')
- emb_grad: float32 [8, 16384, 768], P('data', 'model')
- head_grad: float32 [8, 768, 16384], P('data', None, 'model')
- emb_row: float32 [16384], P('model')
- emb_col: float32 [768], P('data')
- head_row: float32 [16384], P('model')
- head_col: float32 [768], P('data')
Outputs:
- output 1: float32 [16384, 768], P('model', 'data')
- output 2: float32 [768, 16384], P('data', 'model')
- output 3: float32 [16384], P('model')
- output 4: float32 [768], P('data')
- output 5: float32 [16384], P('model')
- output 6: float32 [768], P('data')
- output 7: bfloat16 [16384, 768], P('model', 'data')
- output 8: bfloat16 [768, 16384], P('data', 'model')
All inputs are finite; a program needn't handle non-finite values.
Results may differ from a plain program's by a relative error of at most 0.001.
Values sent between devices are 32-bit elements.
A program may use at most 1 GiB of HBM per device.

v0:
```python
import jax
import jax.numpy as jnp
from jax import lax
from jax.sharding import PartitionSpec as P

TRAIN_STEP = 10
DECAY_EXP = 0.8
EPS_ONE = 1e-30
CLIP_LIMIT = 1.0
SCALE_FLOOR = 1e-3
LEARN_RATE = float(TRAIN_STEP) ** -0.5
BETA_TWO = 1.0 - float(TRAIN_STEP) ** -DECAY_EXP


def apply_step(param, grad_sum, row_old, col_old, row_sq, col_sq, vocab_axis, vocab, embed):
    embed_axis = 1 - vocab_axis
    row_new = BETA_TWO * row_old + (1.0 - BETA_TWO) * (row_sq / embed)
    col_new = BETA_TWO * col_old + (1.0 - BETA_TWO) * (col_sq / vocab)
    row_mean = lax.psum(jnp.sum(row_new), "model") / vocab
    row_factor = jnp.expand_dims(lax.rsqrt(row_new), embed_axis)
    col_factor = jnp.expand_dims(lax.rsqrt(col_new) * jnp.sqrt(row_mean), vocab_axis)
    update = grad_sum * row_factor * col_factor
    update_rms = jnp.sqrt(lax.psum(jnp.sum(update * update), ("model", "data")) / (vocab * embed))
    param_rms = jnp.sqrt(lax.psum(jnp.sum(param * param), ("model", "data")) / (vocab * embed))
    step_size = LEARN_RATE * jnp.maximum(SCALE_FLOOR, param_rms) / jnp.maximum(1.0, update_rms / CLIP_LIMIT)
    return param - step_size * update, row_new, col_new


def block_update(param, grad_sum, row_old, col_old, vocab_axis, vocab, embed):
    embed_axis = 1 - vocab_axis
    grad_sq = grad_sum * grad_sum + EPS_ONE
    row_sq = lax.psum(jnp.sum(grad_sq, axis=embed_axis), "data")
    col_sq = lax.psum(jnp.sum(grad_sq, axis=vocab_axis), "model")
    return apply_step(param, grad_sum, row_old, col_old, row_sq, col_sq, vocab_axis, vocab, embed)


def solution(mesh):
    arg_specs = (P("model", "data"), P("data", "model"), P("data", "model", None), P("data", None, "model"),
                 P("model"), P("data"), P("model"), P("data"))
    result_specs = (P("model", "data"), P("data", "model"), P("model"), P("data"), P("model"), P("data"),
                    P("model", "data"), P("data", "model"))

    def update_tables(emb_param, head_param, emb_grad, head_grad, emb_row, emb_col, head_row, head_col):
        vocab = emb_param.shape[0]
        embed = emb_param.shape[1]

        def local_step(emb_block, head_block, emb_contrib, head_contrib, emb_rows, emb_cols, head_rows, head_cols):
            emb_sum = lax.psum_scatter(emb_contrib[0], "data", scatter_dimension=1, tiled=True)
            head_sum = lax.psum_scatter(head_contrib[0], "data", scatter_dimension=0, tiled=True)
            emb_new, emb_row_new, emb_col_new = block_update(emb_block, emb_sum, emb_rows, emb_cols, 0, vocab, embed)
            head_new, head_row_new, head_col_new = block_update(head_block, head_sum, head_rows, head_cols, 1, vocab, embed)
            return (emb_new, head_new, emb_row_new, emb_col_new, head_row_new, head_col_new,
                    emb_new.astype(jnp.bfloat16), head_new.astype(jnp.bfloat16))

        mapped = jax.shard_map(local_step, mesh=mesh, in_specs=arg_specs, out_specs=result_specs, check_vma=False)
        return mapped(emb_param, head_param, emb_grad, head_grad, emb_row, emb_col, head_row, head_col)

    return update_tables
```

profile of v0, /device:TPU:0, one launch (start us, length us, event | category | flops | bytes accessed | tf_op | source)
XLA Modules:
  0.0 304.2 jit_solution(17207369463311116713)
XLA Ops:
  7.2 0.0 reduce-scatter.3.cloned.1.call-start
  7.2 12.6 %copy.16 = f32[1,4096,768]{1,2,0:T(8,128)} copy(f32[1,4096,768]{2,1,0:T(8,128)} %param.10) | data formatting | bytes 25165824 | tf_op args[2]
  19.9 0.0 reduce-scatter.3.cloned.1.call-update
  19.9 0.0 reduce-scatter.5.cloned.1.call-start
  19.9 0.7 reduce-scatter.5.cloned.1.call-update
  20.6 0.7 copy-done.2
  21.3 1.0 multiply_reduce_fusion.1
  22.3 0.4 copy-done.3
  22.8 1.0 multiply_reduce_fusion.3
  23.8 89.9 %reduce-scatter.3.cloned.1.call-done = f32[4096,96]{0,1:T(8,128)} async-done(((f32[4096,768]{0,1:T(8,128)}), f32[4096,96]{0,1:T(8,128)}) %reduce-scatter.3.cloned.1.call-update) | async-done | bytes 1572880 | tf_op jit(solution)/shard_map/reduce_scatter | solution.py:48
  113.6 1.7 fusion.1
  115.4 92.6 %reduce-scatter.5.cloned.1.call-done = f32[96,4096]{1,0:T(8,128)} async-done(((f32[768,4096]{1,0:T(8,128)}), f32[96,4096]{1,0:T(8,128)}) %reduce-scatter.5.cloned.1.call-update) | async-done | bytes 1572880 | tf_op jit(solution)/shard_map/reduce_scatter | solution.py:49
  208.0 1.7 fusion.3
  209.7 22.8 %all-reduce.1 = (f32[4096]{0:T(1024)S(1)}, f32[4096]{0:T(1024)S(1)}) all-reduce(f32[4096]{0:T(1024)S(1)} %get-tuple-element.10, f32[4096]{0:T(1024)S(1)} %get-tuple-element.8), channel_id=1, replica_groups=mesh['model'=4,'data'=8] {'data'}, use_global_device_ids=true, to_apply=%region_4.0 | all-reduce | flops 8192 | bytes 65536 | tf_op jit(solution)/shard_map/psum | solution.py:32
  232.6 0.6 reduce_sum.93
  233.2 0.6 reduce_sum.98
  233.8 12.3 %all-reduce.2 = (f32[96]{0:T(128)S(1)}, f32[]{:T(128)}, f32[96]{0:T(128)S(1)}, f32[]{:T(128)}) all-reduce(f32[96]{0:T(128)S(1)} %get-tuple-element.11, f32[]{:T(128)} %reduce_sum.93, f32[96]{0:T(128)S(1)} %get-tuple-element.9, f32[]{:T(128)} %reduce_sum.98), channel_id=1, replica_groups=mesh['model'=4,'data'=8] {'model'}, use_global_device_ids=true, to_apply=%region_6.0 | all-reduce | flops 194 | bytes 1552 | tf_op jit(solution)/shard_map/psum | solution.py:33
  247.5 0.5 rsqrt_multiply_fusion
  248.0 0.5 rsqrt_multiply_fusion.1
  248.5 2.6 multiply_reduce_fusion
  251.1 1.1 multiply_reduce_fusion.2
  252.3 37.2 %all-reduce = (f32[]{:T(128)}, f32[]{:T(128)}, f32[]{:T(128)}, f32[]{:T(128)}) all-reduce(f32[]{:T(128)} %multiply_reduce_fusion.3, f32[]{:T(128)} %multiply_reduce_fusion.2, f32[]{:T(128)} %multiply_reduce_fusion.1, f32[]{:T(128)} %multiply_reduce_fusion), channel_id=1, replica_groups=mesh['model'=4,'data'=8] {'model','data'}, use_global_device_ids=true, to_apply=%region_1.0 | all-reduce | flops 4 | bytes 32 | tf_op jit(solution)/shard_map/psum | solution.py:24
  292.4 3.3 %fusion.4 = (bf16[96,4096]{1,0:T(8,128)(2,1)}, f32[96,4096]{1,0:T(8,128)}) fusion(f32[96,4096]{1,0:T(8,128)} %param.9, f32[96]{0:T(128)S(1)} %get-tuple-element.28, f32[96,4096]{1,0:T(8,128)S(1)} %copy-done.1, f32[4096]{0:T(1024)S(1)} %get-tuple-element.26, f32[]{:T(128)S(6)} %div.37), kind=kLoop, calls=%fused_computation.20 | loop fusion | flops 1966080 | bytes 5521796 | tf_op jit(solution)/shard_map/convert_element_type | solution.py:53
  295.6 1.8 fusion.5
  (21 shorter events, 0.1 us)
Async XLA Ops:
  7.2 106.5 %reduce-scatter.3.cloned.1.call-start = ((), (), s32[]{:S(2)}) async-start(), calls=%async_computation.2 | async-start | bytes 14155776 | tf_op jit(solution)/shard_map/reduce_scatter | solution.py:48
  19.9 188.1 %reduce-scatter.5.cloned.1.call-start = ((), (), s32[]{:S(2)}) async-start(), calls=%async_computation.3 | async-start | bytes 14155776 | tf_op jit(solution)/shard_map/reduce_scatter | solution.py:49
  19.9 1.4 copy-start.2
  21.3 1.4 copy-start.3
  23.8 208.8 %copy-start.7 = (f32[4096]{0:T(1024)S(1)}, f32[4096]{0:T(1024)}, u32[]{:S(2)}) copy-start(f32[4096]{0:T(1024)} %param.14) | copy-start | bytes 49156
  23.8 208.8 %copy-start.8 = (f32[4096]{0:T(1024)S(1)}, f32[4096]{0:T(1024)}, u32[]{:S(2)}) copy-start(f32[4096]{0:T(1024)} %param.12) | copy-start | bytes 49156
  23.8 223.7 %copy-start.9 = (f32[96]{0:T(128)S(1)}, f32[96]{0:T(128)}, u32[]{:S(2)}) copy-start(f32[96]{0:T(128)} %param.15) | copy-start | bytes 1156
  23.8 224.3 %copy-start.10 = (f32[96]{0:T(128)S(1)}, f32[96]{0:T(128)}, u32[]{:S(2)}) copy-start(f32[96]{0:T(128)} %param.13) | copy-start | bytes 1156
  115.4 135.8 %copy-start = (f32[4096,96]{0,1:T(8,128)S(1)}, f32[4096,96]{0,1:T(8,128)}, u32[]{:S(2)}) copy-start(f32[4096,96]{0,1:T(8,128)} %reduce-scatter.3.cloned.1.call-done) | copy-start | bytes 4718596
  232.6 19.7 %copy-start.5 = (f32[4096]{0:T(1024)}, f32[4096]{0:T(1024)S(1)}, u32[]{:S(2)}) copy-start(f32[4096]{0:T(1024)S(1)} %get-tuple-element.27) | copy-start | bytes 49156
  232.6 19.7 %copy-start.6 = (f32[4096]{0:T(1024)}, f32[4096]{0:T(1024)S(1)}, u32[]{:S(2)}) copy-start(f32[4096]{0:T(1024)S(1)} %get-tuple-element.35) | copy-start | bytes 49156
  248.5 43.8 %copy-start.1 = (f32[96,4096]{1,0:T(8,128)S(1)}, f32[96,4096]{1,0:T(8,128)}, u32[]{:S(2)}) copy-start(f32[96,4096]{1,0:T(8,128)} %reduce-scatter.5.cloned.1.call-done) | copy-start | bytes 4718596
  292.4 3.3 %copy-start.4 = (f32[4096,96]{0,1:T(8,128)S(1)}, f32[4096,96]{0,1:T(8,128)}, u32[]{:S(2)}) copy-start(f32[4096,96]{0,1:T(8,128)} %param.8) | copy-start | bytes 4718596
Sparse Core Ops, SparseCore 0:
  20.0 93.5 reduce-scatter.2
  117.1 90.8 reduce-scatter.4
where the time goes:
time: 305 us; the launch traced here: 304 us
  waiting for transfers between devices  183 us (60%)
  blocking collectives  72.3 us (24%)
  between operations  18.4 us (6%)
  other arithmetic  16.5 us (5%)
  local copies, waits for them, and re-layouts  13.8 us (5%)
    reduce_scatter x1, waiting for transfers between devices, local_step(): lax.psum_scatter(head_contrib[0], 'data', scatter_dimension=0, tiled=True)  92.6 us
    reduce_scatter x1, waiting for transfers between devices, local_step(): lax.psum_scatter(emb_contrib[0], 'data', scatter_dimension=1, tiled=True)  89.9 us
    psum x1, blocking collectives, apply_step(): lax.psum(jnp.sum(param * param), ('model', 'data')) / (vocab * embed)  37.2 us
    psum x1, blocking collectives, block_update(): row_sq = lax.psum(jnp.sum(grad_sq, axis=embed_axis), 'data')  22.8 us
    unnamed x23, local copies, waits for them, and re-layouts  13.8 us
    psum x1, blocking collectives, block_update(): col_sq = lax.psum(jnp.sum(grad_sq, axis=vocab_axis), 'model')  12.3 us
  transfers between devices with their start and end apart: 2, of which 2 were waited for; matrix products, arithmetic and copies ran while one was open for 1% of the time, Pallas kernels for 0%

commit v1 on v0

v1 whole, which is shorter than its diff:
```python
import functools

import jax
import jax.numpy as jnp
from jax import lax
from jax.experimental import pallas as pl
from jax.experimental.pallas import tpu as pltpu
from jax.sharding import PartitionSpec as P

TRAIN_STEP = 10
DECAY_EXP = 0.8
EPS_ONE = 1e-30
CLIP_LIMIT = 1.0
SCALE_FLOOR = 1e-3
LEARN_RATE = float(TRAIN_STEP) ** -0.5
BETA_TWO = 1.0 - float(TRAIN_STEP) ** -DECAY_EXP

VOCAB = 16384
EMBED = 768
ROWS = VOCAB // 4
COLS = EMBED // 8
CHUNKS = 8
WIDTH = ROWS // 2 // CHUNKS
LANES = 128
TILES = WIDTH // LANES
BLOCKS = 2 * CHUNKS
MESH = pl.DeviceIdType.MESH
PLANE = ((0, 1), (1, 0), (1, 1))


def exchange_kernel(emb_ref, head_ref, emb_p_ref, head_p_ref, emb_r_ref, head_r_ref, emb_c_ref, head_c_ref,
                    emb_out, head_out, row_out, small_out, scale_out,
                    own_e, in0_e, sum_e, sum_h, in0_h, in1_e, in1_h, in2_e, in2_h, peer_e, peer_h,
                    rows, stage_e, stage_h, par_e, par_h, rp_own, rp_in, col_acc, t_acc, rsum, psum, m_own, m_in, s_own, s_in,
                    ld_e, ld_h, s0e_s, s0e_r, s0h_s, s0h_r, s1e_s, s1e_r, s1h_s, s1h_r, s2e_s, s2e_r, s2h_s, s2h_r,
                    de_s, de_r, dh_s, dh_r, rp_s, rp_r, fw_s, fw_r, m_s, m_r, sc_s, sc_r, p_sem, out_sem):
    model = lax.axis_index("model")
    data = lax.axis_index("data")
    c = data % 2
    x = (data // 2) % 2
    y = data // 4
    oc, ox, oy = 1 - c, 1 - x, 1 - y

    def plane_id(fy, fx, fc):
        step = fy * (4 - 8 * y) + fx * (2 - 4 * x) + fc * (1 - 2 * c)
        return (model, data + step)

    def column_id(dz, fc):
        return ((model + dz) % 4, data + fc * (1 - 2 * c))

    core_peer, x_peer, y_peer = plane_id(0, 0, 1), plane_id(0, 1, 0), plane_id(1, 0, 0)

    def remote(src, dst, send, recv, peer):
        return pltpu.make_async_remote_copy(src_ref=src, dst_ref=dst, send_sem=send, recv_sem=recv,
                                            device_id=peer, device_id_type=MESH)

    def vocab_at(core, k):
        return pl.ds(pl.multiple_of(core * (ROWS // 2) + k * WIDTH, WIDTH), WIDTH)

    def load_e(k):
        return pltpu.make_async_copy(emb_ref.at[vocab_at(c, k), :], own_e.at[k], ld_e.at[k])

    def load_h(k):
        return pltpu.make_async_copy(head_ref.at[:, :, :, :, vocab_at(c, k)], sum_h.at[k], ld_h.at[k])

    def zero_e(k):
        return remote(emb_ref.at[vocab_at(oc, k), :], in0_e.at[k], s0e_s.at[k], s0e_r.at[k], core_peer)

    def zero_h(k):
        return remote(head_ref.at[:, :, :, :, vocab_at(oc, k)], in0_h.at[k], s0h_s.at[k], s0h_r.at[k], core_peer)

    def one_e(k):
        return remote(sum_e.at[k, oy], in1_e.at[k], s1e_s.at[k], s1e_r.at[k], y_peer)

    def one_h(k):
        return remote(sum_h.at[k, :, ox], in1_h.at[k], s1h_s.at[k], s1h_r.at[k], x_peer)

    def two_e(k):
        return remote(in1_e.at[k, ox], in2_e.at[k], s2e_s.at[k], s2e_r.at[k], x_peer)

    def two_h(k):
        return remote(in1_h.at[k, oy], in2_h.at[k], s2h_s.at[k], s2h_r.at[k], y_peer)

    def swap_e(k):
        return remote(in2_e.at[k, oc], peer_e.at[k], de_s.at[k], de_r.at[k], core_peer)

    def swap_h(k):
        return remote(in2_h.at[k, oc], peer_h.at[k], dh_s.at[k], dh_r.at[k], core_peer)

    def row_msg(k, i):
        fy, fx = PLANE[i]
        return remote(rp_own.at[k], rp_in.at[i, k], rp_s.at[i, k], rp_r.at[i, k], plane_id(fy, fx, 0))

    def row_fwd(k):
        return remote(rows.at[c * CHUNKS + k], rows.at[c * CHUNKS + k], fw_s.at[k], fw_r.at[k], core_peer)

    def row_fwd_in(k):
        return remote(rows.at[oc * CHUNKS + k], rows.at[oc * CHUNKS + k], fw_s.at[k], fw_r.at[k], core_peer)

    par_loads = (pltpu.make_async_copy(emb_p_ref, par_e, p_sem.at[0]), pltpu.make_async_copy(head_p_ref, par_h, p_sem.at[1]))

    for k in range(CHUNKS):
        load_e(k).start()
        load_h(k).start()

    barrier = pltpu.get_barrier_semaphore()
    greeted = 0
    for fy in range(2):
        for fx in range(2):
            for fc in range(2):
                if fy + fx + fc:
                    pl.semaphore_signal(barrier, inc=1, device_id=plane_id(fy, fx, fc), device_id_type=MESH)
                    greeted += 1
    for dz in range(1, 4):
        for fc in range(2):
            pl.semaphore_signal(barrier, inc=1, device_id=column_id(dz, fc), device_id_type=MESH)
            greeted += 1
    pl.semaphore_wait(barrier, greeted)

    for k in range(CHUNKS):
        zero_e(k).start()
        zero_h(k).start()
    for cp in par_loads:
        cp.start()

    col_acc[...] = jnp.zeros_like(col_acc)
    t_acc[...] = jnp.zeros_like(t_acc)
    rsum[...] = jnp.zeros_like(rsum)
    psum[...] = jnp.zeros_like(psum)

    def combine_cores(k):
        load_e(k).wait()
        zero_e(k).wait_recv()
        for j in range(EMBED // LANES):
            part = pl.ds(LANES * j, LANES)
            strip = (own_e[k, :, part] + in0_e[k, :, part]).T
            at = 0
            while at < LANES:
                eighth, row = divmod(LANES * j + at, COLS)
                size = min(LANES - at, COLS - row)
                sum_e[k, eighth // 4, eighth // 2 % 2, eighth % 2, row:row + size, :] = strip[at:at + size, :]
                at += size
        one_e(k).start()
        load_h(k).wait()
        zero_h(k).wait_recv()
        for a in range(2):
            for b in range(2):
                sum_h[k, a, b] = sum_h[k, a, b] + in0_h[k, a, b]
        one_h(k).start()

    def first_sum(k):
        one_e(k).wait_recv()
        in1_e[k, ox] = in1_e[k, ox] + sum_e[k, y, ox]
        two_e(k).start()
        in1_e[k, x] = in1_e[k, x] + sum_e[k, y, x]
        one_h(k).wait_recv()
        in1_h[k, oy] = in1_h[k, oy] + sum_h[k, oy, x]
        two_h(k).start()
        in1_h[k, y] = in1_h[k, y] + sum_h[k, y, x]

    def finish(k):
        two_e(k).wait_recv()
        for core in range(2):
            in2_e[k, core] = in2_e[k, core] + in1_e[k, x, core]
        swap_e(k).start()
        two_h(k).wait_recv()
        for core in range(2):
            in2_h[k, core] = in2_h[k, core] + in1_h[k, y, core]
        swap_h(k).start()
        for t, total in enumerate((in2_e, in2_h)):
            for i in range(TILES):
                row_part = jnp.zeros((1, LANES), jnp.float32)
                for core in range(2):
                    g = total[k, core, :, i * LANES:(i + 1) * LANES]
                    sq = g * g + EPS_ONE
                    col_acc[t, core] = col_acc[t, core] + sq
                    row_part = row_part + jnp.sum(sq, axis=0, keepdims=True)
                rp_own[k, t * TILES + i:t * TILES + i + 1, :] = row_part
        for i in range(3):
            row_msg(k, i).start()

    def row_stats(k):
        for i in range(3):
            row_msg(k, i).wait_recv()
        block = c * CHUNKS + k
        row_sq = (rp_own[k] + rp_in[0, k]) + (rp_in[1, k] + rp_in[2, k])
        old = jnp.concatenate([emb_r_ref[block], head_r_ref[block]], axis=0)
        row_new = BETA_TWO * old + (1.0 - BETA_TWO) * (row_sq / EMBED)
        rows[block] = row_new
        rsum[...] = rsum[...] + row_new
        inv = 1.0 / row_new
        for t, total in enumerate((in2_e, in2_h)):
            for i in range(TILES):
                r = inv[t * TILES + i:t * TILES + i + 1, :]
                for core in range(2):
                    g = total[k, core, :, i * LANES:(i + 1) * LANES]
                    t_acc[t, core] = t_acc[t, core] + (g * g) * r

    def out_e(block):
        at = pl.ds(pl.multiple_of(block * WIDTH, WIDTH), WIDTH)
        return pltpu.make_async_copy(stage_e.at[:, at], emb_out.at[:, at], out_sem.at[0])

    def out_h(block):
        at = pl.ds(pl.multiple_of(block * WIDTH, WIDTH), WIDTH)
        return pltpu.make_async_copy(stage_h.at[:, at], head_out.at[:, at], out_sem.at[1])

    def scale_rows(block, get_e, get_h):
        factor = lax.rsqrt(rows[block])
        base = pl.multiple_of(block * WIDTH, WIDTH)
        for i in range(TILES):
            lanes = slice(i * LANES, (i + 1) * LANES)
            at = pl.ds(base + i * LANES, LANES)
            stage_e[:, at] = get_e(lanes) * factor[i:i + 1, :]
            stage_h[:, at] = get_h(lanes) * factor[TILES + i:TILES + i + 1, :]
        out_e(block).start()
        out_h(block).start()

    def scale_own(k):
        scale_rows(c * CHUNKS + k, lambda lanes: in2_e[k, c, :, lanes], lambda lanes: in2_h[k, c, :, lanes])

    def scale_peer(k):
        row_fwd_in(k).wait_recv()
        swap_e(k).wait_recv()
        swap_h(k).wait_recv()
        scale_rows(oc * CHUNKS + k, lambda lanes: peer_e[k, :, lanes], lambda lanes: peer_h[k, :, lanes])

    def param_sq(k):
        size = ROWS // CHUNKS
        at = pl.ds(pl.multiple_of(k * size, size), size)
        for t, par in enumerate((par_e, par_h)):
            v = par[:, at]
            v = jnp.sum(v * v, axis=0, keepdims=True)
            for i in range(size // LANES):
                psum[t:t + 1, :] = psum[t:t + 1, :] + v[:, i * LANES:(i + 1) * LANES]

    combine_cores(0)
    for cp in par_loads:
        cp.wait()

    @pl.loop(0, CHUNKS)
    def _(k):
        @pl.when(k + 1 < CHUNKS)
        def _():
            combine_cores(k + 1)

        param_sq(k)
        first_sum(k)

        @pl.when(k >= 1)
        def _():
            finish(k - 1)

        @pl.when(k >= 2)
        def _():
            row_stats(k - 2)
            row_fwd(k - 2).start()
            scale_own(k - 2)

        @pl.when(k >= 3)
        def _():
            scale_peer(k - 3)

    finish(CHUNKS - 1)
    row_stats(CHUNKS - 2)
    row_fwd(CHUNKS - 2).start()
    row_stats(CHUNKS - 1)
    row_fwd(CHUNKS - 1).start()

    lane = lax.broadcasted_iota(jnp.int32, (1, LANES), 1)
    diag = lax.broadcasted_iota(jnp.int32, (COLS, LANES), 0) == lax.broadcasted_iota(jnp.int32, (COLS, LANES), 1)

    def as_row(acc):
        col = jnp.sum(acc, axis=1, keepdims=True)
        return jnp.sum(jnp.where(diag, col, 0.0), axis=0, keepdims=True)

    def total_of(v):
        return jnp.sum(jnp.sum(v, axis=1, keepdims=True), axis=0, keepdims=True)

    for t in range(2):
        r_part = total_of(rsum[t * TILES:(t + 1) * TILES, :])
        p_part = jnp.sum(psum[t:t + 1, :], axis=1, keepdims=True)
        for core in range(2):
            row = as_row(col_acc[t, core])
            row = jnp.where(lane == COLS, r_part, jnp.where(lane == COLS + 1, p_part, row))
            m_own[core, 2 * t:2 * t + 1, :] = row
            m_own[core, 2 * t + 1:2 * t + 2, :] = as_row(t_acc[t, core])

    columns = [(dz, fc) for dz in range(4) for fc in range(2) if dz + fc]

    def column_msg(i):
        dz, fc = columns[i]
        slot = columns.index(((4 - dz) % 4, fc))
        return remote(m_own.at[oc if fc else c], m_in.at[slot], m_s.at[i], m_r.at[slot], column_id(dz, fc))

    def column_msg_in(i):
        dz, fc = columns[i]
        return remote(m_own.at[c], m_in.at[i], m_s.at[i], m_r.at[i], column_id(dz, fc))

    for i in range(len(columns)):
        column_msg(i).start()

    scale_own(CHUNKS - 2)
    scale_own(CHUNKS - 1)
    for i in range(len(columns)):
        column_msg_in(i).wait_recv()

    total = m_own[c]
    for i in range(len(columns)):
        total = total + m_in[i]
    factors, means, message = [], [], jnp.zeros((1, LANES), jnp.float32)
    for t, c_ref in enumerate((emb_c_ref, head_c_ref)):
        cols = total[2 * t:2 * t + 1, :]
        r_mean = jnp.sum(jnp.where(lane == COLS, cols, 0.0), axis=1, keepdims=True) / VOCAB
        p_col = jnp.sum(jnp.where(lane == COLS + 1, cols, 0.0), axis=1, keepdims=True)
        col_new = BETA_TWO * c_ref[...] + (1.0 - BETA_TWO) * (cols[:, :COLS] / VOCAB)
        u_sq = jnp.sum(total[2 * t + 1:2 * t + 2, :COLS] * (r_mean / col_new), axis=1, keepdims=True)
        message = jnp.where(lane == 2 * t, u_sq, jnp.where(lane == 2 * t + 1, 0.5 * p_col, message))
        small_out[t:t + 1, :COLS] = col_new
        factors.append(lax.rsqrt(col_new) * jnp.sqrt(r_mean))
    s_own[...] = message

    flips = [(fy, fx, fc) for fy in range(2) for fx in range(2) for fc in range(2) if fy + fx + fc]

    def scalar_msg(i):
        return remote(s_own, s_in.at[i], sc_s.at[i], sc_r.at[i], plane_id(*flips[i]))

    for i in range(len(flips)):
        scalar_msg(i).start()
    square = diag[:, :COLS]
    factor_cols = [jnp.sum(jnp.where(square, factor, 0.0), axis=1, keepdims=True) for factor in factors]

    @pl.loop(CHUNKS - 3, CHUNKS)
    def _(k):
        scale_peer(k)

    row_out[...] = rows[...]
    for i in range(len(flips)):
        scalar_msg(i).wait_recv()
    message = s_own[...]
    for i in range(len(flips)):
        message = message + s_in[i]
    count = float(VOCAB * EMBED)
    steps = []
    for t in range(2):
        u_sq = jnp.sum(jnp.where(lane == 2 * t, message, 0.0), axis=1, keepdims=True)
        p_sq = jnp.sum(jnp.where(lane == 2 * t + 1, message, 0.0), axis=1, keepdims=True)
        u_rms = jnp.sqrt(u_sq / count)
        p_rms = jnp.sqrt(p_sq / count)
        steps.append(LEARN_RATE * jnp.maximum(SCALE_FLOOR, p_rms) / jnp.maximum(1.0, u_rms / CLIP_LIMIT))
    for t in range(2):
        scale_out[t] = jnp.broadcast_to(factor_cols[t] * steps[t], (COLS, LANES))

    @pl.loop(0, CHUNKS)
    def _(k):
        for make in (zero_e, zero_h, one_e, one_h, two_e, two_h, swap_e, swap_h, row_fwd):
            make(k).wait_send()
        for i in range(3):
            row_msg(k, i).wait_send()

    for i in range(len(columns)):
        column_msg(i).wait_send()
    for i in range(len(flips)):
        scalar_msg(i).wait_send()
    pltpu.make_async_copy(stage_e, emb_out, out_sem.at[0]).wait()
    pltpu.make_async_copy(stage_h, head_out, out_sem.at[1]).wait()


def update_kernel(emb_p, head_p, emb_g, head_g, rows, small, scale,
                  emb_new, head_new, emb_rows, head_rows, emb_cols, head_cols, emb_half, head_half):
    e_new = emb_p[...] - emb_g[...] * scale[0, :, 0:1]
    emb_new[...] = e_new
    emb_half[...] = e_new.astype(jnp.bfloat16)
    h_new = head_p[...] - head_g[...] * scale[1, :, 0:1]
    head_new[...] = h_new
    head_half[...] = h_new.astype(jnp.bfloat16)

    @pl.when(pl.program_id(0) == 0)
    def _():
        emb_rows[...] = rows[:, :TILES, :]
        head_rows[...] = rows[:, TILES:, :]
        emb_cols[...] = small[0:1, :COLS]
        head_cols[...] = small[1:2, :COLS]


def local_step(emb_p, head_p, emb_g, head_g, emb_r, emb_c, head_r, head_c):
    f32 = jnp.float32
    n, w = CHUNKS, WIDTH
    dma = pltpu.SemaphoreType.DMA
    hbm = pl.BlockSpec(memory_space=pl.ANY)
    vmem = pl.BlockSpec(memory_space=pltpu.VMEM)
    rows_shape = (BLOCKS, TILES, LANES)
    table = jax.ShapeDtypeStruct((COLS, ROWS), f32)
    half = jax.ShapeDtypeStruct((COLS, ROWS), jnp.bfloat16)
    emb_p = emb_p.T
    scratch = [
        pltpu.VMEM((n, w, EMBED), f32), pltpu.VMEM((n, w, EMBED), f32),
        pltpu.VMEM((n, 2, 2, 2, COLS, w), f32), pltpu.VMEM((n, 2, 2, 2, COLS, w), f32), pltpu.VMEM((n, 2, 2, 2, COLS, w), f32),
        pltpu.VMEM((n, 2, 2, COLS, w), f32), pltpu.VMEM((n, 2, 2, COLS, w), f32),
        pltpu.VMEM((n, 2, COLS, w), f32), pltpu.VMEM((n, 2, COLS, w), f32),
        pltpu.VMEM((n, COLS, w), f32), pltpu.VMEM((n, COLS, w), f32),
        pltpu.VMEM((BLOCKS, 2 * TILES, LANES), f32),
        pltpu.VMEM((COLS, ROWS), f32), pltpu.VMEM((COLS, ROWS), f32),
        pltpu.VMEM((COLS, ROWS), f32), pltpu.VMEM((COLS, ROWS), f32),
        pltpu.VMEM((n, 2 * TILES, LANES), f32), pltpu.VMEM((3, n, 2 * TILES, LANES), f32),
        pltpu.VMEM((2, 2, COLS, LANES), f32), pltpu.VMEM((2, 2, COLS, LANES), f32),
        pltpu.VMEM((2 * TILES, LANES), f32), pltpu.VMEM((2, LANES), f32),
        pltpu.VMEM((2, 4, LANES), f32), pltpu.VMEM((7, 4, LANES), f32),
        pltpu.VMEM((1, LANES), f32), pltpu.VMEM((7, 1, LANES), f32),
    ]
    scratch += [dma((n,))] * 18 + [dma((3, n))] * 2 + [dma((n,))] * 2 + [dma((7,))] * 4 + [dma((2,))] * 2
    emb_s, head_s, row_new, small, scale = pl.pallas_call(
        exchange_kernel,
        out_shape=(table, table, jax.ShapeDtypeStruct((BLOCKS, 2 * TILES, LANES), f32),
                   jax.ShapeDtypeStruct((2, LANES), f32), jax.ShapeDtypeStruct((2, COLS, LANES), f32)),
        in_specs=[hbm] * 4 + [vmem] * 4,
        out_specs=(hbm, hbm, vmem, vmem, vmem),
        scratch_shapes=scratch,
        compiler_params=pltpu.CompilerParams(collective_id=0, has_side_effects=True, vmem_limit_bytes=63 * 2 ** 20),
        name="exchange",
    )(emb_g.reshape(ROWS, EMBED), head_g.reshape(2, 2, 2, COLS, ROWS), emb_p, head_p,
      emb_r.reshape(rows_shape), head_r.reshape(rows_shape), emb_c.reshape(1, COLS), head_c.reshape(1, COLS))

    steps = 4
    part = ROWS // steps
    wide = pl.BlockSpec((COLS, part), lambda i: (0, i))

    def whole(*shape):
        return pl.BlockSpec(shape, lambda i: (0,) * len(shape))

    outs = pl.pallas_call(
        update_kernel,
        grid=(steps,),
        out_shape=(table, table,
                   jax.ShapeDtypeStruct(rows_shape, f32), jax.ShapeDtypeStruct(rows_shape, f32),
                   jax.ShapeDtypeStruct((1, COLS), f32), jax.ShapeDtypeStruct((1, COLS), f32),
                   half, half),
        in_specs=[wide] * 4 + [whole(BLOCKS, 2 * TILES, LANES), whole(2, LANES), whole(2, COLS, LANES)],
        out_specs=(wide, wide, whole(*rows_shape), whole(*rows_shape), whole(1, COLS), whole(1, COLS), wide, wide),
        name="update",
    )(emb_p, head_p, emb_s, head_s, row_new, small, scale)
    emb_new, head_new, emb_rn, head_rn, emb_cn, head_cn, emb_half, head_half = outs
    return (emb_new.T, head_new, emb_rn.reshape(ROWS), emb_cn.reshape(COLS), head_rn.reshape(ROWS),
            head_cn.reshape(COLS), emb_half.T, head_half)


def solution(mesh):
    arg_specs = (P("model", "data"), P("data", "model"), P("data", "model", None), P("data", None, "model"),
                 P("model"), P("data"), P("model"), P("data"))
    result_specs = (P("model", "data"), P("data", "model"), P("model"), P("data"), P("model"), P("data"),
                    P("model", "data"), P("data", "model"))
    mapped = jax.shard_map(local_step, mesh=mesh, in_specs=arg_specs, out_specs=result_specs, check_vma=False)

    def update_tables(emb_param, head_param, emb_grad, head_grad, emb_row, emb_col, head_row, head_col):
        return mapped(emb_param, head_param, emb_grad, head_grad, emb_row, emb_col, head_row, head_col)

    return update_tables
```

time: 305 us -> 133 us (0.44)
  waiting for transfers between devices: 183 us -> 0 us
  Pallas kernels: 0 us -> 132 us
  blocking collectives: 72.3 us -> 0 us
  between operations: 18.4 us -> 0.64 us
  other arithmetic: 16.5 us -> 0 us
  local copies, waits for them, and re-layouts: 13.8 us -> 0 us
    reduce_scatter x2 -> x0, waiting for transfers between devices: 182 us -> none  [the longest x1 92.6 us: local_step(): lax.psum_scatter(head_contrib[0], 'data', scatter_dimension=0, tiled=True)]
    pallas_call x0 -> x2, Pallas kernels: none -> 132 us  [the longest x1 126 us: local_step(): pl.pallas_call(exchange_kernel, out_shape=(table, table, jax.ShapeDtypeSt...]
    psum x3 -> x0, blocking collectives: 72.3 us -> none  [the longest x1 37.2 us: apply_step(): lax.psum(jnp.sum(param * param), ('model', 'data')) / (vocab * embed)]
    unnamed x23 -> x0, local copies, waits for them, and re-layouts: 13.8 us -> none
    reduce_sum x8 -> x0, other arithmetic: 10.4 us -> none  [the longest x2 3.74 us: apply_step(): jnp.sum(update * update)]
    convert_element_type x2 -> x0, other arithmetic: 5.03 us -> none  [the longest x1 3.28 us: local_step(): head_new.astype(jnp.bfloat16)]
  transfers between devices with their start and end apart: 2 -> 0, of which waited for: 2 -> 0; matrix products, arithmetic and copies ran while one was open for 1% -> 0% of each run, Pallas kernels for 0% -> 0%
where the time goes in v1:
time: 133 us; the launch traced here: 132 us
  Pallas kernels  132 us (99%)
    pallas_call x1, Pallas kernels, local_step(): pl.pallas_call(exchange_kernel, out_shape=(table, table, jax.ShapeDtypeSt...  126 us
    pallas_call x1, Pallas kernels, local_step(): pl.pallas_call(update_kernel, grid=(steps,), out_shape=(table, table, jax...  5.63 us

profile of v1, /device:TPU:0, one launch (start us, length us, event | category | flops | bytes accessed | tf_op | source)
XLA Modules:
  0.0 132.5 jit_solution(8609500466036976223)
XLA Ops:
  0.6 126.2 %exchange.1 = (f32[96,4096]{1,0:T(8,128)}, f32[96,4096]{1,0:T(8,128)}, f32[16,4,128]{2,1,0:T(4,128)}, f32[2,128]{1,0:T(2,128)}, f32[2,96,128]{2,1,0:T(8,128)}) custom-call(f32[4096,768]{1,0:T(8,128)} %bitcast.13, f32[2,2,2,96,4096]{4,3,2,1,0:T(8,128)} %bitcast.14, f32[96,4096]{1,0:T(8,128)} %bitcast.15, f32[96,4096]{1,0:T(8,128)} %head_p.1, ...), custom_call_target="tpu_custom_call" | custom-call | tf_op jit(solution)/shard_map/exchange/pallas_call | solution.py:411
  126.8 5.6 %update.1 = (f32[96,4096]{1,0:T(8,128)}, f32[96,4096]{1,0:T(8,128)}, f32[16,2,128]{2,1,0:T(2,128)}, f32[16,2,128]{2,1,0:T(2,128)}, f32[1,96]{1,0:T(1,128)}, /*in...) custom-call(f32[96,4096]{1,0:T(8,128)} %bitcast.16, f32[96,4096]{1,0:T(8,128)} %head_p.1, ...), custom_call_target="tpu_custom_call" | custom-call | tf_op jit(solution)/shard_map/update/pallas_call | solution.py:430

commit v2 on v1

--- a/solution.py
+++ b/solution.py
@@ -24,16 +24,17 @@
 LANES = 128
 TILES = WIDTH // LANES
 BLOCKS = 2 * CHUNKS
+PARTS = 4
 MESH = pl.DeviceIdType.MESH
 PLANE = ((0, 1), (1, 0), (1, 1))
 
 
 def exchange_kernel(emb_ref, head_ref, emb_p_ref, head_p_ref, emb_r_ref, head_r_ref, emb_c_ref, head_c_ref,
-                    emb_out, head_out, row_out, small_out, scale_out,
+                    stage_e, stage_h, par_e, par_h, emb_rows_out, head_rows_out, emb_cols_out, head_cols_out, scale_out,
                     own_e, in0_e, sum_e, sum_h, in0_h, in1_e, in1_h, in2_e, in2_h, peer_e, peer_h,
-                    rows, stage_e, stage_h, par_e, par_h, rp_own, rp_in, col_acc, t_acc, rsum, psum, m_own, m_in, s_own, s_in,
+                    rows, old_rows, old_cols, rp_own, rp_in, col_acc, t_acc, rsum, psum, m_own, m_in, s_own, s_in,
                     ld_e, ld_h, s0e_s, s0e_r, s0h_s, s0h_r, s1e_s, s1e_r, s1h_s, s1h_r, s2e_s, s2e_r, s2h_s, s2h_r,
-                    de_s, de_r, dh_s, dh_r, rp_s, rp_r, fw_s, fw_r, m_s, m_r, sc_s, sc_r, p_sem, out_sem):
+                    de_s, de_r, dh_s, dh_r, rp_s, rp_r, fw_s, fw_r, m_s, m_r, sc_s, sc_r, in_sem):
     model = lax.axis_index("model")
     data = lax.axis_index("data")
     c = data % 2
@@ -97,11 +98,9 @@
     def row_fwd_in(k):
         return remote(rows.at[oc * CHUNKS + k], rows.at[oc * CHUNKS + k], fw_s.at[k], fw_r.at[k], core_peer)
 
-    par_loads = (pltpu.make_async_copy(emb_p_ref, par_e, p_sem.at[0]), pltpu.make_async_copy(head_p_ref, par_h, p_sem.at[1]))
-
-    for k in range(CHUNKS):
-        load_e(k).start()
-        load_h(k).start()
+    small_loads = [pltpu.make_async_copy(src, dst, in_sem.at[i]) for i, (src, dst) in enumerate(
+        ((emb_p_ref, par_e), (head_p_ref, par_h), (emb_r_ref, old_rows.at[0]), (head_r_ref, old_rows.at[1]),
+         (emb_c_ref, old_cols.at[0]), (head_c_ref, old_cols.at[1])))]
 
     barrier = pltpu.get_barrier_semaphore()
     greeted = 0
@@ -115,12 +114,15 @@
         for fc in range(2):
             pl.semaphore_signal(barrier, inc=1, device_id=column_id(dz, fc), device_id_type=MESH)
             greeted += 1
+    for k in range(CHUNKS):
+        load_e(k).start()
+        load_h(k).start()
     pl.semaphore_wait(barrier, greeted)
 
     for k in range(CHUNKS):
         zero_e(k).start()
         zero_h(k).start()
-    for cp in par_loads:
+    for cp in small_loads:
         cp.start()
 
     col_acc[...] = jnp.zeros_like(col_acc)
@@ -184,7 +186,7 @@
             row_msg(k, i).wait_recv()
         block = c * CHUNKS + k
         row_sq = (rp_own[k] + rp_in[0, k]) + (rp_in[1, k] + rp_in[2, k])
-        old = jnp.concatenate([emb_r_ref[block], head_r_ref[block]], axis=0)
+        old = jnp.concatenate([old_rows[0, block], old_rows[1, block]], axis=0)
         row_new = BETA_TWO * old + (1.0 - BETA_TWO) * (row_sq / EMBED)
         rows[block] = row_new
         rsum[...] = rsum[...] + row_new
@@ -196,14 +198,6 @@
                     g = total[k, core, :, i * LANES:(i + 1) * LANES]
                     t_acc[t, core] = t_acc[t, core] + (g * g) * r
 
-    def out_e(block):
-        at = pl.ds(pl.multiple_of(block * WIDTH, WIDTH), WIDTH)
-        return pltpu.make_async_copy(stage_e.at[:, at], emb_out.at[:, at], out_sem.at[0])
-
-    def out_h(block):
-        at = pl.ds(pl.multiple_of(block * WIDTH, WIDTH), WIDTH)
-        return pltpu.make_async_copy(stage_h.at[:, at], head_out.at[:, at], out_sem.at[1])
-
     def scale_rows(block, get_e, get_h):
         factor = lax.rsqrt(rows[block])
         base = pl.multiple_of(block * WIDTH, WIDTH)
@@ -212,8 +206,6 @@
             at = pl.ds(base + i * LANES, LANES)
             stage_e[:, at] = get_e(lanes) * factor[i:i + 1, :]
             stage_h[:, at] = get_h(lanes) * factor[TILES + i:TILES + i + 1, :]
-        out_e(block).start()
-        out_h(block).start()
 
     def scale_own(k):
         scale_rows(c * CHUNKS + k, lambda lanes: in2_e[k, c, :, lanes], lambda lanes: in2_h[k, c, :, lanes])
@@ -234,7 +226,7 @@
                 psum[t:t + 1, :] = psum[t:t + 1, :] + v[:, i * LANES:(i + 1) * LANES]
 
     combine_cores(0)
-    for cp in par_loads:
+    for cp in small_loads:
         cp.wait()
 
     @pl.loop(0, CHUNKS)
@@ -308,14 +300,14 @@
     for i in range(len(columns)):
         total = total + m_in[i]
     factors, means, message = [], [], jnp.zeros((1, LANES), jnp.float32)
-    for t, c_ref in enumerate((emb_c_ref, head_c_ref)):
+    for t, c_out in enumerate((emb_cols_out, head_cols_out)):
         cols = total[2 * t:2 * t + 1, :]
         r_mean = jnp.sum(jnp.where(lane == COLS, cols, 0.0), axis=1, keepdims=True) / VOCAB
         p_col = jnp.sum(jnp.where(lane == COLS + 1, cols, 0.0), axis=1, keepdims=True)
-        col_new = BETA_TWO * c_ref[...] + (1.0 - BETA_TWO) * (cols[:, :COLS] / VOCAB)
+        col_new = BETA_TWO * old_cols[t] + (1.0 - BETA_TWO) * (cols[:, :COLS] / VOCAB)
         u_sq = jnp.sum(total[2 * t + 1:2 * t + 2, :COLS] * (r_mean / col_new), axis=1, keepdims=True)
         message = jnp.where(lane == 2 * t, u_sq, jnp.where(lane == 2 * t + 1, 0.5 * p_col, message))
-        small_out[t:t + 1, :COLS] = col_new
+        c_out[...] = col_new
         factors.append(lax.rsqrt(col_new) * jnp.sqrt(r_mean))
     s_own[...] = message
 
@@ -333,7 +325,8 @@
     def _(k):
         scale_peer(k)
 
-    row_out[...] = rows[...]
+    emb_rows_out[...] = rows[:, :TILES, :]
+    head_rows_out[...] = rows[:, TILES:, :]
     for i in range(len(flips)):
         scalar_msg(i).wait_recv()
     message = s_own[...]
@@ -361,32 +354,36 @@
         column_msg(i).wait_send()
     for i in range(len(flips)):
         scalar_msg(i).wait_send()
-    pltpu.make_async_copy(stage_e, emb_out, out_sem.at[0]).wait()
-    pltpu.make_async_copy(stage_h, head_out, out_sem.at[1]).wait()
-
-
-def update_kernel(emb_p, head_p, emb_g, head_g, rows, small, scale,
-                  emb_new, head_new, emb_rows, head_rows, emb_cols, head_cols, emb_half, head_half):
-    e_new = emb_p[...] - emb_g[...] * scale[0, :, 0:1]
-    emb_new[...] = e_new
-    emb_half[...] = e_new.astype(jnp.bfloat16)
-    h_new = head_p[...] - head_g[...] * scale[1, :, 0:1]
-    head_new[...] = h_new
-    head_half[...] = h_new.astype(jnp.bfloat16)
-
-    @pl.when(pl.program_id(0) == 0)
-    def _():
-        emb_rows[...] = rows[:, :TILES, :]
-        head_rows[...] = rows[:, TILES:, :]
-        emb_cols[...] = small[0:1, :COLS]
-        head_cols[...] = small[1:2, :COLS]
+
+
+def update_kernel(emb_g, head_g, emb_p, head_p, emb_rows, head_rows, emb_cols, head_cols, scale,
+                  emb_new, head_new, emb_rows_new, head_rows_new, emb_cols_new, head_cols_new, emb_half, head_half,
+                  new_buf, half_buf, small_sem, new_sem, half_sem):
+    small = [pltpu.make_async_copy(src, dst, small_sem.at[i]) for i, (src, dst) in enumerate(
+        ((emb_rows, emb_rows_new), (head_rows, head_rows_new), (emb_cols, emb_cols_new), (head_cols, head_cols_new)))]
+    for cp in small:
+        cp.start()
+    big = []
+    size = ROWS // PARTS
+    for i in range(PARTS):
+        part = slice(i * size, (i + 1) * size)
+        for t, (p, g, new, half) in enumerate(((emb_p, emb_g, emb_new, emb_half), (head_p, head_g, head_new, head_half))):
+            value = p[:, part] - g[:, part] * scale[t, :, 0:1]
+            new_buf[t, :, part] = value
+            half_buf[t, :, part] = value.astype(jnp.bfloat16)
+            big.append(pltpu.make_async_copy(new_buf.at[t, :, part], new.at[:, part], new_sem.at[t, i]))
+            big.append(pltpu.make_async_copy(half_buf.at[t, :, part], half.at[:, part], half_sem.at[t, i]))
+            big[-2].start()
+            big[-1].start()
+    for cp in small + big:
+        cp.wait()
 
 
 def local_step(emb_p, head_p, emb_g, head_g, emb_r, emb_c, head_r, head_c):
     f32 = jnp.float32
     n, w = CHUNKS, WIDTH
     dma = pltpu.SemaphoreType.DMA
-    hbm = pl.BlockSpec(memory_space=pl.ANY)
+    hbm = pl.BlockSpec(memory_space=pltpu.HBM)
     vmem = pl.BlockSpec(memory_space=pltpu.VMEM)
     rows_shape = (BLOCKS, TILES, LANES)
     table = jax.ShapeDtypeStruct((COLS, ROWS), f32)
@@ -399,45 +396,38 @@
         pltpu.VMEM((n, 2, COLS, w), f32), pltpu.VMEM((n, 2, COLS, w), f32),
         pltpu.VMEM((n, COLS, w), f32), pltpu.VMEM((n, COLS, w), f32),
         pltpu.VMEM((BLOCKS, 2 * TILES, LANES), f32),
-        pltpu.VMEM((COLS, ROWS), f32), pltpu.VMEM((COLS, ROWS), f32),
-        pltpu.VMEM((COLS, ROWS), f32), pltpu.VMEM((COLS, ROWS), f32),
+        pltpu.VMEM((2, BLOCKS, TILES, LANES), f32), pltpu.VMEM((2, 1, COLS), f32),
         pltpu.VMEM((n, 2 * TILES, LANES), f32), pltpu.VMEM((3, n, 2 * TILES, LANES), f32),
         pltpu.VMEM((2, 2, COLS, LANES), f32), pltpu.VMEM((2, 2, COLS, LANES), f32),
         pltpu.VMEM((2 * TILES, LANES), f32), pltpu.VMEM((2, LANES), f32),
         pltpu.VMEM((2, 4, LANES), f32), pltpu.VMEM((7, 4, LANES), f32),
         pltpu.VMEM((1, LANES), f32), pltpu.VMEM((7, 1, LANES), f32),
     ]
-    scratch += [dma((n,))] * 18 + [dma((3, n))] * 2 + [dma((n,))] * 2 + [dma((7,))] * 4 + [dma((2,))] * 2
-    emb_s, head_s, row_new, small, scale = pl.pallas_call(
+    scratch += [dma((n,))] * 18 + [dma((3, n))] * 2 + [dma((n,))] * 2 + [dma((7,))] * 4 + [dma((6,))]
+    kept = [pltpu.VMEM((COLS, ROWS), f32)] * 4 + [pltpu.VMEM(rows_shape, f32)] * 2 + [pltpu.VMEM((1, COLS), f32)] * 2
+    kept.append(pltpu.VMEM((2, COLS, LANES), f32))
+    state = pl.pallas_call(
         exchange_kernel,
-        out_shape=(table, table, jax.ShapeDtypeStruct((BLOCKS, 2 * TILES, LANES), f32),
-                   jax.ShapeDtypeStruct((2, LANES), f32), jax.ShapeDtypeStruct((2, COLS, LANES), f32)),
-        in_specs=[hbm] * 4 + [vmem] * 4,
-        out_specs=(hbm, hbm, vmem, vmem, vmem),
+        out_shape=tuple(kept),
+        in_specs=[hbm] * 8,
+        out_specs=(vmem,) * 9,
         scratch_shapes=scratch,
-        compiler_params=pltpu.CompilerParams(collective_id=0, has_side_effects=True, vmem_limit_bytes=63 * 2 ** 20),
+        compiler_params=pltpu.CompilerParams(collective_id=0, has_side_effects=True, vmem_limit_bytes=60_000_000),
         name="exchange",
     )(emb_g.reshape(ROWS, EMBED), head_g.reshape(2, 2, 2, COLS, ROWS), emb_p, head_p,
       emb_r.reshape(rows_shape), head_r.reshape(rows_shape), emb_c.reshape(1, COLS), head_c.reshape(1, COLS))
 
-    steps = 4
-    part = ROWS // steps
-    wide = pl.BlockSpec((COLS, part), lambda i: (0, i))
-
-    def whole(*shape):
-        return pl.BlockSpec(shape, lambda i: (0,) * len(shape))
-
     outs = pl.pallas_call(
         update_kernel,
-        grid=(steps,),
-        out_shape=(table, table,
-                   jax.ShapeDtypeStruct(rows_shape, f32), jax.ShapeDtypeStruct(rows_shape, f32),
-                   jax.ShapeDtypeStruct((1, COLS), f32), jax.ShapeDtypeStruct((1, COLS), f32),
-                   half, half),
-        in_specs=[wide] * 4 + [whole(BLOCKS, 2 * TILES, LANES), whole(2, LANES), whole(2, COLS, LANES)],
-        out_specs=(wide, wide, whole(*rows_shape), whole(*rows_shape), whole(1, COLS), whole(1, COLS), wide, wide),
+        out_shape=(table, table, jax.ShapeDtypeStruct(rows_shape, f32), jax.ShapeDtypeStruct(rows_shape, f32),
+                   jax.ShapeDtypeStruct((1, COLS), f32), jax.ShapeDtypeStruct((1, COLS), f32), half, half),
+        in_specs=[vmem] * 9,
+        out_specs=(hbm,) * 8,
+        scratch_shapes=[pltpu.VMEM((2, COLS, ROWS), f32), pltpu.VMEM((2, COLS, ROWS), jnp.bfloat16),
+                        dma((4,)), dma((2, PARTS)), dma((2, PARTS))],
+        compiler_params=pltpu.CompilerParams(vmem_limit_bytes=16 * 2 ** 20),
         name="update",
-    )(emb_p, head_p, emb_s, head_s, row_new, small, scale)
+    )(*state)
     emb_new, head_new, emb_rn, head_rn, emb_cn, head_cn, emb_half, head_half = outs
     return (emb_new.T, head_new, emb_rn.reshape(ROWS), emb_cn.reshape(COLS), head_rn.reshape(ROWS),
             head_cn.reshape(COLS), emb_half.T, head_half)

time: 133 us -> 128 us (0.962)
  Pallas kernels: 132 us -> 127 us
    pallas_call x2, Pallas kernels: 132 us -> 127 us  [the longest x1 125 us: local_step(): pl.pallas_call(exchange_kernel, out_shape=tuple(kept), in_specs=[hbm] * 8...]
where the time goes in v2:
time: 128 us
  Pallas kernels  127 us (99%)
    pallas_call x1, Pallas kernels, local_step(): pl.pallas_call(exchange_kernel, out_shape=tuple(kept), in_specs=[hbm] * 8...  125 us

profile of v2, /device:TPU:0, one launch (start us, length us, event | category | flops | bytes accessed | tf_op | source)
XLA Modules:
  0.0 128.0 jit_solution(968757989361135340)
XLA Ops:
  0.6 124.8 %exchange.1 = (f32[96,4096]{1,0:T(8,128)S(1)}, f32[96,4096]{1,0:T(8,128)S(1)}, f32[96,4096]{1,0:T(8,128)S(1)}, f32[96,4096]{1,0:T(8,128)S(1)}, f32[16,2,128]{2,1...) custom-call(f32[4096,768]{1,0:T(8,128)} %bitcast.13, ...), custom_call_target="tpu_custom_call" | custom-call | tf_op jit(solution)/shard_map/exchange/pallas_call | solution.py:409
  125.5 2.5 %update.1 = (f32[96,4096]{1,0:T(8,128)}, f32[96,4096]{1,0:T(8,128)}, f32[16,2,128]{2,1,0:T(2,128)}, f32[16,2,128]{2,1,0:T(2,128)}, f32[1,96]{1,0:T(1,128)}, /*in...) custom-call(f32[96,4096]{1,0:T(8,128)S(1)} %get-tuple-element.25.emb_g, ...), custom_call_target="tpu_custom_call" | custom-call | tf_op jit(solution)/shard_map/update/pallas_call | solution.py:420

commit v3 on v2

v3 whole, which is shorter than its diff:
```python
import functools

import jax
import jax.numpy as jnp
from jax import lax
from jax.experimental import pallas as pl
from jax.experimental.pallas import tpu as pltpu
from jax.sharding import PartitionSpec as P

TRAIN_STEP = 10
DECAY_EXP = 0.8
EPS_ONE = 1e-30
CLIP_LIMIT = 1.0
SCALE_FLOOR = 1e-3
LEARN_RATE = float(TRAIN_STEP) ** -0.5
BETA_TWO = 1.0 - float(TRAIN_STEP) ** -DECAY_EXP

VOCAB = 16384
EMBED = 768
ROWS = VOCAB // 4
COLS = EMBED // 8
LANES = 128
CHUNKS = ROWS // 2 // LANES
GROUPS = ((0, 1), (1, 1), (2, 2), (4, 4), (8, 8))
PAIRS = CHUNKS // 2
BLOCKS = 2 * PAIRS
RING = 4
PARTS = 4
MESH = pl.DeviceIdType.MESH
PLANE = ((0, 1), (1, 0), (1, 1))


def exchange_kernel(emb_ref, head_ref, emb_p_ref, head_p_ref, emb_r_ref, head_r_ref, emb_c_ref, head_c_ref,
                    stage_e, stage_h, par_e, par_h, emb_rows_out, head_rows_out, emb_cols_out, head_cols_out, scale_out,
                    own_e, in0_e, sum_e, sum_h, in0_h, in1_e, in1_h, in2_e, in2_h, peer,
                    rows, old_rows, old_cols, rp_own, rp_in, col_acc, t_acc, rsum, psum, m_own, m_in, s_own, s_in,
                    ld_e, ld_h, s0e_r, s0h_r, s1e_r, s1h_r, s2e_r, s2h_r, swap_r, rp_r, fw_r, send, last_r, in_sem):
    model = lax.axis_index("model")
    data = lax.axis_index("data")
    c = data % 2
    x = (data // 2) % 2
    y = data // 4
    oc, ox, oy = 1 - c, 1 - x, 1 - y

    def plane_id(fy, fx, fc):
        step = fy * (4 - 8 * y) + fx * (2 - 4 * x) + fc * (1 - 2 * c)
        return (model, data + step)

    def column_id(dz, fc):
        return ((model + dz) % 4, data + fc * (1 - 2 * c))

    core_peer, x_peer, y_peer = plane_id(0, 0, 1), plane_id(0, 1, 0), plane_id(1, 0, 0)

    def remote(src, dst, send_sem, recv_sem, peer_id):
        return pltpu.make_async_remote_copy(src_ref=src, dst_ref=dst, send_sem=send_sem, recv_sem=recv_sem,
                                            device_id=peer_id, device_id_type=MESH)

    def arrived(ref, sem):
        pltpu.make_async_copy(ref, ref, sem).wait()

    def vocab_at(core, first, count):
        return pl.ds(pl.multiple_of(core * (ROWS // 2) + first * LANES, LANES), count * LANES)

    half_of = 4 * COLS

    def first_e(q):
        cols = pl.ds(pl.multiple_of((oy if q == 0 else y) * half_of, LANES), half_of)
        return (pltpu.make_async_copy(emb_ref.at[vocab_at(c, 0, 1), cols], own_e.at[0:LANES, cols], ld_e.at[q]),
                remote(emb_ref.at[vocab_at(oc, 0, 1), cols], in0_e.at[0:LANES, cols], send.at[0], s0e_r.at[q], core_peer))

    def first_h(q):
        part = ox if q == 0 else x
        return (pltpu.make_async_copy(head_ref.at[:, part, :, :, vocab_at(c, 0, 1)], sum_h.at[0, :, part], ld_h.at[q]),
                remote(head_ref.at[:, part, :, :, vocab_at(oc, 0, 1)], in0_h.at[0, :, part], send.at[1], s0h_r.at[q], core_peer))

    def group_e(i):
        first, count = GROUPS[i]
        at = slice(first * LANES, (first + count) * LANES)
        return (pltpu.make_async_copy(emb_ref.at[vocab_at(c, first, count), :], own_e.at[at, :], ld_e.at[i + 1]),
                remote(emb_ref.at[vocab_at(oc, first, count), :], in0_e.at[at, :], send.at[0], s0e_r.at[i + 1], core_peer))

    def group_h(i):
        first, count = GROUPS[i]
        pairs = []
        for j in range(first, first + count):
            pairs.append((pltpu.make_async_copy(head_ref.at[:, :, :, :, vocab_at(c, j, 1)], sum_h.at[j], ld_h.at[i + 1]),
                          remote(head_ref.at[:, :, :, :, vocab_at(oc, j, 1)], in0_h.at[j], send.at[1], s0h_r.at[i + 1],
                                 core_peer)))
        return pairs

    def one_e(k):
        return remote(sum_e.at[k, oy], in1_e.at[k], send.at[2], s1e_r.at[k % RING], y_peer)

    def one_h(k):
        return remote(sum_h.at[k, :, ox], in1_h.at[k], send.at[3], s1h_r.at[k % RING], x_peer)

    def two_e(k):
        return remote(in1_e.at[k, ox], in2_e.at[k], send.at[4], s2e_r.at[k % RING], x_peer)

    def two_h(k):
        return remote(in1_h.at[k, oy], in2_h.at[k], send.at[5], s2h_r.at[k % RING], y_peer)

    def swap(q):
        return [remote(total.at[pl.ds(2 * q, 2), oc], peer.at[q, t], send.at[6], swap_r.at[q], core_peer)
                for t, total in enumerate((in2_e, in2_h))]

    def row_msg(q, i):
        fy, fx = PLANE[i]
        return remote(rp_own.at[q], rp_in.at[q, i], send.at[7], rp_r.at[q], plane_id(fy, fx, 0))

    def row_fwd(q):
        return remote(rows.at[c * PAIRS + q], rows.at[c * PAIRS + q], send.at[8], fw_r.at[q], core_peer)

    small_loads = [pltpu.make_async_copy(src, dst, in_sem.at[i]) for i, (src, dst) in (
        (0, (emb_p_ref, par_e)), (1, (head_p_ref, par_h)), (2, (emb_r_ref, old_rows.at[0])), (2, (head_r_ref, old_rows.at[1])),
        (3, (emb_c_ref, old_cols.at[0])), (3, (head_c_ref, old_cols.at[1])))]

    barrier = pltpu.get_barrier_semaphore()
    greeted = 0
    for fy in range(2):
        for fx in range(2):
            for fc in range(2):
                if fy + fx + fc:
                    pl.semaphore_signal(barrier, inc=1, device_id=plane_id(fy, fx, fc), device_id_type=MESH)
                    greeted += 1
    for dz in range(1, 4):
        for fc in range(2):
            pl.semaphore_signal(barrier, inc=1, device_id=column_id(dz, fc), device_id_type=MESH)
            greeted += 1
    for q in range(2):
        first_e(q)[0].start()
        first_h(q)[0].start()
    for i in range(1, len(GROUPS)):
        group_e(i)[0].start()
        for cp, _ in group_h(i):
            cp.start()
    pl.semaphore_wait(barrier, greeted)

    for q in range(2):
        first_e(q)[1].start()
        first_h(q)[1].start()
    for i in range(1, len(GROUPS)):
        group_e(i)[1].start()
        for _, cp in group_h(i):
            cp.start()
    for cp in small_loads:
        cp.start()

    col_acc[...] = jnp.zeros_like(col_acc)
    t_acc[...] = jnp.zeros_like(t_acc)
    rsum[...] = jnp.zeros_like(rsum)
    psum[...] = jnp.zeros_like(psum)

    def flip_e(k, half):
        at = pl.ds(pl.multiple_of(k * LANES, LANES), LANES)
        for j in range(half_of // LANES):
            cols = pl.ds(pl.multiple_of(half * half_of + j * LANES, LANES), LANES)
            strip = (own_e[at, cols] + in0_e[at, cols]).T
            done = 0
            while done < LANES:
                block, row = divmod(LANES * j + done, COLS)
                size = min(LANES - done, COLS - row)
                sum_e[k, half, block // 2, block % 2, row:row + size, :] = strip[done:done + size, :]
                done += size

    def add_h(k, part):
        for a in range(2):
            for b in range(2):
                sum_h[k, a, part, b] = sum_h[k, a, part, b] + in0_h[k, a, part, b]

    def combine_cores(k):
        flip_e(k, oy)
        one_e(k).start()
        add_h(k, ox)
        one_h(k).start()
        flip_e(k, y)
        add_h(k, x)

    def first_sum(k):
        one_e(k).wait_recv()
        in1_e[k, ox] = in1_e[k, ox] + sum_e[k, y, ox]
        two_e(k).start()
        in1_e[k, x] = in1_e[k, x] + sum_e[k, y, x]
        one_h(k).wait_recv()
        in1_h[k, oy] = in1_h[k, oy] + sum_h[k, oy, x]
        two_h(k).start()
        in1_h[k, y] = in1_h[k, y] + sum_h[k, y, x]

    def finish(k, q, i):
        two_e(k).wait_recv()
        for core in range(2):
            in2_e[k, core] = in2_e[k, core] + in1_e[k, x, core]
        two_h(k).wait_recv()
        for core in range(2):
            in2_h[k, core] = in2_h[k, core] + in1_h[k, y, core]
        for t, total in enumerate((in2_e, in2_h)):
            row_part = jnp.zeros((1, LANES), jnp.float32)
            for core in range(2):
                g = total[k, core]
                sq = g * g + EPS_ONE
                col_acc[t, core] = col_acc[t, core] + sq
                row_part = row_part + jnp.sum(sq, axis=0, keepdims=True)
            rp_own[q, 2 * t + i:2 * t + i + 1, :] = row_part

    def publish(q):
        for i in range(3):
            row_msg(q, i).start()
        for cp in swap(q):
            cp.start()

    def row_stats(q):
        arrived(rp_in.at[q], rp_r.at[q])
        block = c * PAIRS + q
        row_sq = (rp_own[q] + rp_in[q, 0]) + (rp_in[q, 1] + rp_in[q, 2])
        old = jnp.concatenate([old_rows[0, block], old_rows[1, block]], axis=0)
        row_new = BETA_TWO * old + (1.0 - BETA_TWO) * (row_sq / EMBED)
        rows[block] = row_new
        rsum[...] = rsum[...] + row_new
        inv = 1.0 / row_new
        for t, total in enumerate((in2_e, in2_h)):
            for core in range(2):
                acc = t_acc[t, core]
                for i in range(2):
                    g = total[2 * q + i, core]
                    acc = acc + (g * g) * inv[2 * t + i:2 * t + i + 1, :]
                t_acc[t, core] = acc

    def scale_rows(block, get):
        factor = lax.rsqrt(rows[block])
        base = pl.multiple_of(block * (2 * LANES), 2 * LANES)
        for t, stage in enumerate((stage_e, stage_h)):
            for i in range(2):
                stage[:, pl.ds(base + i * LANES, LANES)] = get(t, i) * factor[2 * t + i:2 * t + i + 1, :]

    def scale_own(q):
        totals = (in2_e, in2_h)
        scale_rows(c * PAIRS + q, lambda t, i: totals[t][2 * q + i, c])

    def scale_peer(q):
        arrived(rows.at[oc * PAIRS + q], fw_r.at[q])
        arrived(peer.at[q], swap_r.at[q])
        scale_rows(oc * PAIRS + q, lambda t, i: peer[q, t, i])

    def param_sq(k):
        size = ROWS // CHUNKS
        at = pl.ds(pl.multiple_of(k * size, size), size)
        for t, par in enumerate((par_e, par_h)):
            v = par[:, at]
            v = jnp.sum(v * v, axis=0, keepdims=True)
            for i in range(size // LANES):
                psum[t:t + 1, :] = psum[t:t + 1, :] + v[:, i * LANES:(i + 1) * LANES]

    for q in range(2):
        load, cross = first_e(q)
        load.wait()
        cross.wait_recv()
        flip_e(0, oy if q == 0 else y)
        if q == 0:
            one_e(0).start()
        load, cross = first_h(q)
        load.wait()
        cross.wait_recv()
        add_h(0, ox if q == 0 else x)
        if q == 0:
            one_h(0).start()
    arrived(par_e, in_sem.at[0])
    arrived(par_h, in_sem.at[1])
    arrived(old_rows, in_sem.at[2])
    arrived(old_cols, in_sem.at[3])

    @pl.loop(0, CHUNKS)
    def _(k):
        for i in range(1, len(GROUPS)):
            first, count = GROUPS[i]

            @pl.when(k + 1 == first)
            def _():
                at = slice(first * LANES, (first + count) * LANES)
                arrived(own_e.at[at, :], ld_e.at[i + 1])
                arrived(in0_e.at[at, :], s0e_r.at[i + 1])
                arrived(sum_h.at[first:first + count], ld_h.at[i + 1])
                arrived(in0_h.at[first:first + count], s0h_r.at[i + 1])

        @pl.when(k + 1 < CHUNKS)
        def _():
            combine_cores(k + 1)

        param_sq(k)
        first_sum(k)
        pair = k // 2

        @pl.when((k >= 1) & (k % 2 == 1))
        def _():
            finish(k - 1, pair, 0)

        @pl.when((k >= 2) & (k % 2 == 0))
        def _():
            finish(k - 1, pair - 1, 1)
            publish(pair - 1)

        @pl.when((k >= 4) & (k % 2 == 0))
        def _():
            row_stats(pair - 2)
            row_fwd(pair - 2).start()
            scale_own(pair - 2)

        @pl.when((k >= 6) & (k % 2 == 0))
        def _():
            scale_peer(pair - 3)

    finish(CHUNKS - 1, PAIRS - 1, 1)
    publish(PAIRS - 1)
    row_stats(PAIRS - 2)
    row_fwd(PAIRS - 2).start()
    row_stats(PAIRS - 1)
    row_fwd(PAIRS - 1).start()

    lane = lax.broadcasted_iota(jnp.int32, (1, LANES), 1)
    diag = lax.broadcasted_iota(jnp.int32, (COLS, LANES), 0) == lax.broadcasted_iota(jnp.int32, (COLS, LANES), 1)

    def as_row(acc):
        col = jnp.sum(acc, axis=1, keepdims=True)
        return jnp.sum(jnp.where(diag, col, 0.0), axis=0, keepdims=True)

    def total_of(v):
        return jnp.sum(jnp.sum(v, axis=1, keepdims=True), axis=0, keepdims=True)

    for t in range(2):
        r_part = total_of(rsum[2 * t:2 * t + 2, :])
        p_part = jnp.sum(psum[t:t + 1, :], axis=1, keepdims=True)
        for core in range(2):
            row = as_row(col_acc[t, core])
            row = jnp.where(lane == COLS, r_part, jnp.where(lane == COLS + 1, p_part, row))
            m_own[core, 2 * t:2 * t + 1, :] = row
            m_own[core, 2 * t + 1:2 * t + 2, :] = as_row(t_acc[t, core])

    columns = [(dz, fc) for dz in range(4) for fc in range(2) if dz + fc]

    def column_msg(i):
        dz, fc = columns[i]
        slot = columns.index(((4 - dz) % 4, fc))
        return remote(m_own.at[oc if fc else c], m_in.at[slot], send.at[9], last_r.at[0], column_id(dz, fc))

    for i in range(len(columns)):
        column_msg(i).start()

    scale_own(PAIRS - 2)
    scale_own(PAIRS - 1)
    arrived(m_in, last_r.at[0])

    total = m_own[c]
    for i in range(len(columns)):
        total = total + m_in[i]
    factors, message = [], jnp.zeros((1, LANES), jnp.float32)
    for t, c_out in enumerate((emb_cols_out, head_cols_out)):
        cols = total[2 * t:2 * t + 1, :]
        r_mean = jnp.sum(jnp.where(lane == COLS, cols, 0.0), axis=1, keepdims=True) / VOCAB
        p_col = jnp.sum(jnp.where(lane == COLS + 1, cols, 0.0), axis=1, keepdims=True)
        col_new = BETA_TWO * old_cols[t] + (1.0 - BETA_TWO) * (cols[:, :COLS] / VOCAB)
        u_sq = jnp.sum(total[2 * t + 1:2 * t + 2, :COLS] * (r_mean / col_new), axis=1, keepdims=True)
        message = jnp.where(lane == 2 * t, u_sq, jnp.where(lane == 2 * t + 1, 0.5 * p_col, message))
        c_out[...] = col_new
        factors.append(lax.rsqrt(col_new) * jnp.sqrt(r_mean))
    s_own[...] = message

    flips = [(fy, fx, fc) for fy in range(2) for fx in range(2) for fc in range(2) if fy + fx + fc]

    def scalar_msg(i):
        return remote(s_own, s_in.at[i], send.at[10], last_r.at[1], plane_id(*flips[i]))

    for i in range(len(flips)):
        scalar_msg(i).start()
    square = diag[:, :COLS]
    factor_cols = [jnp.sum(jnp.where(square, factor, 0.0), axis=1, keepdims=True) for factor in factors]

    @pl.loop(PAIRS - 3, PAIRS)
    def _(q):
        scale_peer(q)

    emb_rows_out[...] = rows[:, :2, :]
    head_rows_out[...] = rows[:, 2:, :]
    arrived(in0_e, send.at[0])
    arrived(in0_h, send.at[1])
    arrived(in1_e, send.at[2])
    arrived(in1_h, send.at[3])
    arrived(in2_e, send.at[4])
    arrived(in2_h, send.at[5])
    arrived(peer, send.at[6])
    arrived(rp_in, send.at[7])
    arrived(rows.at[0:PAIRS], send.at[8])
    arrived(m_in, send.at[9])
    arrived(s_in, last_r.at[1])
    message = s_own[...]
    for i in range(len(flips)):
        message = message + s_in[i]
    count = float(VOCAB * EMBED)
    for t in range(2):
        u_sq = jnp.sum(jnp.where(lane == 2 * t, message, 0.0), axis=1, keepdims=True)
        p_sq = jnp.sum(jnp.where(lane == 2 * t + 1, message, 0.0), axis=1, keepdims=True)
        u_rms = jnp.sqrt(u_sq / count)
        p_rms = jnp.sqrt(p_sq / count)
        step = LEARN_RATE * jnp.maximum(SCALE_FLOOR, p_rms) / jnp.maximum(1.0, u_rms / CLIP_LIMIT)
        scale_out[t] = jnp.broadcast_to(factor_cols[t] * step, (COLS, LANES))
    arrived(s_in, send.at[10])


def update_kernel(emb_g, head_g, emb_p, head_p, emb_rows, head_rows, emb_cols, head_cols, scale,
                  emb_new, head_new, emb_rows_new, head_rows_new, emb_cols_new, head_cols_new, emb_half, head_half,
                  new_buf, half_buf, small_sem, big_sem):
    small = [pltpu.make_async_copy(src, dst, small_sem.at[i]) for i, (src, dst) in enumerate(
        ((emb_rows, emb_rows_new), (head_rows, head_rows_new), (emb_cols, emb_cols_new), (head_cols, head_cols_new)))]
    for cp in small:
        cp.start()
    size = ROWS // PARTS
    for i in range(PARTS):
        part = slice(i * size, (i + 1) * size)
        for t, (p, g, new, half) in enumerate(((emb_p, emb_g, emb_new, emb_half), (head_p, head_g, head_new, head_half))):
            value = p[:, part] - g[:, part] * scale[t, :, 0:1]
            new_buf[t, :, part] = value
            half_buf[t, :, part] = value.astype(jnp.bfloat16)
            pltpu.make_async_copy(new_buf.at[t, :, part], new.at[:, part], big_sem.at[0]).start()
            pltpu.make_async_copy(half_buf.at[t, :, part], half.at[:, part], big_sem.at[1]).start()
    for cp in small:
        cp.wait()
    pltpu.make_async_copy(new_buf, new_buf, big_sem.at[0]).wait()
    pltpu.make_async_copy(half_buf, half_buf, big_sem.at[1]).wait()


def local_step(emb_p, head_p, emb_g, head_g, emb_r, emb_c, head_r, head_c):
    f32 = jnp.float32
    n = CHUNKS
    dma = pltpu.SemaphoreType.DMA
    hbm = pl.BlockSpec(memory_space=pltpu.HBM)
    vmem = pl.BlockSpec(memory_space=pltpu.VMEM)
    rows_shape = (BLOCKS, 2, LANES)
    table = jax.ShapeDtypeStruct((COLS, ROWS), f32)
    half = jax.ShapeDtypeStruct((COLS, ROWS), jnp.bfloat16)
    emb_p = emb_p.T
    shapes = [(ROWS // 2, EMBED)] * 2 + [(n, 2, 2, 2, COLS, LANES)] * 3
    shapes += [(n, 2, 2, COLS, LANES)] * 2 + [(n, 2, COLS, LANES)] * 2 + [(PAIRS, 2, 2, COLS, LANES)]
    shapes += [(BLOCKS, 4, LANES), (2, *rows_shape), (2, 1, COLS)]
    shapes += [(PAIRS, 4, LANES), (PAIRS, 3, 4, LANES)]
    shapes += [(2, 2, COLS, LANES)] * 2 + [(4, LANES), (2, LANES)]
    shapes += [(2, 4, LANES), (7, 4, LANES), (1, LANES), (7, 1, LANES)]
    scratch = [pltpu.VMEM(shape, f32) for shape in shapes]
    scratch += [dma((len(GROUPS) + 1,))] * 4 + [dma((RING,))] * 4 + [dma((PAIRS,))] * 3
    scratch += [dma((11,)), dma((2,)), dma((4,))]
    kept = [pltpu.VMEM((COLS, ROWS), f32)] * 4 + [pltpu.VMEM(rows_shape, f32)] * 2 + [pltpu.VMEM((1, COLS), f32)] * 2
    kept.append(pltpu.VMEM((2, COLS, LANES), f32))
    state = pl.pallas_call(
        exchange_kernel,
        out_shape=tuple(kept),
        in_specs=[hbm] * 8,
        out_specs=(vmem,) * 9,
        scratch_shapes=scratch,
        compiler_params=pltpu.CompilerParams(collective_id=0, has_side_effects=True, vmem_limit_bytes=60_000_000),
        name="exchange",
    )(emb_g.reshape(ROWS, EMBED), head_g.reshape(2, 2, 2, COLS, ROWS), emb_p, head_p,
      emb_r.reshape(rows_shape), head_r.reshape(rows_shape), emb_c.reshape(1, COLS), head_c.reshape(1, COLS))

    outs = pl.pallas_call(
        update_kernel,
        out_shape=(table, table, jax.ShapeDtypeStruct(rows_shape, f32), jax.ShapeDtypeStruct(rows_shape, f32),
                   jax.ShapeDtypeStruct((1, COLS), f32), jax.ShapeDtypeStruct((1, COLS), f32), half, half),
        in_specs=[vmem] * 9,
        out_specs=(hbm,) * 8,
        scratch_shapes=[pltpu.VMEM((2, COLS, ROWS), f32), pltpu.VMEM((2, COLS, ROWS), jnp.bfloat16),
                        dma((4,)), dma((2,))],
        compiler_params=pltpu.CompilerParams(vmem_limit_bytes=16 * 2 ** 20),
        name="update",
    )(*state)
    emb_new, head_new, emb_rn, head_rn, emb_cn, head_cn, emb_half, head_half = outs
    return (emb_new.T, head_new, emb_rn.reshape(ROWS), emb_cn.reshape(COLS), head_rn.reshape(ROWS),
            head_cn.reshape(COLS), emb_half.T, head_half)


def solution(mesh):
    arg_specs = (P("model", "data"), P("data", "model"), P("data", "model", None), P("data", None, "model"),
                 P("model"), P("data"), P("model"), P("data"))
    result_specs = (P("model", "data"), P("data", "model"), P("model"), P("data"), P("model"), P("data"),
                    P("model", "data"), P("data", "model"))
    mapped = jax.shard_map(local_step, mesh=mesh, in_specs=arg_specs, out_specs=result_specs, check_vma=False)

    def update_tables(emb_param, head_param, emb_grad, head_grad, emb_row, emb_col, head_row, head_col):
        return mapped(emb_param, head_param, emb_grad, head_grad, emb_row, emb_col, head_row, head_col)

    return update_tables
```

time: 128 us -> 125 us (0.977)
  Pallas kernels: 127 us -> 124 us
    pallas_call x1, Pallas kernels: 125 us -> 121 us  [local_step(): pl.pallas_call(exchange_kernel, out_shape=tuple(kept), in_specs=[hbm] * 8...]
where the time goes in v3:
time: 125 us; the launch traced here: 124 us
  Pallas kernels  124 us (99%)
    pallas_call x1, Pallas kernels, local_step(): pl.pallas_call(exchange_kernel, out_shape=tuple(kept), in_specs=[hbm] * 8...  121 us

profile of v3, /device:TPU:0, one launch (start us, length us, event | category | flops | bytes accessed | tf_op | source)
XLA Modules:
  0.0 124.5 jit_solution(11155142139082923964)
XLA Ops:
  0.6 121.5 %exchange.1 = (f32[96,4096]{1,0:T(8,128)S(1)}, f32[96,4096]{1,0:T(8,128)S(1)}, f32[96,4096]{1,0:T(8,128)S(1)}, f32[96,4096]{1,0:T(8,128)S(1)}, f32[16,2,128]{2,1...) custom-call(f32[4096,768]{1,0:T(8,128)} %bitcast.13, ...), custom_call_target="tpu_custom_call" | custom-call | tf_op jit(solution)/shard_map/exchange/pallas_call | solution.py:450
  122.1 2.4 %update.1 = (f32[96,4096]{1,0:T(8,128)}, f32[96,4096]{1,0:T(8,128)}, f32[16,2,128]{2,1,0:T(2,128)}, f32[16,2,128]{2,1,0:T(2,128)}, f32[1,96]{1,0:T(1,128)}, /*in...) custom-call(f32[96,4096]{1,0:T(8,128)S(1)} %get-tuple-element.25.emb_g, ...), custom_call_target="tpu_custom_call" | custom-call | tf_op jit(solution)/shard_map/update/pallas_call | solution.py:461

commit v4 on v3

--- a/solution.py
+++ b/solution.py
@@ -21,20 +21,20 @@
 COLS = EMBED // 8
 LANES = 128
 CHUNKS = ROWS // 2 // LANES
-GROUPS = ((0, 1), (1, 1), (2, 2), (4, 4), (8, 8))
+GROUPS = ((0, 1), (1, 1), (2, 2), (4, 12))
 PAIRS = CHUNKS // 2
 BLOCKS = 2 * PAIRS
 RING = 4
-PARTS = 4
+PARTS = 3
 MESH = pl.DeviceIdType.MESH
 PLANE = ((0, 1), (1, 0), (1, 1))
 
 
 def exchange_kernel(emb_ref, head_ref, emb_p_ref, head_p_ref, emb_r_ref, head_r_ref, emb_c_ref, head_c_ref,
                     stage_e, stage_h, par_e, par_h, emb_rows_out, head_rows_out, emb_cols_out, head_cols_out, scale_out,
-                    own_e, in0_e, sum_e, sum_h, in0_h, in1_e, in1_h, in2_e, in2_h, peer,
+                    both_e, sum_e, both_h, in1_e, in1_h, in2_e, in2_h, peer,
                     rows, old_rows, old_cols, rp_own, rp_in, col_acc, t_acc, rsum, psum, m_own, m_in, s_own, s_in,
-                    ld_e, ld_h, s0e_r, s0h_r, s1e_r, s1h_r, s2e_r, s2h_r, swap_r, rp_r, fw_r, send, last_r, in_sem):
+                    s0e_r, s0h_r, s1e_r, s1h_r, s2e_r, s2h_r, swap_r, rp_r, fw_r, send, last_r, in_sem, token):
     model = lax.axis_index("model")
     data = lax.axis_index("data")
     c = data % 2
@@ -65,26 +65,26 @@
 
     def first_e(q):
         cols = pl.ds(pl.multiple_of((oy if q == 0 else y) * half_of, LANES), half_of)
-        return (pltpu.make_async_copy(emb_ref.at[vocab_at(c, 0, 1), cols], own_e.at[0:LANES, cols], ld_e.at[q]),
-                remote(emb_ref.at[vocab_at(oc, 0, 1), cols], in0_e.at[0:LANES, cols], send.at[0], s0e_r.at[q], core_peer))
+        return (pltpu.make_async_copy(emb_ref.at[vocab_at(c, 0, 1), cols], both_e.at[0, 0:LANES, cols], s0e_r.at[q]),
+                remote(emb_ref.at[vocab_at(oc, 0, 1), cols], both_e.at[1, 0:LANES, cols], send.at[0], s0e_r.at[q], core_peer))
 
     def first_h(q):
         part = ox if q == 0 else x
-        return (pltpu.make_async_copy(head_ref.at[:, part, :, :, vocab_at(c, 0, 1)], sum_h.at[0, :, part], ld_h.at[q]),
-                remote(head_ref.at[:, part, :, :, vocab_at(oc, 0, 1)], in0_h.at[0, :, part], send.at[1], s0h_r.at[q], core_peer))
+        return (pltpu.make_async_copy(head_ref.at[:, part, :, :, vocab_at(c, 0, 1)], both_h.at[0, 0, :, part], s0h_r.at[q]),
+                remote(head_ref.at[:, part, :, :, vocab_at(oc, 0, 1)], both_h.at[1, 0, :, part], send.at[1], s0h_r.at[q], core_peer))
 
     def group_e(i):
         first, count = GROUPS[i]
         at = slice(first * LANES, (first + count) * LANES)
-        return (pltpu.make_async_copy(emb_ref.at[vocab_at(c, first, count), :], own_e.at[at, :], ld_e.at[i + 1]),
-                remote(emb_ref.at[vocab_at(oc, first, count), :], in0_e.at[at, :], send.at[0], s0e_r.at[i + 1], core_peer))
+        return (pltpu.make_async_copy(emb_ref.at[vocab_at(c, first, count), :], both_e.at[0, at, :], s0e_r.at[i + 1]),
+                remote(emb_ref.at[vocab_at(oc, first, count), :], both_e.at[1, at, :], send.at[0], s0e_r.at[i + 1], core_peer))
 
     def group_h(i):
         first, count = GROUPS[i]
         pairs = []
         for j in range(first, first + count):
-            pairs.append((pltpu.make_async_copy(head_ref.at[:, :, :, :, vocab_at(c, j, 1)], sum_h.at[j], ld_h.at[i + 1]),
-                          remote(head_ref.at[:, :, :, :, vocab_at(oc, j, 1)], in0_h.at[j], send.at[1], s0h_r.at[i + 1],
+            pairs.append((pltpu.make_async_copy(head_ref.at[:, :, :, :, vocab_at(c, j, 1)], both_h.at[0, j], s0h_r.at[i + 1]),
+                          remote(head_ref.at[:, :, :, :, vocab_at(oc, j, 1)], both_h.at[1, j], send.at[1], s0h_r.at[i + 1],
                                  core_peer)))
         return pairs
 
@@ -92,7 +92,7 @@
         return remote(sum_e.at[k, oy], in1_e.at[k], send.at[2], s1e_r.at[k % RING], y_peer)
 
     def one_h(k):
-        return remote(sum_h.at[k, :, ox], in1_h.at[k], send.at[3], s1h_r.at[k % RING], x_peer)
+        return remote(both_h.at[0, k, :, ox], in1_h.at[k], send.at[3], s1h_r.at[k % RING], x_peer)
 
     def two_e(k):
         return remote(in1_e.at[k, ox], in2_e.at[k], send.at[4], s2e_r.at[k % RING], x_peer)
@@ -101,32 +101,24 @@
         return remote(in1_h.at[k, oy], in2_h.at[k], send.at[5], s2h_r.at[k % RING], y_peer)
 
     def swap(q):
-        return [remote(total.at[pl.ds(2 * q, 2), oc], peer.at[q, t], send.at[6], swap_r.at[q], core_peer)
+        return [remote(total.at[pl.ds(2 * q, 2), oc], peer.at[q, t], send.at[6], swap_r.at[q % RING], core_peer)
                 for t, total in enumerate((in2_e, in2_h))]
 
     def row_msg(q, i):
         fy, fx = PLANE[i]
-        return remote(rp_own.at[q], rp_in.at[q, i], send.at[7], rp_r.at[q], plane_id(fy, fx, 0))
+        return remote(rp_own.at[q], rp_in.at[q, i], send.at[7], rp_r.at[q % RING], plane_id(fy, fx, 0))
 
     def row_fwd(q):
-        return remote(rows.at[c * PAIRS + q], rows.at[c * PAIRS + q], send.at[8], fw_r.at[q], core_peer)
+        return remote(rows.at[c * PAIRS + q], rows.at[c * PAIRS + q], send.at[8], fw_r.at[q % RING], core_peer)
 
     small_loads = [pltpu.make_async_copy(src, dst, in_sem.at[i]) for i, (src, dst) in (
         (0, (emb_p_ref, par_e)), (1, (head_p_ref, par_h)), (2, (emb_r_ref, old_rows.at[0])), (2, (head_r_ref, old_rows.at[1])),
         (3, (emb_c_ref, old_cols.at[0])), (3, (head_c_ref, old_cols.at[1])))]
 
     barrier = pltpu.get_barrier_semaphore()
-    greeted = 0
-    for fy in range(2):
-        for fx in range(2):
-            for fc in range(2):
-                if fy + fx + fc:
-                    pl.semaphore_signal(barrier, inc=1, device_id=plane_id(fy, fx, fc), device_id_type=MESH)
-                    greeted += 1
-    for dz in range(1, 4):
-        for fc in range(2):
-            pl.semaphore_signal(barrier, inc=1, device_id=column_id(dz, fc), device_id_type=MESH)
-            greeted += 1
+    above, below = column_id(1, 0), column_id(3, 0)
+    for peer_id in (core_peer, x_peer, y_peer, above, below):
+        pl.semaphore_signal(barrier, inc=1, device_id=peer_id, device_id_type=MESH)
     for q in range(2):
         first_e(q)[0].start()
         first_h(q)[0].start()
@@ -134,7 +126,7 @@
         group_e(i)[0].start()
         for cp, _ in group_h(i):
             cp.start()
-    pl.semaphore_wait(barrier, greeted)
+    pl.semaphore_wait(barrier, 5)
 
     for q in range(2):
         first_e(q)[1].start()
@@ -145,6 +137,8 @@
             cp.start()
     for cp in small_loads:
         cp.start()
+    for peer_id in (above, below):
+        pl.semaphore_signal(token, inc=1, device_id=peer_id, device_id_type=MESH)
 
     col_acc[...] = jnp.zeros_like(col_acc)
     t_acc[...] = jnp.zeros_like(t_acc)
@@ -155,7 +149,7 @@
         at = pl.ds(pl.multiple_of(k * LANES, LANES), LANES)
         for j in range(half_of // LANES):
             cols = pl.ds(pl.multiple_of(half * half_of + j * LANES, LANES), LANES)
-            strip = (own_e[at, cols] + in0_e[at, cols]).T
+            strip = (both_e[0, at, cols] + both_e[1, at, cols]).T
             done = 0
             while done < LANES:
                 block, row = divmod(LANES * j + done, COLS)
@@ -166,7 +160,7 @@
     def add_h(k, part):
         for a in range(2):
             for b in range(2):
-                sum_h[k, a, part, b] = sum_h[k, a, part, b] + in0_h[k, a, part, b]
+                both_h[0, k, a, part, b] = both_h[0, k, a, part, b] + both_h[1, k, a, part, b]
 
     def combine_cores(k):
         flip_e(k, oy)
@@ -182,9 +176,9 @@
         two_e(k).start()
         in1_e[k, x] = in1_e[k, x] + sum_e[k, y, x]
         one_h(k).wait_recv()
-        in1_h[k, oy] = in1_h[k, oy] + sum_h[k, oy, x]
+        in1_h[k, oy] = in1_h[k, oy] + both_h[0, k, oy, x]
         two_h(k).start()
-        in1_h[k, y] = in1_h[k, y] + sum_h[k, y, x]
+        in1_h[k, y] = in1_h[k, y] + both_h[0, k, y, x]
 
     def finish(k, q, i):
         two_e(k).wait_recv()
@@ -209,7 +203,7 @@
             cp.start()
 
     def row_stats(q):
-        arrived(rp_in.at[q], rp_r.at[q])
+        arrived(rp_in.at[q], rp_r.at[q % RING])
         block = c * PAIRS + q
         row_sq = (rp_own[q] + rp_in[q, 0]) + (rp_in[q, 1] + rp_in[q, 2])
         old = jnp.concatenate([old_rows[0, block], old_rows[1, block]], axis=0)
@@ -237,8 +231,8 @@
         scale_rows(c * PAIRS + q, lambda t, i: totals[t][2 * q + i, c])
 
     def scale_peer(q):
-        arrived(rows.at[oc * PAIRS + q], fw_r.at[q])
-        arrived(peer.at[q], swap_r.at[q])
+        arrived(rows.at[oc * PAIRS + q], fw_r.at[q % RING])
+        arrived(peer.at[q], swap_r.at[q % RING])
         scale_rows(oc * PAIRS + q, lambda t, i: peer[q, t, i])
 
     def param_sq(k):
@@ -251,18 +245,17 @@
                 psum[t:t + 1, :] = psum[t:t + 1, :] + v[:, i * LANES:(i + 1) * LANES]
 
     for q in range(2):
-        load, cross = first_e(q)
-        load.wait()
-        cross.wait_recv()
+        cols = pl.ds(pl.multiple_of((oy if q == 0 else y) * half_of, LANES), half_of)
+        arrived(both_e.at[:, 0:LANES, cols], s0e_r.at[q])
         flip_e(0, oy if q == 0 else y)
         if q == 0:
             one_e(0).start()
-        load, cross = first_h(q)
-        load.wait()
-        cross.wait_recv()
-        add_h(0, ox if q == 0 else x)
+        part = ox if q == 0 else x
+        arrived(both_h.at[:, 0, :, part], s0h_r.at[q])
+        add_h(0, part)
         if q == 0:
             one_h(0).start()
+    pl.semaphore_wait(token, 2)
     arrived(par_e, in_sem.at[0])
     arrived(par_h, in_sem.at[1])
     arrived(old_rows, in_sem.at[2])
@@ -276,10 +269,8 @@
             @pl.when(k + 1 == first)
             def _():
                 at = slice(first * LANES, (first + count) * LANES)
-                arrived(own_e.at[at, :], ld_e.at[i + 1])
-                arrived(in0_e.at[at, :], s0e_r.at[i + 1])
-                arrived(sum_h.at[first:first + count], ld_h.at[i + 1])
-                arrived(in0_h.at[first:first + count], s0h_r.at[i + 1])
+                arrived(both_e.at[:, at, :], s0e_r.at[i + 1])
+                arrived(both_h.at[:, first:first + count], s0h_r.at[i + 1])
 
         @pl.when(k + 1 < CHUNKS)
         def _():
@@ -297,16 +288,16 @@
         def _():
             finish(k - 1, pair - 1, 1)
             publish(pair - 1)
+
+        @pl.when((k >= 6) & (k % 2 == 0))
+        def _():
+            scale_peer(pair - 3)
 
         @pl.when((k >= 4) & (k % 2 == 0))
         def _():
             row_stats(pair - 2)
             row_fwd(pair - 2).start()
             scale_own(pair - 2)
-
-        @pl.when((k >= 6) & (k % 2 == 0))
-        def _():
-            scale_peer(pair - 3)
 
     finish(CHUNKS - 1, PAIRS - 1, 1)
     publish(PAIRS - 1)
@@ -379,8 +370,8 @@
 
     emb_rows_out[...] = rows[:, :2, :]
     head_rows_out[...] = rows[:, 2:, :]
-    arrived(in0_e, send.at[0])
-    arrived(in0_h, send.at[1])
+    arrived(both_e.at[0], send.at[0])
+    arrived(both_h.at[0], send.at[1])
     arrived(in1_e, send.at[2])
     arrived(in1_h, send.at[3])
     arrived(in2_e, send.at[4])
@@ -411,15 +402,15 @@
         ((emb_rows, emb_rows_new), (head_rows, head_rows_new), (emb_cols, emb_cols_new), (head_cols, head_cols_new)))]
     for cp in small:
         cp.start()
-    size = ROWS // PARTS
+    size = COLS // PARTS
     for i in range(PARTS):
         part = slice(i * size, (i + 1) * size)
         for t, (p, g, new, half) in enumerate(((emb_p, emb_g, emb_new, emb_half), (head_p, head_g, head_new, head_half))):
-            value = p[:, part] - g[:, part] * scale[t, :, 0:1]
-            new_buf[t, :, part] = value
-            half_buf[t, :, part] = value.astype(jnp.bfloat16)
-            pltpu.make_async_copy(new_buf.at[t, :, part], new.at[:, part], big_sem.at[0]).start()
-            pltpu.make_async_copy(half_buf.at[t, :, part], half.at[:, part], big_sem.at[1]).start()
+            value = p[part, :] - g[part, :] * scale[t, part, 0:1]
+            new_buf[t, part, :] = value
+            half_buf[t, part, :] = value.astype(jnp.bfloat16)
+            pltpu.make_async_copy(new_buf.at[t, part, :], new.at[part, :], big_sem.at[0]).start()
+            pltpu.make_async_copy(half_buf.at[t, part, :], half.at[part, :], big_sem.at[1]).start()
     for cp in small:
         cp.wait()
     pltpu.make_async_copy(new_buf, new_buf, big_sem.at[0]).wait()
@@ -436,15 +427,15 @@
     table = jax.ShapeDtypeStruct((COLS, ROWS), f32)
     half = jax.ShapeDtypeStruct((COLS, ROWS), jnp.bfloat16)
     emb_p = emb_p.T
-    shapes = [(ROWS // 2, EMBED)] * 2 + [(n, 2, 2, 2, COLS, LANES)] * 3
+    shapes = [(2, ROWS // 2, EMBED), (n, 2, 2, 2, COLS, LANES), (2, n, 2, 2, 2, COLS, LANES)]
     shapes += [(n, 2, 2, COLS, LANES)] * 2 + [(n, 2, COLS, LANES)] * 2 + [(PAIRS, 2, 2, COLS, LANES)]
     shapes += [(BLOCKS, 4, LANES), (2, *rows_shape), (2, 1, COLS)]
     shapes += [(PAIRS, 4, LANES), (PAIRS, 3, 4, LANES)]
     shapes += [(2, 2, COLS, LANES)] * 2 + [(4, LANES), (2, LANES)]
     shapes += [(2, 4, LANES), (7, 4, LANES), (1, LANES), (7, 1, LANES)]
     scratch = [pltpu.VMEM(shape, f32) for shape in shapes]
-    scratch += [dma((len(GROUPS) + 1,))] * 4 + [dma((RING,))] * 4 + [dma((PAIRS,))] * 3
-    scratch += [dma((11,)), dma((2,)), dma((4,))]
+    scratch += [dma((len(GROUPS) + 1,))] * 2 + [dma((RING,))] * 7
+    scratch += [dma((11,)), dma((2,)), dma((4,)), pltpu.SemaphoreType.REGULAR]
     kept = [pltpu.VMEM((COLS, ROWS), f32)] * 4 + [pltpu.VMEM(rows_shape, f32)] * 2 + [pltpu.VMEM((1, COLS), f32)] * 2
     kept.append(pltpu.VMEM((2, COLS, LANES), f32))
     state = pl.pallas_call(

time: 125 us -> 124 us (level)
  no operation moved by 1% of the time
where the time goes in v4:
time: 124 us
  Pallas kernels  123 us (99%)
    pallas_call x1, Pallas kernels, local_step(): pl.pallas_call(exchange_kernel, out_shape=tuple(kept), in_specs=[hbm] * 8...  121 us

profile of v4, /device:TPU:0, one launch (start us, length us, event | category | flops | bytes accessed | tf_op | source)
XLA Modules:
  0.0 124.0 jit_solution(12837122280817082371)
XLA Ops:
  0.6 121.0 %exchange.1 = (f32[96,4096]{1,0:T(8,128)S(1)}, f32[96,4096]{1,0:T(8,128)S(1)}, f32[96,4096]{1,0:T(8,128)S(1)}, f32[96,4096]{1,0:T(8,128)S(1)}, f32[16,2,128]{2,1...) custom-call(f32[4096,768]{1,0:T(8,128)} %bitcast.13, ...), custom_call_target="tpu_custom_call" | custom-call | tf_op jit(solution)/shard_map/exchange/pallas_call | solution.py:441
  121.6 2.4 %update.1 = (f32[96,4096]{1,0:T(8,128)}, f32[96,4096]{1,0:T(8,128)}, f32[16,2,128]{2,1,0:T(2,128)}, f32[16,2,128]{2,1,0:T(2,128)}, f32[1,96]{1,0:T(1,128)}, /*in...) custom-call(f32[96,4096]{1,0:T(8,128)S(1)} %get-tuple-element.25.emb_g, ...), custom_call_target="tpu_custom_call" | custom-call | tf_op jit(solution)/shard_map/update/pallas_call | solution.py:452

commit v5 on v4

--- a/solution.py
+++ b/solution.py
@@ -33,7 +33,7 @@
 def exchange_kernel(emb_ref, head_ref, emb_p_ref, head_p_ref, emb_r_ref, head_r_ref, emb_c_ref, head_c_ref,
                     stage_e, stage_h, par_e, par_h, emb_rows_out, head_rows_out, emb_cols_out, head_cols_out, scale_out,
                     both_e, sum_e, both_h, in1_e, in1_h, in2_e, in2_h, peer,
-                    rows, old_rows, old_cols, rp_own, rp_in, col_acc, t_acc, rsum, psum, m_own, m_in, s_own, s_in,
+                    rows, old_rows, old_cols, rp_own, rp_in, col_acc, t_acc, rsum, psum, m_own, m_in, m_sum, s_own, s_in,
                     s0e_r, s0h_r, s1e_r, s1h_r, s2e_r, s2h_r, swap_r, rp_r, fw_r, send, last_r, in_sem, token):
     model = lax.axis_index("model")
     data = lax.axis_index("data")
@@ -113,12 +113,27 @@
 
     small_loads = [pltpu.make_async_copy(src, dst, in_sem.at[i]) for i, (src, dst) in (
         (0, (emb_p_ref, par_e)), (1, (head_p_ref, par_h)), (2, (emb_r_ref, old_rows.at[0])), (2, (head_r_ref, old_rows.at[1])),
-        (3, (emb_c_ref, old_cols.at[0])), (3, (head_c_ref, old_cols.at[1])))]
+        (3, (emb_c_ref, old_cols.at[0, c])), (3, (head_c_ref, old_cols.at[1, c])))]
+    small_loads += [remote(src, old_cols.at[t, c], send.at[11], in_sem.at[4], core_peer)
+                    for t, src in enumerate((emb_c_ref, head_c_ref))]
 
     barrier = pltpu.get_barrier_semaphore()
     above, below = column_id(1, 0), column_id(3, 0)
-    for peer_id in (core_peer, x_peer, y_peer, above, below):
+    for peer_id in (core_peer, x_peer, y_peer):
         pl.semaphore_signal(barrier, inc=1, device_id=peer_id, device_id_type=MESH)
+
+    z_count = 1 + model * (3 - model) // 2
+
+    def along_z(act):
+        @pl.when(model < 3)
+        def _():
+            act(above)
+
+        @pl.when(model > 0)
+        def _():
+            act(below)
+
+    along_z(lambda peer_id: pl.semaphore_signal(barrier, inc=1, device_id=peer_id, device_id_type=MESH))
     for q in range(2):
         first_e(q)[0].start()
         first_h(q)[0].start()
@@ -126,7 +141,7 @@
         group_e(i)[0].start()
         for cp, _ in group_h(i):
             cp.start()
-    pl.semaphore_wait(barrier, 5)
+    pl.semaphore_wait(barrier, 3 + z_count)
 
     for q in range(2):
         first_e(q)[1].start()
@@ -137,8 +152,7 @@
             cp.start()
     for cp in small_loads:
         cp.start()
-    for peer_id in (above, below):
-        pl.semaphore_signal(token, inc=1, device_id=peer_id, device_id_type=MESH)
+    along_z(lambda peer_id: pl.semaphore_signal(token.at[0], inc=1, device_id=peer_id, device_id_type=MESH))
 
     col_acc[...] = jnp.zeros_like(col_acc)
     t_acc[...] = jnp.zeros_like(t_acc)
@@ -255,12 +269,6 @@
         add_h(0, part)
         if q == 0:
             one_h(0).start()
-    pl.semaphore_wait(token, 2)
-    arrived(par_e, in_sem.at[0])
-    arrived(par_h, in_sem.at[1])
-    arrived(old_rows, in_sem.at[2])
-    arrived(old_cols, in_sem.at[3])
-
     @pl.loop(0, CHUNKS)
     def _(k):
         for i in range(1, len(GROUPS)):
@@ -276,9 +284,24 @@
         def _():
             combine_cores(k + 1)
 
-        param_sq(k)
         first_sum(k)
         pair = k // 2
+
+        @pl.when(k == 0)
+        def _():
+            arrived(par_e, in_sem.at[0])
+            arrived(par_h, in_sem.at[1])
+            arrived(old_rows, in_sem.at[2])
+            arrived(old_cols.at[:, c], in_sem.at[3])
+            arrived(old_cols.at[:, oc], in_sem.at[4])
+            pl.semaphore_wait(token.at[0], z_count)
+            along_z(lambda peer_id: pl.semaphore_signal(token.at[1], inc=1, device_id=peer_id, device_id_type=MESH))
+
+        @pl.when(k == 1)
+        def _():
+            pl.semaphore_wait(token.at[1], z_count)
+
+        param_sq(k)
 
         @pl.when((k >= 1) & (k % 2 == 1))
         def _():
@@ -330,7 +353,7 @@
     def column_msg(i):
         dz, fc = columns[i]
         slot = columns.index(((4 - dz) % 4, fc))
-        return remote(m_own.at[oc if fc else c], m_in.at[slot], send.at[9], last_r.at[0], column_id(dz, fc))
+        return remote(m_own, m_in.at[slot], send.at[9], last_r.at[0], column_id(dz, fc))
 
     for i in range(len(columns)):
         column_msg(i).start()
@@ -339,30 +362,39 @@
     scale_own(PAIRS - 1)
     arrived(m_in, last_r.at[0])
 
-    total = m_own[c]
+    total = m_own[...]
     for i in range(len(columns)):
         total = total + m_in[i]
-    factors, message = [], jnp.zeros((1, LANES), jnp.float32)
-    for t, c_out in enumerate((emb_cols_out, head_cols_out)):
-        cols = total[2 * t:2 * t + 1, :]
+    m_sum[...] = total
+    message = jnp.zeros((1, LANES), jnp.float32)
+    for t in range(2):
+        cols = total[0, 2 * t:2 * t + 1, :]
         r_mean = jnp.sum(jnp.where(lane == COLS, cols, 0.0), axis=1, keepdims=True) / VOCAB
         p_col = jnp.sum(jnp.where(lane == COLS + 1, cols, 0.0), axis=1, keepdims=True)
-        col_new = BETA_TWO * old_cols[t] + (1.0 - BETA_TWO) * (cols[:, :COLS] / VOCAB)
-        u_sq = jnp.sum(total[2 * t + 1:2 * t + 2, :COLS] * (r_mean / col_new), axis=1, keepdims=True)
-        message = jnp.where(lane == 2 * t, u_sq, jnp.where(lane == 2 * t + 1, 0.5 * p_col, message))
+        u_sq = jnp.zeros((1, 1), jnp.float32)
+        for core in range(2):
+            col_new = BETA_TWO * old_cols[t, core] + (1.0 - BETA_TWO) * (total[core, 2 * t:2 * t + 1, :COLS] / VOCAB)
+            u_sq = u_sq + jnp.sum(total[core, 2 * t + 1:2 * t + 2, :COLS] * (r_mean / col_new), axis=1, keepdims=True)
+        message = jnp.where(lane == 2 * t, u_sq, jnp.where(lane == 2 * t + 1, p_col, message))
+    s_own[...] = message
+
+    def scalar_msg(i, fc):
+        return remote(s_own, s_in.at[i], send.at[10], last_r.at[1], plane_id(*PLANE[i], fc))
+
+    @pl.when(c == 1)
+    def _():
+        for fc in (1, 0):
+            for i in (2, 0, 1):
+                scalar_msg(i, fc).start()
+
+    factor_cols = []
+    for t, c_out in enumerate((emb_cols_out, head_cols_out)):
+        cols = m_sum[c, 2 * t:2 * t + 1, :]
+        r_mean = jnp.sum(jnp.where(lane == COLS, cols, 0.0), axis=1, keepdims=True) / VOCAB
+        col_new = BETA_TWO * old_cols[t, c] + (1.0 - BETA_TWO) * (cols[:, :COLS] / VOCAB)
         c_out[...] = col_new
-        factors.append(lax.rsqrt(col_new) * jnp.sqrt(r_mean))
-    s_own[...] = message
-
-    flips = [(fy, fx, fc) for fy in range(2) for fx in range(2) for fc in range(2) if fy + fx + fc]
-
-    def scalar_msg(i):
-        return remote(s_own, s_in.at[i], send.at[10], last_r.at[1], plane_id(*flips[i]))
-
-    for i in range(len(flips)):
-        scalar_msg(i).start()
-    square = diag[:, :COLS]
-    factor_cols = [jnp.sum(jnp.where(square, factor, 0.0), axis=1, keepdims=True) for factor in factors]
+        factor = lax.rsqrt(col_new) * jnp.sqrt(r_mean)
+        factor_cols.append(jnp.sum(jnp.where(diag[:, :COLS], factor, 0.0), axis=1, keepdims=True))
 
     @pl.loop(PAIRS - 3, PAIRS)
     def _(q):
@@ -380,9 +412,10 @@
     arrived(rp_in, send.at[7])
     arrived(rows.at[0:PAIRS], send.at[8])
     arrived(m_in, send.at[9])
+    arrived(old_cols.at[:, c], send.at[11])
     arrived(s_in, last_r.at[1])
     message = s_own[...]
-    for i in range(len(flips)):
+    for i in range(3):
         message = message + s_in[i]
     count = float(VOCAB * EMBED)
     for t in range(2):
@@ -392,7 +425,11 @@
         p_rms = jnp.sqrt(p_sq / count)
         step = LEARN_RATE * jnp.maximum(SCALE_FLOOR, p_rms) / jnp.maximum(1.0, u_rms / CLIP_LIMIT)
         scale_out[t] = jnp.broadcast_to(factor_cols[t] * step, (COLS, LANES))
-    arrived(s_in, send.at[10])
+
+    @pl.when(c == 1)
+    def _():
+        for fc in range(2):
+            arrived(s_in, send.at[10])
 
 
 def update_kernel(emb_g, head_g, emb_p, head_p, emb_rows, head_rows, emb_cols, head_cols, scale,
@@ -429,13 +466,13 @@
     emb_p = emb_p.T
     shapes = [(2, ROWS // 2, EMBED), (n, 2, 2, 2, COLS, LANES), (2, n, 2, 2, 2, COLS, LANES)]
     shapes += [(n, 2, 2, COLS, LANES)] * 2 + [(n, 2, COLS, LANES)] * 2 + [(PAIRS, 2, 2, COLS, LANES)]
-    shapes += [(BLOCKS, 4, LANES), (2, *rows_shape), (2, 1, COLS)]
+    shapes += [(BLOCKS, 4, LANES), (2, *rows_shape), (2, 2, 1, COLS)]
     shapes += [(PAIRS, 4, LANES), (PAIRS, 3, 4, LANES)]
     shapes += [(2, 2, COLS, LANES)] * 2 + [(4, LANES), (2, LANES)]
-    shapes += [(2, 4, LANES), (7, 4, LANES), (1, LANES), (7, 1, LANES)]
+    shapes += [(2, 4, LANES), (7, 2, 4, LANES), (2, 4, LANES), (1, LANES), (3, 1, LANES)]
     scratch = [pltpu.VMEM(shape, f32) for shape in shapes]
     scratch += [dma((len(GROUPS) + 1,))] * 2 + [dma((RING,))] * 7
-    scratch += [dma((11,)), dma((2,)), dma((4,)), pltpu.SemaphoreType.REGULAR]
+    scratch += [dma((12,)), dma((2,)), dma((5,)), pltpu.SemaphoreType.REGULAR((2,))]
     kept = [pltpu.VMEM((COLS, ROWS), f32)] * 4 + [pltpu.VMEM(rows_shape, f32)] * 2 + [pltpu.VMEM((1, COLS), f32)] * 2
     kept.append(pltpu.VMEM((2, COLS, LANES), f32))
     state = pl.pallas_call(

time: 124 us -> 131 us (1.056)
  Pallas kernels: 123 us -> 130 us
    pallas_call x1, Pallas kernels: 121 us -> 128 us  [local_step(): pl.pallas_call(exchange_kernel, out_shape=tuple(kept), in_specs=[hbm] * 8...]
where the time goes in v5:
time: 131 us
  Pallas kernels  130 us (99%)
    pallas_call x1, Pallas kernels, local_step(): pl.pallas_call(exchange_kernel, out_shape=tuple(kept), in_specs=[hbm] * 8...  128 us

profile of v5, /device:TPU:0, one launch (start us, length us, event | category | flops | bytes accessed | tf_op | source)
XLA Modules:
  0.0 130.6 jit_solution(16085414981917006949)
XLA Ops:
  0.6 127.5 %exchange.1 = (f32[96,4096]{1,0:T(8,128)S(1)}, f32[96,4096]{1,0:T(8,128)S(1)}, f32[96,4096]{1,0:T(8,128)S(1)}, f32[96,4096]{1,0:T(8,128)S(1)}, f32[16,2,128]{2,1...) custom-call(f32[4096,768]{1,0:T(8,128)} %bitcast.13, ...), custom_call_target="tpu_custom_call" | custom-call | tf_op jit(solution)/shard_map/exchange/pallas_call | solution.py:478
  128.2 2.4 %update.1 = (f32[96,4096]{1,0:T(8,128)}, f32[96,4096]{1,0:T(8,128)}, f32[16,2,128]{2,1,0:T(2,128)}, f32[16,2,128]{2,1,0:T(2,128)}, f32[1,96]{1,0:T(1,128)}, /*in...) custom-call(f32[96,4096]{1,0:T(8,128)S(1)} %get-tuple-element.25.emb_g, ...), custom_call_target="tpu_custom_call" | custom-call | tf_op jit(solution)/shard_map/update/pallas_call | solution.py:489

commit v6 on v5

--- a/solution.py
+++ b/solution.py
@@ -114,7 +114,7 @@
     small_loads = [pltpu.make_async_copy(src, dst, in_sem.at[i]) for i, (src, dst) in (
         (0, (emb_p_ref, par_e)), (1, (head_p_ref, par_h)), (2, (emb_r_ref, old_rows.at[0])), (2, (head_r_ref, old_rows.at[1])),
         (3, (emb_c_ref, old_cols.at[0, c])), (3, (head_c_ref, old_cols.at[1, c])))]
-    small_loads += [remote(src, old_cols.at[t, c], send.at[11], in_sem.at[4], core_peer)
+    old_cols_out = [remote(src, old_cols.at[t, c], send.at[11], in_sem.at[4], core_peer)
                     for t, src in enumerate((emb_c_ref, head_c_ref))]
 
     barrier = pltpu.get_barrier_semaphore()
@@ -146,6 +146,8 @@
     for q in range(2):
         first_e(q)[1].start()
         first_h(q)[1].start()
+    for cp in old_cols_out:
+        cp.start()
     for i in range(1, len(GROUPS)):
         group_e(i)[1].start()
         for _, cp in group_h(i):
@@ -250,7 +252,7 @@
         scale_rows(oc * PAIRS + q, lambda t, i: peer[q, t, i])
 
     def param_sq(k):
-        size = ROWS // CHUNKS
+        size = ROWS // CHUNKS * 2
         at = pl.ds(pl.multiple_of(k * size, size), size)
         for t, par in enumerate((par_e, par_h)):
             v = par[:, at]
@@ -287,21 +289,24 @@
         first_sum(k)
         pair = k // 2
 
-        @pl.when(k == 0)
+        @pl.when(k == 1)
+        def _():
+            pl.semaphore_wait(token.at[0], z_count)
+            along_z(lambda peer_id: pl.semaphore_signal(token.at[1], inc=1, device_id=peer_id, device_id_type=MESH))
+
+        @pl.when(k == 2)
+        def _():
+            pl.semaphore_wait(token.at[1], z_count)
+
+        @pl.when(k == 3)
         def _():
             arrived(par_e, in_sem.at[0])
             arrived(par_h, in_sem.at[1])
             arrived(old_rows, in_sem.at[2])
-            arrived(old_cols.at[:, c], in_sem.at[3])
-            arrived(old_cols.at[:, oc], in_sem.at[4])
-            pl.semaphore_wait(token.at[0], z_count)
-            along_z(lambda peer_id: pl.semaphore_signal(token.at[1], inc=1, device_id=peer_id, device_id_type=MESH))
-
-        @pl.when(k == 1)
-        def _():
-            pl.semaphore_wait(token.at[1], z_count)
-
-        param_sq(k)
+
+        @pl.when(k >= CHUNKS // 2)
+        def _():
+            param_sq(k - CHUNKS // 2)
 
         @pl.when((k >= 1) & (k % 2 == 1))
         def _():
@@ -360,6 +365,8 @@
 
     scale_own(PAIRS - 2)
     scale_own(PAIRS - 1)
+    arrived(old_cols.at[:, c], in_sem.at[3])
+    arrived(old_cols.at[:, oc], in_sem.at[4])
     arrived(m_in, last_r.at[0])
 
     total = m_own[...]

time: 131 us -> 124 us (0.947)
  Pallas kernels: 130 us -> 123 us
    pallas_call x1, Pallas kernels: 128 us -> 120 us  [local_step(): pl.pallas_call(exchange_kernel, out_shape=tuple(kept), in_specs=[hbm] * 8...]
where the time goes in v6:
time: 124 us; the launch traced here: 123 us
  Pallas kernels  123 us (99%)
    pallas_call x1, Pallas kernels, local_step(): pl.pallas_call(exchange_kernel, out_shape=tuple(kept), in_specs=[hbm] * 8...  120 us

profile of v6, /device:TPU:0, one launch (start us, length us, event | category | flops | bytes accessed | tf_op | source)
XLA Modules:
  0.0 123.5 jit_solution(17890353943308599985)
XLA Ops:
  0.6 120.4 %exchange.1 = (f32[96,4096]{1,0:T(8,128)S(1)}, f32[96,4096]{1,0:T(8,128)S(1)}, f32[96,4096]{1,0:T(8,128)S(1)}, f32[96,4096]{1,0:T(8,128)S(1)}, f32[16,2,128]{2,1...) custom-call(f32[4096,768]{1,0:T(8,128)} %bitcast.13, ...), custom_call_target="tpu_custom_call" | custom-call | tf_op jit(solution)/shard_map/exchange/pallas_call | solution.py:485
  121.0 2.4 %update.1 = (f32[96,4096]{1,0:T(8,128)}, f32[96,4096]{1,0:T(8,128)}, f32[16,2,128]{2,1,0:T(2,128)}, f32[16,2,128]{2,1,0:T(2,128)}, f32[1,96]{1,0:T(1,128)}, /*in...) custom-call(f32[96,4096]{1,0:T(8,128)S(1)} %get-tuple-element.25.emb_g, ...), custom_call_target="tpu_custom_call" | custom-call | tf_op jit(solution)/shard_map/update/pallas_call | solution.py:496

commit v7 on v6

--- a/solution.py
+++ b/solution.py
@@ -24,6 +24,8 @@
 GROUPS = ((0, 1), (1, 1), (2, 2), (4, 12))
 PAIRS = CHUNKS // 2
 BLOCKS = 2 * PAIRS
+AHEAD = 2
+DEEP = 6
 RING = 4
 PARTS = 3
 MESH = pl.DeviceIdType.MESH
@@ -89,10 +91,10 @@
         return pairs
 
     def one_e(k):
-        return remote(sum_e.at[k, oy], in1_e.at[k], send.at[2], s1e_r.at[k % RING], y_peer)
+        return remote(sum_e.at[k, oy], in1_e.at[k], send.at[2], s1e_r.at[k % DEEP], y_peer)
 
     def one_h(k):
-        return remote(both_h.at[0, k, :, ox], in1_h.at[k], send.at[3], s1h_r.at[k % RING], x_peer)
+        return remote(both_h.at[0, k, :, ox], in1_h.at[k], send.at[3], s1h_r.at[k % DEEP], x_peer)
 
     def two_e(k):
         return remote(in1_e.at[k, ox], in2_e.at[k], send.at[4], s2e_r.at[k % RING], x_peer)
@@ -212,19 +214,25 @@
                 row_part = row_part + jnp.sum(sq, axis=0, keepdims=True)
             rp_own[q, 2 * t + i:2 * t + i + 1, :] = row_part
 
-    def publish(q):
-        for i in range(3):
+    def send_rows(q):
+        for i in (2, 1, 0):
             row_msg(q, i).start()
+
+    def send_swap(q):
         for cp in swap(q):
             cp.start()
 
-    def row_stats(q):
+    def new_rows(q):
         arrived(rp_in.at[q], rp_r.at[q % RING])
         block = c * PAIRS + q
         row_sq = (rp_own[q] + rp_in[q, 0]) + (rp_in[q, 1] + rp_in[q, 2])
         old = jnp.concatenate([old_rows[0, block], old_rows[1, block]], axis=0)
         row_new = BETA_TWO * old + (1.0 - BETA_TWO) * (row_sq / EMBED)
         rows[block] = row_new
+        return row_new
+
+    def row_stats(q):
+        row_new = new_rows(q)
         rsum[...] = rsum[...] + row_new
         inv = 1.0 / row_new
         for t, total in enumerate((in2_e, in2_h)):
@@ -271,20 +279,24 @@
         add_h(0, part)
         if q == 0:
             one_h(0).start()
+    def group_arrived(i):
+        first, count = GROUPS[i]
+        arrived(both_e.at[:, first * LANES:(first + count) * LANES, :], s0e_r.at[i + 1])
+        arrived(both_h.at[:, first:first + count], s0h_r.at[i + 1])
+
+    group_arrived(1)
+    combine_cores(1)
+
     @pl.loop(0, CHUNKS)
     def _(k):
-        for i in range(1, len(GROUPS)):
-            first, count = GROUPS[i]
-
-            @pl.when(k + 1 == first)
+        for i in range(2, len(GROUPS)):
+            @pl.when(k + AHEAD == GROUPS[i][0])
             def _():
-                at = slice(first * LANES, (first + count) * LANES)
-                arrived(both_e.at[:, at, :], s0e_r.at[i + 1])
-                arrived(both_h.at[:, first:first + count], s0h_r.at[i + 1])
-
-        @pl.when(k + 1 < CHUNKS)
-        def _():
-            combine_cores(k + 1)
+                group_arrived(i)
+
+        @pl.when(k + AHEAD < CHUNKS)
+        def _():
+            combine_cores(k + AHEAD)
 
         first_sum(k)
         pair = k // 2
@@ -315,7 +327,8 @@
         @pl.when((k >= 2) & (k % 2 == 0))
         def _():
             finish(k - 1, pair - 1, 1)
-            publish(pair - 1)
+            send_rows(pair - 1)
+            send_swap(pair - 1)
 
         @pl.when((k >= 6) & (k % 2 == 0))
         def _():
@@ -327,13 +340,6 @@
             row_fwd(pair - 2).start()
             scale_own(pair - 2)
 
-    finish(CHUNKS - 1, PAIRS - 1, 1)
-    publish(PAIRS - 1)
-    row_stats(PAIRS - 2)
-    row_fwd(PAIRS - 2).start()
-    row_stats(PAIRS - 1)
-    row_fwd(PAIRS - 1).start()
-
     lane = lax.broadcasted_iota(jnp.int32, (1, LANES), 1)
     diag = lax.broadcasted_iota(jnp.int32, (COLS, LANES), 0) == lax.broadcasted_iota(jnp.int32, (COLS, LANES), 1)
 
@@ -344,14 +350,21 @@
     def total_of(v):
         return jnp.sum(jnp.sum(v, axis=1, keepdims=True), axis=0, keepdims=True)
 
+    row_stats(PAIRS - 2)
+    row_fwd(PAIRS - 2).start()
+    r_parts = [total_of(rsum[2 * t:2 * t + 2, :]) for t in range(2)]
+    p_parts = [jnp.sum(psum[t:t + 1, :], axis=1, keepdims=True) for t in range(2)]
     for t in range(2):
-        r_part = total_of(rsum[2 * t:2 * t + 2, :])
-        p_part = jnp.sum(psum[t:t + 1, :], axis=1, keepdims=True)
+        for core in range(2):
+            m_own[core, 2 * t + 1:2 * t + 2, :] = as_row(t_acc[t, core])
+    scale_own(PAIRS - 2)
+
+    finish(CHUNKS - 1, PAIRS - 1, 1)
+    send_rows(PAIRS - 1)
+    for t in range(2):
         for core in range(2):
             row = as_row(col_acc[t, core])
-            row = jnp.where(lane == COLS, r_part, jnp.where(lane == COLS + 1, p_part, row))
-            m_own[core, 2 * t:2 * t + 1, :] = row
-            m_own[core, 2 * t + 1:2 * t + 2, :] = as_row(t_acc[t, core])
+            m_own[core, 2 * t:2 * t + 1, :] = jnp.where(lane == COLS, r_parts[t], jnp.where(lane == COLS + 1, p_parts[t], row))
 
     columns = [(dz, fc) for dz in range(4) for fc in range(2) if dz + fc]
 
@@ -360,10 +373,22 @@
         slot = columns.index(((4 - dz) % 4, fc))
         return remote(m_own, m_in.at[slot], send.at[9], last_r.at[0], column_id(dz, fc))
 
-    for i in range(len(columns)):
+    for i in (3, 4, 1, 2, 5, 6, 0):
         column_msg(i).start()
-
-    scale_own(PAIRS - 2)
+    send_swap(PAIRS - 1)
+
+    row_new = new_rows(PAIRS - 1)
+    row_fwd(PAIRS - 1).start()
+    inv = 1.0 / row_new
+    t_last, r_last = [], []
+    for t, sums in enumerate((in2_e, in2_h)):
+        r_last.append(total_of(row_new[2 * t:2 * t + 2, :]))
+        for core in range(2):
+            acc = jnp.zeros((COLS, LANES), jnp.float32)
+            for i in range(2):
+                g = sums[2 * (PAIRS - 1) + i, core]
+                acc = acc + (g * g) * inv[2 * t + i:2 * t + i + 1, :]
+            t_last.append(as_row(acc))
     scale_own(PAIRS - 1)
     arrived(old_cols.at[:, c], in_sem.at[3])
     arrived(old_cols.at[:, oc], in_sem.at[4])
@@ -374,34 +399,38 @@
         total = total + m_in[i]
     m_sum[...] = total
     message = jnp.zeros((1, LANES), jnp.float32)
+    r_firsts = []
     for t in range(2):
         cols = total[0, 2 * t:2 * t + 1, :]
-        r_mean = jnp.sum(jnp.where(lane == COLS, cols, 0.0), axis=1, keepdims=True) / VOCAB
+        r_first = jnp.sum(jnp.where(lane == COLS, cols, 0.0), axis=1, keepdims=True) / VOCAB
         p_col = jnp.sum(jnp.where(lane == COLS + 1, cols, 0.0), axis=1, keepdims=True)
-        u_sq = jnp.zeros((1, 1), jnp.float32)
+        u_sq = jnp.zeros((1, COLS), jnp.float32)
         for core in range(2):
             col_new = BETA_TWO * old_cols[t, core] + (1.0 - BETA_TWO) * (total[core, 2 * t:2 * t + 1, :COLS] / VOCAB)
-            u_sq = u_sq + jnp.sum(total[core, 2 * t + 1:2 * t + 2, :COLS] * (r_mean / col_new), axis=1, keepdims=True)
-        message = jnp.where(lane == 2 * t, u_sq, jnp.where(lane == 2 * t + 1, p_col, message))
+            t_sum = 0.125 * total[core, 2 * t + 1:2 * t + 2, :COLS] + t_last[2 * t + core][:, :COLS]
+            u_sq = u_sq + t_sum * (r_first / col_new)
+        u_sq = jnp.sum(u_sq, axis=1, keepdims=True)
+        message = jnp.where(lane == 3 * t, u_sq, jnp.where(lane == 3 * t + 1, 0.125 * p_col, message))
+        message = jnp.where(lane == 3 * t + 2, 0.03125 * r_first + 0.25 * r_last[t] / VOCAB, message)
+        r_firsts.append(r_first)
     s_own[...] = message
 
-    def scalar_msg(i, fc):
-        return remote(s_own, s_in.at[i], send.at[10], last_r.at[1], plane_id(*PLANE[i], fc))
-
-    @pl.when(c == 1)
-    def _():
-        for fc in (1, 0):
-            for i in (2, 0, 1):
-                scalar_msg(i, fc).start()
+    others = [(dz, fy, fx, fc) for dz in range(4) for fy in range(2) for fx in range(2) for fc in range(2) if dz + fy + fx + fc]
+
+    def scalar_msg(i):
+        dz, fy, fx, fc = others[i]
+        slot = others.index(((4 - dz) % 4, fy, fx, fc))
+        return remote(s_own, s_in.at[slot], send.at[10], last_r.at[1], ((model + dz) % 4, plane_id(fy, fx, fc)[1]))
+
+    for i in sorted(range(len(others)), key=lambda i: -sum(others[i][1:3])):
+        scalar_msg(i).start()
 
     factor_cols = []
     for t, c_out in enumerate((emb_cols_out, head_cols_out)):
         cols = m_sum[c, 2 * t:2 * t + 1, :]
-        r_mean = jnp.sum(jnp.where(lane == COLS, cols, 0.0), axis=1, keepdims=True) / VOCAB
         col_new = BETA_TWO * old_cols[t, c] + (1.0 - BETA_TWO) * (cols[:, :COLS] / VOCAB)
         c_out[...] = col_new
-        factor = lax.rsqrt(col_new) * jnp.sqrt(r_mean)
-        factor_cols.append(jnp.sum(jnp.where(diag[:, :COLS], factor, 0.0), axis=1, keepdims=True))
+        factor_cols.append(jnp.sum(jnp.where(diag[:, :COLS], lax.rsqrt(col_new), 0.0), axis=1, keepdims=True))
 
     @pl.loop(PAIRS - 3, PAIRS)
     def _(q):
@@ -421,22 +450,15 @@
     arrived(m_in, send.at[9])
     arrived(old_cols.at[:, c], send.at[11])
     arrived(s_in, last_r.at[1])
-    message = s_own[...]
-    for i in range(3):
-        message = message + s_in[i]
+    message = s_own[...] + jnp.sum(s_in[...], axis=0)
     count = float(VOCAB * EMBED)
     for t in range(2):
-        u_sq = jnp.sum(jnp.where(lane == 2 * t, message, 0.0), axis=1, keepdims=True)
-        p_sq = jnp.sum(jnp.where(lane == 2 * t + 1, message, 0.0), axis=1, keepdims=True)
-        u_rms = jnp.sqrt(u_sq / count)
+        u_sq, p_sq, r_mean = [jnp.sum(jnp.where(lane == 3 * t + i, message, 0.0), axis=1, keepdims=True) for i in range(3)]
+        u_rms = jnp.sqrt(u_sq * (r_mean / r_firsts[t]) / count)
         p_rms = jnp.sqrt(p_sq / count)
         step = LEARN_RATE * jnp.maximum(SCALE_FLOOR, p_rms) / jnp.maximum(1.0, u_rms / CLIP_LIMIT)
-        scale_out[t] = jnp.broadcast_to(factor_cols[t] * step, (COLS, LANES))
-
-    @pl.when(c == 1)
-    def _():
-        for fc in range(2):
-            arrived(s_in, send.at[10])
+        scale_out[t] = jnp.broadcast_to(factor_cols[t] * (step * jnp.sqrt(r_mean)), (COLS, LANES))
+    arrived(s_in, send.at[10])
 
 
 def update_kernel(emb_g, head_g, emb_p, head_p, emb_rows, head_rows, emb_cols, head_cols, scale,
@@ -476,9 +498,9 @@
     shapes += [(BLOCKS, 4, LANES), (2, *rows_shape), (2, 2, 1, COLS)]
     shapes += [(PAIRS, 4, LANES), (PAIRS, 3, 4, LANES)]
     shapes += [(2, 2, COLS, LANES)] * 2 + [(4, LANES), (2, LANES)]
-    shapes += [(2, 4, LANES), (7, 2, 4, LANES), (2, 4, LANES), (1, LANES), (3, 1, LANES)]
+    shapes += [(2, 4, LANES), (7, 2, 4, LANES), (2, 4, LANES), (1, LANES), (31, 1, LANES)]
     scratch = [pltpu.VMEM(shape, f32) for shape in shapes]
-    scratch += [dma((len(GROUPS) + 1,))] * 2 + [dma((RING,))] * 7
+    scratch += [dma((len(GROUPS) + 1,))] * 2 + [dma((DEEP,))] * 2 + [dma((RING,))] * 5
     scratch += [dma((12,)), dma((2,)), dma((5,)), pltpu.SemaphoreType.REGULAR((2,))]
     kept = [pltpu.VMEM((COLS, ROWS), f32)] * 4 + [pltpu.VMEM(rows_shape, f32)] * 2 + [pltpu.VMEM((1, COLS), f32)] * 2
     kept.append(pltpu.VMEM((2, COLS, LANES), f32))

time: 124 us -> 122 us (0.984)
  Pallas kernels: 123 us -> 121 us
    pallas_call x1, Pallas kernels: 120 us -> 119 us  [local_step(): pl.pallas_call(exchange_kernel, out_shape=tuple(kept), in_specs=[hbm] * 8...]
where the time goes in v7:
time: 122 us
  Pallas kernels  121 us (99%)
    pallas_call x1, Pallas kernels, local_step(): pl.pallas_call(exchange_kernel, out_shape=tuple(kept), in_specs=[hbm] * 8...  119 us

profile of v7, /device:TPU:0, one launch (start us, length us, event | category | flops | bytes accessed | tf_op | source)
XLA Modules:
  0.0 121.9 jit_solution(13804732384146838467)
XLA Ops:
  0.6 118.9 %exchange.1 = (f32[96,4096]{1,0:T(8,128)S(1)}, f32[96,4096]{1,0:T(8,128)S(1)}, f32[96,4096]{1,0:T(8,128)S(1)}, f32[96,4096]{1,0:T(8,128)S(1)}, f32[16,2,128]{2,1...) custom-call(f32[4096,768]{1,0:T(8,128)} %bitcast.13, ...), custom_call_target="tpu_custom_call" | custom-call | tf_op jit(solution)/shard_map/exchange/pallas_call | solution.py:507
  119.5 2.4 %update.1 = (f32[96,4096]{1,0:T(8,128)}, f32[96,4096]{1,0:T(8,128)}, f32[16,2,128]{2,1,0:T(2,128)}, f32[16,2,128]{2,1,0:T(2,128)}, f32[1,96]{1,0:T(1,128)}, /*in...) custom-call(f32[96,4096]{1,0:T(8,128)S(1)} %get-tuple-element.25.emb_g, ...), custom_call_target="tpu_custom_call" | custom-call | tf_op jit(solution)/shard_map/update/pallas_call | solution.py:518

commit v8 on v7

--- a/solution.py
+++ b/solution.py
@@ -25,8 +25,8 @@
 PAIRS = CHUNKS // 2
 BLOCKS = 2 * PAIRS
 AHEAD = 2
-DEEP = 6
-RING = 4
+RING = 6
+SHORT = 4
 PARTS = 3
 MESH = pl.DeviceIdType.MESH
 PLANE = ((0, 1), (1, 0), (1, 1))
@@ -34,9 +34,9 @@
 
 def exchange_kernel(emb_ref, head_ref, emb_p_ref, head_p_ref, emb_r_ref, head_r_ref, emb_c_ref, head_c_ref,
                     stage_e, stage_h, par_e, par_h, emb_rows_out, head_rows_out, emb_cols_out, head_cols_out, scale_out,
-                    both_e, sum_e, both_h, in1_e, in1_h, in2_e, in2_h, peer,
+                    both_e, sum_e, both_h, in1, in2, peer,
                     rows, old_rows, old_cols, rp_own, rp_in, col_acc, t_acc, rsum, psum, m_own, m_in, m_sum, s_own, s_in,
-                    s0e_r, s0h_r, s1e_r, s1h_r, s2e_r, s2h_r, swap_r, rp_r, fw_r, send, last_r, in_sem, token):
+                    s0e_r, s0h_r, s1_r, s2_r, swap_r, rp_r, fw_r, send, last_r, in_sem, token):
     model = lax.axis_index("model")
     data = lax.axis_index("data")
     c = data % 2
@@ -91,32 +91,32 @@
         return pairs
 
     def one_e(k):
-        return remote(sum_e.at[k, oy], in1_e.at[k], send.at[2], s1e_r.at[k % DEEP], y_peer)
+        return remote(sum_e.at[k, oy], in1.at[k, 0], send.at[2], s1_r.at[k % RING], y_peer)
 
     def one_h(k):
-        return remote(both_h.at[0, k, :, ox], in1_h.at[k], send.at[3], s1h_r.at[k % DEEP], x_peer)
+        return remote(both_h.at[0, k, :, ox], in1.at[k, 1], send.at[2], s1_r.at[k % RING], x_peer)
 
     def two_e(k):
-        return remote(in1_e.at[k, ox], in2_e.at[k], send.at[4], s2e_r.at[k % RING], x_peer)
+        return remote(in1.at[k, 0, ox], in2.at[k, 0], send.at[3], s2_r.at[k % RING], x_peer)
 
     def two_h(k):
-        return remote(in1_h.at[k, oy], in2_h.at[k], send.at[5], s2h_r.at[k % RING], y_peer)
+        return remote(in1.at[k, 1, oy], in2.at[k, 1], send.at[3], s2_r.at[k % RING], y_peer)
 
     def swap(q):
-        return [remote(total.at[pl.ds(2 * q, 2), oc], peer.at[q, t], send.at[6], swap_r.at[q % RING], core_peer)
-                for t, total in enumerate((in2_e, in2_h))]
+        return [remote(in2.at[pl.ds(2 * q, 2), t, oc], peer.at[q, t], send.at[4], swap_r.at[q % SHORT], core_peer)
+                for t in range(2)]
 
     def row_msg(q, i):
         fy, fx = PLANE[i]
-        return remote(rp_own.at[q], rp_in.at[q, i], send.at[7], rp_r.at[q % RING], plane_id(fy, fx, 0))
+        return remote(rp_own.at[q], rp_in.at[q, i], send.at[5], rp_r.at[q % SHORT], plane_id(fy, fx, 0))
 
     def row_fwd(q):
-        return remote(rows.at[c * PAIRS + q], rows.at[c * PAIRS + q], send.at[8], fw_r.at[q % RING], core_peer)
+        return remote(rows.at[c * PAIRS + q], rows.at[c * PAIRS + q], send.at[6], fw_r.at[q % SHORT], core_peer)
 
     small_loads = [pltpu.make_async_copy(src, dst, in_sem.at[i]) for i, (src, dst) in (
         (0, (emb_p_ref, par_e)), (1, (head_p_ref, par_h)), (2, (emb_r_ref, old_rows.at[0])), (2, (head_r_ref, old_rows.at[1])),
         (3, (emb_c_ref, old_cols.at[0, c])), (3, (head_c_ref, old_cols.at[1, c])))]
-    old_cols_out = [remote(src, old_cols.at[t, c], send.at[11], in_sem.at[4], core_peer)
+    old_cols_out = [remote(src, old_cols.at[t, c], send.at[8], in_sem.at[4], core_peer)
                     for t, src in enumerate((emb_c_ref, head_c_ref))]
 
     barrier = pltpu.get_barrier_semaphore()
@@ -189,26 +189,23 @@
         add_h(k, x)
 
     def first_sum(k):
-        one_e(k).wait_recv()
-        in1_e[k, ox] = in1_e[k, ox] + sum_e[k, y, ox]
+        arrived(in1.at[k], s1_r.at[k % RING])
+        in1[k, 0, ox] = in1[k, 0, ox] + sum_e[k, y, ox]
         two_e(k).start()
-        in1_e[k, x] = in1_e[k, x] + sum_e[k, y, x]
-        one_h(k).wait_recv()
-        in1_h[k, oy] = in1_h[k, oy] + both_h[0, k, oy, x]
+        in1[k, 1, oy] = in1[k, 1, oy] + both_h[0, k, oy, x]
         two_h(k).start()
-        in1_h[k, y] = in1_h[k, y] + both_h[0, k, y, x]
+        in1[k, 0, x] = in1[k, 0, x] + sum_e[k, y, x]
+        in1[k, 1, y] = in1[k, 1, y] + both_h[0, k, y, x]
 
     def finish(k, q, i):
-        two_e(k).wait_recv()
-        for core in range(2):
-            in2_e[k, core] = in2_e[k, core] + in1_e[k, x, core]
-        two_h(k).wait_recv()
-        for core in range(2):
-            in2_h[k, core] = in2_h[k, core] + in1_h[k, y, core]
-        for t, total in enumerate((in2_e, in2_h)):
+        arrived(in2.at[k], s2_r.at[k % RING])
+        for t, mine in enumerate((x, y)):
+            for core in range(2):
+                in2[k, t, core] = in2[k, t, core] + in1[k, t, mine, core]
+        for t in range(2):
             row_part = jnp.zeros((1, LANES), jnp.float32)
             for core in range(2):
-                g = total[k, core]
+                g = in2[k, t, core]
                 sq = g * g + EPS_ONE
                 col_acc[t, core] = col_acc[t, core] + sq
                 row_part = row_part + jnp.sum(sq, axis=0, keepdims=True)
@@ -223,7 +220,7 @@
             cp.start()
 
     def new_rows(q):
-        arrived(rp_in.at[q], rp_r.at[q % RING])
+        arrived(rp_in.at[q], rp_r.at[q % SHORT])
         block = c * PAIRS + q
         row_sq = (rp_own[q] + rp_in[q, 0]) + (rp_in[q, 1] + rp_in[q, 2])
         old = jnp.concatenate([old_rows[0, block], old_rows[1, block]], axis=0)
@@ -235,11 +232,11 @@
         row_new = new_rows(q)
         rsum[...] = rsum[...] + row_new
         inv = 1.0 / row_new
-        for t, total in enumerate((in2_e, in2_h)):
+        for t in range(2):
             for core in range(2):
                 acc = t_acc[t, core]
                 for i in range(2):
-                    g = total[2 * q + i, core]
+                    g = in2[2 * q + i, t, core]
                     acc = acc + (g * g) * inv[2 * t + i:2 * t + i + 1, :]
                 t_acc[t, core] = acc
 
@@ -251,12 +248,11 @@
                 stage[:, pl.ds(base + i * LANES, LANES)] = get(t, i) * factor[2 * t + i:2 * t + i + 1, :]
 
     def scale_own(q):
-        totals = (in2_e, in2_h)
-        scale_rows(c * PAIRS + q, lambda t, i: totals[t][2 * q + i, c])
+        scale_rows(c * PAIRS + q, lambda t, i: in2[2 * q + i, t, c])
 
     def scale_peer(q):
-        arrived(rows.at[oc * PAIRS + q], fw_r.at[q % RING])
-        arrived(peer.at[q], swap_r.at[q % RING])
+        arrived(rows.at[oc * PAIRS + q], fw_r.at[q % SHORT])
+        arrived(peer.at[q], swap_r.at[q % SHORT])
         scale_rows(oc * PAIRS + q, lambda t, i: peer[q, t, i])
 
     def param_sq(k):
@@ -273,18 +269,30 @@
         arrived(both_e.at[:, 0:LANES, cols], s0e_r.at[q])
         flip_e(0, oy if q == 0 else y)
         if q == 0:
-            one_e(0).start()
+            @pl.when(c == 0)
+            def _():
+                one_e(0).start()
+
         part = ox if q == 0 else x
         arrived(both_h.at[:, 0, :, part], s0h_r.at[q])
         add_h(0, part)
         if q == 0:
-            one_h(0).start()
+            @pl.when(c == 0)
+            def _():
+                one_h(0).start()
+
     def group_arrived(i):
         first, count = GROUPS[i]
         arrived(both_e.at[:, first * LANES:(first + count) * LANES, :], s0e_r.at[i + 1])
         arrived(both_h.at[:, first:first + count], s0h_r.at[i + 1])
 
     group_arrived(1)
+
+    @pl.when(c == 1)
+    def _():
+        one_e(0).start()
+        one_h(0).start()
+
     combine_cores(1)
 
     @pl.loop(0, CHUNKS)
@@ -320,21 +328,21 @@
         def _():
             param_sq(k - CHUNKS // 2)
 
-        @pl.when((k >= 1) & (k % 2 == 1))
-        def _():
-            finish(k - 1, pair, 0)
-
         @pl.when((k >= 2) & (k % 2 == 0))
         def _():
-            finish(k - 1, pair - 1, 1)
+            finish(k - 2, pair - 1, 0)
+
+        @pl.when((k >= 3) & (k % 2 == 1))
+        def _():
+            finish(k - 2, pair - 1, 1)
             send_rows(pair - 1)
             send_swap(pair - 1)
 
-        @pl.when((k >= 6) & (k % 2 == 0))
+        @pl.when((k >= 7) & (k % 2 == 1))
         def _():
             scale_peer(pair - 3)
 
-        @pl.when((k >= 4) & (k % 2 == 0))
+        @pl.when((k >= 5) & (k % 2 == 1))
         def _():
             row_stats(pair - 2)
             row_fwd(pair - 2).start()
@@ -348,8 +356,9 @@
         return jnp.sum(jnp.where(diag, col, 0.0), axis=0, keepdims=True)
 
     def total_of(v):
-        return jnp.sum(jnp.sum(v, axis=1, keepdims=True), axis=0, keepdims=True)
-
+        return jnp.sum(jnp.sum(v, axis=0, keepdims=True), axis=1, keepdims=True)
+
+    finish(CHUNKS - 2, PAIRS - 1, 0)
     row_stats(PAIRS - 2)
     row_fwd(PAIRS - 2).start()
     r_parts = [total_of(rsum[2 * t:2 * t + 2, :]) for t in range(2)]
@@ -371,48 +380,45 @@
     def column_msg(i):
         dz, fc = columns[i]
         slot = columns.index(((4 - dz) % 4, fc))
-        return remote(m_own, m_in.at[slot], send.at[9], last_r.at[0], column_id(dz, fc))
+        return remote(m_own, m_in.at[slot], send.at[7], last_r.at[0], column_id(dz, fc))
 
     for i in (3, 4, 1, 2, 5, 6, 0):
         column_msg(i).start()
     send_swap(PAIRS - 1)
 
-    row_new = new_rows(PAIRS - 1)
-    row_fwd(PAIRS - 1).start()
-    inv = 1.0 / row_new
-    t_last, r_last = [], []
-    for t, sums in enumerate((in2_e, in2_h)):
-        r_last.append(total_of(row_new[2 * t:2 * t + 2, :]))
-        for core in range(2):
-            acc = jnp.zeros((COLS, LANES), jnp.float32)
-            for i in range(2):
-                g = sums[2 * (PAIRS - 1) + i, core]
-                acc = acc + (g * g) * inv[2 * t + i:2 * t + i + 1, :]
-            t_last.append(as_row(acc))
-    scale_own(PAIRS - 1)
     arrived(old_cols.at[:, c], in_sem.at[3])
     arrived(old_cols.at[:, oc], in_sem.at[4])
     arrived(m_in, last_r.at[0])
-
     total = m_own[...]
     for i in range(len(columns)):
         total = total + m_in[i]
     m_sum[...] = total
-    message = jnp.zeros((1, LANES), jnp.float32)
-    r_firsts = []
+    r_firsts, p_cols, u_firsts, weights = [], [], [], []
     for t in range(2):
         cols = total[0, 2 * t:2 * t + 1, :]
         r_first = jnp.sum(jnp.where(lane == COLS, cols, 0.0), axis=1, keepdims=True) / VOCAB
-        p_col = jnp.sum(jnp.where(lane == COLS + 1, cols, 0.0), axis=1, keepdims=True)
-        u_sq = jnp.zeros((1, COLS), jnp.float32)
+        u_first = jnp.zeros((1, COLS), jnp.float32)
         for core in range(2):
             col_new = BETA_TWO * old_cols[t, core] + (1.0 - BETA_TWO) * (total[core, 2 * t:2 * t + 1, :COLS] / VOCAB)
-            t_sum = 0.125 * total[core, 2 * t + 1:2 * t + 2, :COLS] + t_last[2 * t + core][:, :COLS]
-            u_sq = u_sq + t_sum * (r_first / col_new)
-        u_sq = jnp.sum(u_sq, axis=1, keepdims=True)
-        message = jnp.where(lane == 3 * t, u_sq, jnp.where(lane == 3 * t + 1, 0.125 * p_col, message))
-        message = jnp.where(lane == 3 * t + 2, 0.03125 * r_first + 0.25 * r_last[t] / VOCAB, message)
+            weight = r_first / col_new
+            u_first = u_first + total[core, 2 * t + 1:2 * t + 2, :COLS] * weight
+            weights.append(jnp.sum(jnp.where(diag[:, :COLS], weight, 0.0), axis=1, keepdims=True))
         r_firsts.append(r_first)
+        p_cols.append(jnp.sum(jnp.where(lane == COLS + 1, cols, 0.0), axis=1, keepdims=True))
+        u_firsts.append(0.125 * jnp.sum(u_first, axis=1, keepdims=True))
+
+    row_new = new_rows(PAIRS - 1)
+    inv = 1.0 / row_new
+    message = jnp.zeros((1, LANES), jnp.float32)
+    for t in range(2):
+        acc = jnp.zeros((COLS, LANES), jnp.float32)
+        for core in range(2):
+            for i in range(2):
+                g = in2[2 * (PAIRS - 1) + i, t, core]
+                acc = acc + (g * g) * inv[2 * t + i:2 * t + i + 1, :] * weights[2 * t + core]
+        r_mean = 0.03125 * r_firsts[t] + 0.25 * total_of(row_new[2 * t:2 * t + 2, :]) / VOCAB
+        for i, value in enumerate((u_firsts[t] + total_of(acc), 0.125 * p_cols[t], r_mean)):
+            message = jnp.where(lane == 3 * t + i, value, message)
     s_own[...] = message
 
     others = [(dz, fy, fx, fc) for dz in range(4) for fy in range(2) for fx in range(2) for fc in range(2) if dz + fy + fx + fc]
@@ -420,10 +426,12 @@
     def scalar_msg(i):
         dz, fy, fx, fc = others[i]
         slot = others.index(((4 - dz) % 4, fy, fx, fc))
-        return remote(s_own, s_in.at[slot], send.at[10], last_r.at[1], ((model + dz) % 4, plane_id(fy, fx, fc)[1]))
+        return remote(s_own, s_in.at[slot], send.at[9], last_r.at[1], ((model + dz) % 4, plane_id(fy, fx, fc)[1]))
 
     for i in sorted(range(len(others)), key=lambda i: -sum(others[i][1:3])):
         scalar_msg(i).start()
+    row_fwd(PAIRS - 1).start()
+    scale_own(PAIRS - 1)
 
     factor_cols = []
     for t, c_out in enumerate((emb_cols_out, head_cols_out)):
@@ -440,15 +448,13 @@
     head_rows_out[...] = rows[:, 2:, :]
     arrived(both_e.at[0], send.at[0])
     arrived(both_h.at[0], send.at[1])
-    arrived(in1_e, send.at[2])
-    arrived(in1_h, send.at[3])
-    arrived(in2_e, send.at[4])
-    arrived(in2_h, send.at[5])
-    arrived(peer, send.at[6])
-    arrived(rp_in, send.at[7])
-    arrived(rows.at[0:PAIRS], send.at[8])
-    arrived(m_in, send.at[9])
-    arrived(old_cols.at[:, c], send.at[11])
+    arrived(in1, send.at[2])
+    arrived(in2, send.at[3])
+    arrived(peer, send.at[4])
+    arrived(rp_in, send.at[5])
+    arrived(rows.at[0:PAIRS], send.at[6])
+    arrived(m_in, send.at[7])
+    arrived(old_cols.at[:, c], send.at[8])
     arrived(s_in, last_r.at[1])
     message = s_own[...] + jnp.sum(s_in[...], axis=0)
     count = float(VOCAB * EMBED)
@@ -458,7 +464,7 @@
         p_rms = jnp.sqrt(p_sq / count)
         step = LEARN_RATE * jnp.maximum(SCALE_FLOOR, p_rms) / jnp.maximum(1.0, u_rms / CLIP_LIMIT)
         scale_out[t] = jnp.broadcast_to(factor_cols[t] * (step * jnp.sqrt(r_mean)), (COLS, LANES))
-    arrived(s_in, send.at[10])
+    arrived(s_in, send.at[9])
 
 
 def update_kernel(emb_g, head_g, emb_p, head_p, emb_rows, head_rows, emb_cols, head_cols, scale,
@@ -494,14 +500,14 @@
     half = jax.ShapeDtypeStruct((COLS, ROWS), jnp.bfloat16)
     emb_p = emb_p.T
     shapes = [(2, ROWS // 2, EMBED), (n, 2, 2, 2, COLS, LANES), (2, n, 2, 2, 2, COLS, LANES)]
-    shapes += [(n, 2, 2, COLS, LANES)] * 2 + [(n, 2, COLS, LANES)] * 2 + [(PAIRS, 2, 2, COLS, LANES)]
+    shapes += [(n, 2, 2, 2, COLS, LANES), (n, 2, 2, COLS, LANES), (PAIRS, 2, 2, COLS, LANES)]
     shapes += [(BLOCKS, 4, LANES), (2, *rows_shape), (2, 2, 1, COLS)]
     shapes += [(PAIRS, 4, LANES), (PAIRS, 3, 4, LANES)]
     shapes += [(2, 2, COLS, LANES)] * 2 + [(4, LANES), (2, LANES)]
     shapes += [(2, 4, LANES), (7, 2, 4, LANES), (2, 4, LANES), (1, LANES), (31, 1, LANES)]
     scratch = [pltpu.VMEM(shape, f32) for shape in shapes]
-    scratch += [dma((len(GROUPS) + 1,))] * 2 + [dma((DEEP,))] * 2 + [dma((RING,))] * 5
-    scratch += [dma((12,)), dma((2,)), dma((5,)), pltpu.SemaphoreType.REGULAR((2,))]
+    scratch += [dma((len(GROUPS) + 1,))] * 2 + [dma((RING,))] * 2 + [dma((SHORT,))] * 3
+    scratch += [dma((10,)), dma((2,)), dma((5,)), pltpu.SemaphoreType.REGULAR((2,))]
     kept = [pltpu.VMEM((COLS, ROWS), f32)] * 4 + [pltpu.VMEM(rows_shape, f32)] * 2 + [pltpu.VMEM((1, COLS), f32)] * 2
     kept.append(pltpu.VMEM((2, COLS, LANES), f32))
     state = pl.pallas_call(

time: 122 us -> 121 us (level)
  no operation moved by 1% of the time
where the time goes in v8:
time: 121 us
  Pallas kernels  120 us (99%)
    pallas_call x1, Pallas kernels, local_step(): pl.pallas_call(exchange_kernel, out_shape=tuple(kept), in_specs=[hbm] * 8...  118 us

profile of v8, /device:TPU:0, one launch (start us, length us, event | category | flops | bytes accessed | tf_op | source)
XLA Modules:
  0.0 121.0 jit_solution(17076132003332566902)
XLA Ops:
  0.6 117.9 %exchange.1 = (f32[96,4096]{1,0:T(8,128)S(1)}, f32[96,4096]{1,0:T(8,128)S(1)}, f32[96,4096]{1,0:T(8,128)S(1)}, f32[96,4096]{1,0:T(8,128)S(1)}, f32[16,2,128]{2,1...) custom-call(f32[4096,768]{1,0:T(8,128)} %bitcast.13, ...), custom_call_target="tpu_custom_call" | custom-call | tf_op jit(solution)/shard_map/exchange/pallas_call | solution.py:513
  118.6 2.4 %update.1 = (f32[96,4096]{1,0:T(8,128)}, f32[96,4096]{1,0:T(8,128)}, f32[16,2,128]{2,1,0:T(2,128)}, f32[16,2,128]{2,1,0:T(2,128)}, f32[1,96]{1,0:T(1,128)}, /*in...) custom-call(f32[96,4096]{1,0:T(8,128)S(1)} %get-tuple-element.25.emb_g, ...), custom_call_target="tpu_custom_call" | custom-call | tf_op jit(solution)/shard_map/update/pallas_call | solution.py:524

commit v9 on v8

--- a/solution.py
+++ b/solution.py
@@ -27,7 +27,7 @@
 AHEAD = 2
 RING = 6
 SHORT = 4
-PARTS = 3
+PARTS = 8
 MESH = pl.DeviceIdType.MESH
 PLANE = ((0, 1), (1, 0), (1, 1))
 
@@ -288,16 +288,22 @@
 
     group_arrived(1)
 
+    @pl.when(c == 0)
+    def _():
+        combine_cores(1)
+
+    group_arrived(2)
+
     @pl.when(c == 1)
     def _():
         one_e(0).start()
         one_h(0).start()
-
-    combine_cores(1)
+        combine_cores(1)
+
 
     @pl.loop(0, CHUNKS)
     def _(k):
-        for i in range(2, len(GROUPS)):
+        for i in range(3, len(GROUPS)):
             @pl.when(k + AHEAD == GROUPS[i][0])
             def _():
                 group_arrived(i)
@@ -358,84 +364,91 @@
     def total_of(v):
         return jnp.sum(jnp.sum(v, axis=0, keepdims=True), axis=1, keepdims=True)
 
-    finish(CHUNKS - 2, PAIRS - 1, 0)
-    row_stats(PAIRS - 2)
-    row_fwd(PAIRS - 2).start()
     r_parts = [total_of(rsum[2 * t:2 * t + 2, :]) for t in range(2)]
     p_parts = [jnp.sum(psum[t:t + 1, :], axis=1, keepdims=True) for t in range(2)]
     for t in range(2):
         for core in range(2):
-            m_own[core, 2 * t + 1:2 * t + 2, :] = as_row(t_acc[t, core])
-    scale_own(PAIRS - 2)
-
+            m_own[0, core, t:t + 1, :] = as_row(t_acc[t, core])
+
+    def to_column(kind):
+        for z in range(4):
+            for fc in (1, 0):
+                def send_it(z=z, fc=fc):
+                    remote(m_own.at[kind], m_in.at[2 * model + c, kind], send.at[7], last_r.at[0], (z, data + fc * (1 - 2 * c))).start()
+
+                if fc:
+                    send_it()
+                else:
+                    pl.when(model != z)(send_it)
+
+    to_column(0)
+    finish(CHUNKS - 2, PAIRS - 1, 0)
     finish(CHUNKS - 1, PAIRS - 1, 1)
     send_rows(PAIRS - 1)
     for t in range(2):
         for core in range(2):
             row = as_row(col_acc[t, core])
-            m_own[core, 2 * t:2 * t + 1, :] = jnp.where(lane == COLS, r_parts[t], jnp.where(lane == COLS + 1, p_parts[t], row))
-
-    columns = [(dz, fc) for dz in range(4) for fc in range(2) if dz + fc]
-
-    def column_msg(i):
-        dz, fc = columns[i]
-        slot = columns.index(((4 - dz) % 4, fc))
-        return remote(m_own, m_in.at[slot], send.at[7], last_r.at[0], column_id(dz, fc))
-
-    for i in (3, 4, 1, 2, 5, 6, 0):
-        column_msg(i).start()
+            m_own[1, core, t:t + 1, :] = jnp.where(lane == COLS, r_parts[t], jnp.where(lane == COLS + 1, p_parts[t], row))
+    to_column(1)
+    m_in[2 * model + c] = m_own[...]
     send_swap(PAIRS - 1)
 
     arrived(old_cols.at[:, c], in_sem.at[3])
     arrived(old_cols.at[:, oc], in_sem.at[4])
-    arrived(m_in, last_r.at[0])
-    total = m_own[...]
-    for i in range(len(columns)):
-        total = total + m_in[i]
+    arrived(m_in.at[0:7], last_r.at[0])
+    total = jnp.sum(m_in[...], axis=0)
     m_sum[...] = total
     r_firsts, p_cols, u_firsts, weights = [], [], [], []
     for t in range(2):
-        cols = total[0, 2 * t:2 * t + 1, :]
+        cols = total[1, 0, t:t + 1, :]
         r_first = jnp.sum(jnp.where(lane == COLS, cols, 0.0), axis=1, keepdims=True) / VOCAB
         u_first = jnp.zeros((1, COLS), jnp.float32)
         for core in range(2):
-            col_new = BETA_TWO * old_cols[t, core] + (1.0 - BETA_TWO) * (total[core, 2 * t:2 * t + 1, :COLS] / VOCAB)
+            col_new = BETA_TWO * old_cols[t, core] + (1.0 - BETA_TWO) * (total[1, core, t:t + 1, :COLS] / VOCAB)
             weight = r_first / col_new
-            u_first = u_first + total[core, 2 * t + 1:2 * t + 2, :COLS] * weight
+            u_first = u_first + total[0, core, t:t + 1, :COLS] * weight
             weights.append(jnp.sum(jnp.where(diag[:, :COLS], weight, 0.0), axis=1, keepdims=True))
         r_firsts.append(r_first)
         p_cols.append(jnp.sum(jnp.where(lane == COLS + 1, cols, 0.0), axis=1, keepdims=True))
         u_firsts.append(0.125 * jnp.sum(u_first, axis=1, keepdims=True))
 
-    row_new = new_rows(PAIRS - 1)
-    inv = 1.0 / row_new
+    late = (PAIRS - 2, PAIRS - 1)
+    row_new = [new_rows(q) for q in late]
+    inv = [1.0 / r for r in row_new]
     message = jnp.zeros((1, LANES), jnp.float32)
     for t in range(2):
         acc = jnp.zeros((COLS, LANES), jnp.float32)
         for core in range(2):
-            for i in range(2):
-                g = in2[2 * (PAIRS - 1) + i, t, core]
-                acc = acc + (g * g) * inv[2 * t + i:2 * t + i + 1, :] * weights[2 * t + core]
-        r_mean = 0.03125 * r_firsts[t] + 0.25 * total_of(row_new[2 * t:2 * t + 2, :]) / VOCAB
+            part = jnp.zeros((COLS, LANES), jnp.float32)
+            for q, r in zip(late, inv):
+                for i in range(2):
+                    g = in2[2 * q + i, t, core]
+                    part = part + (g * g) * r[2 * t + i:2 * t + i + 1, :]
+            acc = acc + part * weights[2 * t + core]
+        r_mean = 0.03125 * r_firsts[t] + 0.25 * total_of((row_new[0] + row_new[1])[2 * t:2 * t + 2, :]) / VOCAB
         for i, value in enumerate((u_firsts[t] + total_of(acc), 0.125 * p_cols[t], r_mean)):
             message = jnp.where(lane == 3 * t + i, value, message)
     s_own[...] = message
 
-    others = [(dz, fy, fx, fc) for dz in range(4) for fy in range(2) for fx in range(2) for fc in range(2) if dz + fy + fx + fc]
-
-    def scalar_msg(i):
-        dz, fy, fx, fc = others[i]
-        slot = others.index(((4 - dz) % 4, fy, fx, fc))
-        return remote(s_own, s_in.at[slot], send.at[9], last_r.at[1], ((model + dz) % 4, plane_id(fy, fx, fc)[1]))
-
-    for i in sorted(range(len(others)), key=lambda i: -sum(others[i][1:3])):
-        scalar_msg(i).start()
-    row_fwd(PAIRS - 1).start()
-    scale_own(PAIRS - 1)
+    me = 8 * model + data
+    s_in[me] = message
+    for z in range(4):
+        for fy, fx, fc in ((1, 1, 1), (1, 1, 0), (0, 1, 1), (1, 0, 1), (0, 1, 0), (1, 0, 0), (0, 0, 1), (0, 0, 0)):
+            def send_it(z=z, fy=fy, fx=fx, fc=fc):
+                remote(s_own, s_in.at[me], send.at[9], last_r.at[1], (z, plane_id(fy, fx, fc)[1])).start()
+
+            if fy + fx + fc:
+                send_it()
+            else:
+                pl.when(model != z)(send_it)
+
+    for q in late:
+        row_fwd(q).start()
+        scale_own(q)
 
     factor_cols = []
     for t, c_out in enumerate((emb_cols_out, head_cols_out)):
-        cols = m_sum[c, 2 * t:2 * t + 1, :]
+        cols = m_sum[1, c, t:t + 1, :]
         col_new = BETA_TWO * old_cols[t, c] + (1.0 - BETA_TWO) * (cols[:, :COLS] / VOCAB)
         c_out[...] = col_new
         factor_cols.append(jnp.sum(jnp.where(diag[:, :COLS], lax.rsqrt(col_new), 0.0), axis=1, keepdims=True))
@@ -453,10 +466,10 @@
     arrived(peer, send.at[4])
     arrived(rp_in, send.at[5])
     arrived(rows.at[0:PAIRS], send.at[6])
-    arrived(m_in, send.at[7])
+    arrived(m_in.at[0:7], send.at[7])
     arrived(old_cols.at[:, c], send.at[8])
-    arrived(s_in, last_r.at[1])
-    message = s_own[...] + jnp.sum(s_in[...], axis=0)
+    arrived(s_in.at[0:31], last_r.at[1])
+    message = jnp.sum(s_in[...], axis=0)
     count = float(VOCAB * EMBED)
     for t in range(2):
         u_sq, p_sq, r_mean = [jnp.sum(jnp.where(lane == 3 * t + i, message, 0.0), axis=1, keepdims=True) for i in range(3)]
@@ -464,7 +477,7 @@
         p_rms = jnp.sqrt(p_sq / count)
         step = LEARN_RATE * jnp.maximum(SCALE_FLOOR, p_rms) / jnp.maximum(1.0, u_rms / CLIP_LIMIT)
         scale_out[t] = jnp.broadcast_to(factor_cols[t] * (step * jnp.sqrt(r_mean)), (COLS, LANES))
-    arrived(s_in, send.at[9])
+    arrived(s_in.at[0:31], send.at[9])
 
 
 def update_kernel(emb_g, head_g, emb_p, head_p, emb_rows, head_rows, emb_cols, head_cols, scale,
@@ -474,15 +487,16 @@
         ((emb_rows, emb_rows_new), (head_rows, head_rows_new), (emb_cols, emb_cols_new), (head_cols, head_cols_new)))]
     for cp in small:
         cp.start()
-    size = COLS // PARTS
+    size = ROWS // PARTS
+    tables = ((emb_p, emb_g, emb_new, emb_half), (head_p, head_g, head_new, head_half))
     for i in range(PARTS):
         part = slice(i * size, (i + 1) * size)
-        for t, (p, g, new, half) in enumerate(((emb_p, emb_g, emb_new, emb_half), (head_p, head_g, head_new, head_half))):
-            value = p[part, :] - g[part, :] * scale[t, part, 0:1]
-            new_buf[t, part, :] = value
-            half_buf[t, part, :] = value.astype(jnp.bfloat16)
-            pltpu.make_async_copy(new_buf.at[t, part, :], new.at[part, :], big_sem.at[0]).start()
-            pltpu.make_async_copy(half_buf.at[t, part, :], half.at[part, :], big_sem.at[1]).start()
+        for t, (p, g, new, half) in enumerate(tables):
+            value = p[:, part] - g[:, part] * scale[t, :, 0:1]
+            new_buf[t, :, part] = value
+            half_buf[t, :, part] = value.astype(jnp.bfloat16)
+            pltpu.make_async_copy(new_buf.at[t, :, part], new.at[:, part], big_sem.at[0]).start()
+            pltpu.make_async_copy(half_buf.at[t, :, part], half.at[:, part], big_sem.at[1]).start()
     for cp in small:
         cp.wait()
     pltpu.make_async_copy(new_buf, new_buf, big_sem.at[0]).wait()
@@ -504,7 +518,7 @@
     shapes += [(BLOCKS, 4, LANES), (2, *rows_shape), (2, 2, 1, COLS)]
     shapes += [(PAIRS, 4, LANES), (PAIRS, 3, 4, LANES)]
     shapes += [(2, 2, COLS, LANES)] * 2 + [(4, LANES), (2, LANES)]
-    shapes += [(2, 4, LANES), (7, 2, 4, LANES), (2, 4, LANES), (1, LANES), (31, 1, LANES)]
+    shapes += [(2, 2, 2, LANES), (8, 2, 2, 2, LANES), (2, 2, 2, LANES), (1, LANES), (32, 1, LANES)]
     scratch = [pltpu.VMEM(shape, f32) for shape in shapes]
     scratch += [dma((len(GROUPS) + 1,))] * 2 + [dma((RING,))] * 2 + [dma((SHORT,))] * 3
     scratch += [dma((10,)), dma((2,)), dma((5,)), pltpu.SemaphoreType.REGULAR((2,))]

time: 121 us -> 121 us (level)
  no operation moved by 1% of the time
where the time goes in v9:
time: 121 us
  Pallas kernels  120 us (99%)
    pallas_call x1, Pallas kernels, local_step(): pl.pallas_call(exchange_kernel, out_shape=tuple(kept), in_specs=[hbm] * 8...  118 us

profile of v9, /device:TPU:0, one launch (start us, length us, event | category | flops | bytes accessed | tf_op | source)
XLA Modules:
  0.0 120.5 jit_solution(2762009026191411293)
XLA Ops:
  0.6 117.6 %exchange.1 = (f32[96,4096]{1,0:T(8,128)S(1)}, f32[96,4096]{1,0:T(8,128)S(1)}, f32[96,4096]{1,0:T(8,128)S(1)}, f32[96,4096]{1,0:T(8,128)S(1)}, f32[16,2,128]{2,1...) custom-call(f32[4096,768]{1,0:T(8,128)} %bitcast.13, ...), custom_call_target="tpu_custom_call" | custom-call | tf_op jit(solution)/shard_map/exchange/pallas_call | solution.py:527
  118.2 2.3 %update.1 = (f32[96,4096]{1,0:T(8,128)}, f32[96,4096]{1,0:T(8,128)}, f32[16,2,128]{2,1,0:T(2,128)}, f32[16,2,128]{2,1,0:T(2,128)}, f32[1,96]{1,0:T(1,128)}, /*in...) custom-call(f32[96,4096]{1,0:T(8,128)S(1)} %get-tuple-element.25.emb_g, ...), custom_call_target="tpu_custom_call" | custom-call | tf_op jit(solution)/shard_map/update/pallas_call | solution.py:538

commit v10 on v9

--- a/solution.py
+++ b/solution.py
@@ -364,12 +364,6 @@
     def total_of(v):
         return jnp.sum(jnp.sum(v, axis=0, keepdims=True), axis=1, keepdims=True)
 
-    r_parts = [total_of(rsum[2 * t:2 * t + 2, :]) for t in range(2)]
-    p_parts = [jnp.sum(psum[t:t + 1, :], axis=1, keepdims=True) for t in range(2)]
-    for t in range(2):
-        for core in range(2):
-            m_own[0, core, t:t + 1, :] = as_row(t_acc[t, core])
-
     def to_column(kind):
         for z in range(4):
             for fc in (1, 0):
@@ -381,69 +375,88 @@
                 else:
                     pl.when(model != z)(send_it)
 
-    to_column(0)
+    def send_weighted():
+        for t in range(2):
+            r_part = total_of(rsum[2 * t:2 * t + 2, :])
+            p_part = jnp.sum(psum[t:t + 1, :], axis=1, keepdims=True)
+            for core in range(2):
+                row = as_row(t_acc[t, core])
+                row = jnp.where(lane == COLS, r_part, jnp.where(lane == COLS + 1, p_part, row))
+                m_own[0, core, t:t + 1, :] = row
+        to_column(0)
+
+    late = (PAIRS - 2, PAIRS - 1)
+
+    pl.when(c == 1)(send_weighted)
     finish(CHUNKS - 2, PAIRS - 1, 0)
     finish(CHUNKS - 1, PAIRS - 1, 1)
     send_rows(PAIRS - 1)
     for t in range(2):
         for core in range(2):
-            row = as_row(col_acc[t, core])
-            m_own[1, core, t:t + 1, :] = jnp.where(lane == COLS, r_parts[t], jnp.where(lane == COLS + 1, p_parts[t], row))
+            m_own[1, core, t:t + 1, :] = as_row(col_acc[t, core])
     to_column(1)
+    send_swap(PAIRS - 1)
+
+    @pl.when(c == 0)
+    def _():
+        for q in late:
+            row_stats(q)
+            row_fwd(q).start()
+        send_weighted()
+
     m_in[2 * model + c] = m_own[...]
-    send_swap(PAIRS - 1)
-
     arrived(old_cols.at[:, c], in_sem.at[3])
     arrived(old_cols.at[:, oc], in_sem.at[4])
     arrived(m_in.at[0:7], last_r.at[0])
     total = jnp.sum(m_in[...], axis=0)
     m_sum[...] = total
-    r_firsts, p_cols, u_firsts, weights = [], [], [], []
-    for t in range(2):
-        cols = total[1, 0, t:t + 1, :]
-        r_first = jnp.sum(jnp.where(lane == COLS, cols, 0.0), axis=1, keepdims=True) / VOCAB
-        u_first = jnp.zeros((1, COLS), jnp.float32)
-        for core in range(2):
-            col_new = BETA_TWO * old_cols[t, core] + (1.0 - BETA_TWO) * (total[1, core, t:t + 1, :COLS] / VOCAB)
-            weight = r_first / col_new
-            u_first = u_first + total[0, core, t:t + 1, :COLS] * weight
-            weights.append(jnp.sum(jnp.where(diag[:, :COLS], weight, 0.0), axis=1, keepdims=True))
-        r_firsts.append(r_first)
-        p_cols.append(jnp.sum(jnp.where(lane == COLS + 1, cols, 0.0), axis=1, keepdims=True))
-        u_firsts.append(0.125 * jnp.sum(u_first, axis=1, keepdims=True))
-
-    late = (PAIRS - 2, PAIRS - 1)
-    row_new = [new_rows(q) for q in late]
-    inv = [1.0 / r for r in row_new]
-    message = jnp.zeros((1, LANES), jnp.float32)
-    for t in range(2):
-        acc = jnp.zeros((COLS, LANES), jnp.float32)
-        for core in range(2):
-            part = jnp.zeros((COLS, LANES), jnp.float32)
-            for q, r in zip(late, inv):
-                for i in range(2):
-                    g = in2[2 * q + i, t, core]
-                    part = part + (g * g) * r[2 * t + i:2 * t + i + 1, :]
-            acc = acc + part * weights[2 * t + core]
-        r_mean = 0.03125 * r_firsts[t] + 0.25 * total_of((row_new[0] + row_new[1])[2 * t:2 * t + 2, :]) / VOCAB
-        for i, value in enumerate((u_firsts[t] + total_of(acc), 0.125 * p_cols[t], r_mean)):
-            message = jnp.where(lane == 3 * t + i, value, message)
-    s_own[...] = message
-
-    me = 8 * model + data
-    s_in[me] = message
-    for z in range(4):
-        for fy, fx, fc in ((1, 1, 1), (1, 1, 0), (0, 1, 1), (1, 0, 1), (0, 1, 0), (1, 0, 0), (0, 0, 1), (0, 0, 0)):
-            def send_it(z=z, fy=fy, fx=fx, fc=fc):
-                remote(s_own, s_in.at[me], send.at[9], last_r.at[1], (z, plane_id(fy, fx, fc)[1])).start()
-
-            if fy + fx + fc:
-                send_it()
-            else:
-                pl.when(model != z)(send_it)
+    firsts = total[0, 0]
+    r_firsts = [jnp.sum(jnp.where(lane == COLS, firsts[t:t + 1, :], 0.0), axis=1, keepdims=True) / VOCAB for t in range(2)]
+    chip = 4 * model + data // 2
+
+    @pl.when(c == 1)
+    def _():
+        message = jnp.zeros((1, LANES), jnp.float32)
+        u_firsts, weights = [], []
+        for t in range(2):
+            u_first = jnp.zeros((1, COLS), jnp.float32)
+            for core in range(2):
+                col_new = BETA_TWO * old_cols[t, core] + (1.0 - BETA_TWO) * (m_sum[1, core, t:t + 1, :COLS] / VOCAB)
+                weight = r_firsts[t] / col_new
+                u_first = u_first + m_sum[0, core, t:t + 1, :COLS] * weight
+                weights.append(jnp.sum(jnp.where(diag[:, :COLS], weight, 0.0), axis=1, keepdims=True))
+            u_firsts.append(0.25 * jnp.sum(u_first, axis=1, keepdims=True))
+        row_new = [new_rows(q) for q in late]
+        inv = [1.0 / r for r in row_new]
+        for t in range(2):
+            acc = jnp.zeros((COLS, LANES), jnp.float32)
+            for core in range(2):
+                part = jnp.zeros((COLS, LANES), jnp.float32)
+                for q, r in zip(late, inv):
+                    for i in range(2):
+                        g = in2[2 * q + i, t, core]
+                        part = part + (g * g) * r[2 * t + i:2 * t + i + 1, :]
+                acc = acc + part * weights[2 * t + core]
+            r_mean = 0.0625 * r_firsts[t] + 0.25 * total_of((row_new[0] + row_new[1])[2 * t:2 * t + 2, :]) / VOCAB
+            p_col = 0.25 * jnp.sum(jnp.where(lane == COLS + 1, m_sum[0, 0, t:t + 1, :], 0.0), axis=1, keepdims=True)
+            for i, value in enumerate((u_firsts[t] + total_of(acc), p_col, r_mean)):
+                message = jnp.where(lane == 3 * t + i, value, message)
+        s_own[...] = message
+        s_in[chip] = message
+        for z in range(4):
+            for fy, fx, fc in ((1, 1, 1), (1, 1, 0), (0, 1, 1), (1, 0, 1), (0, 1, 0), (1, 0, 0), (0, 0, 1), (0, 0, 0)):
+                def send_it(z=z, fy=fy, fx=fx, fc=fc):
+                    remote(s_own, s_in.at[chip], send.at[9], last_r.at[1], (z, plane_id(fy, fx, fc)[1])).start()
+
+                if fy + fx + fc:
+                    send_it()
+                else:
+                    pl.when(model != z)(send_it)
+
+        for q in late:
+            row_fwd(q).start()
 
     for q in late:
-        row_fwd(q).start()
         scale_own(q)
 
     factor_cols = []
@@ -468,8 +481,16 @@
     arrived(rows.at[0:PAIRS], send.at[6])
     arrived(m_in.at[0:7], send.at[7])
     arrived(old_cols.at[:, c], send.at[8])
-    arrived(s_in.at[0:31], last_r.at[1])
-    message = jnp.sum(s_in[...], axis=0)
+
+    @pl.when(c == 0)
+    def _():
+        arrived(s_in.at[0:16], last_r.at[1])
+
+    @pl.when(c == 1)
+    def _():
+        arrived(s_in.at[0:15], last_r.at[1])
+
+    message = jnp.sum(s_in[0:16], axis=0)
     count = float(VOCAB * EMBED)
     for t in range(2):
         u_sq, p_sq, r_mean = [jnp.sum(jnp.where(lane == 3 * t + i, message, 0.0), axis=1, keepdims=True) for i in range(3)]
@@ -477,7 +498,10 @@
         p_rms = jnp.sqrt(p_sq / count)
         step = LEARN_RATE * jnp.maximum(SCALE_FLOOR, p_rms) / jnp.maximum(1.0, u_rms / CLIP_LIMIT)
         scale_out[t] = jnp.broadcast_to(factor_cols[t] * (step * jnp.sqrt(r_mean)), (COLS, LANES))
-    arrived(s_in.at[0:31], send.at[9])
+
+    @pl.when(c == 1)
+    def _():
+        arrived(s_in.at[0:31], send.at[9])
 
 
 def update_kernel(emb_g, head_g, emb_p, head_p, emb_rows, head_rows, emb_cols, head_cols, scale,

time: 121 us -> 120 us (level)
  no operation moved by 1% of the time
where the time goes in v10:
time: 120 us
  Pallas kernels  120 us (100%)
    pallas_call x1, Pallas kernels, local_step(): pl.pallas_call(exchange_kernel, out_shape=tuple(kept), in_specs=[hbm] * 8...  117 us

profile of v10, /device:TPU:0, one launch (start us, length us, event | category | flops | bytes accessed | tf_op | source)
XLA Modules:
  0.0 120.1 jit_solution(534490496426376170)
XLA Ops:
  0.6 117.2 %exchange.1 = (f32[96,4096]{1,0:T(8,128)S(1)}, f32[96,4096]{1,0:T(8,128)S(1)}, f32[96,4096]{1,0:T(8,128)S(1)}, f32[96,4096]{1,0:T(8,128)S(1)}, f32[16,2,128]{2,1...) custom-call(f32[4096,768]{1,0:T(8,128)} %bitcast.13, ...), custom_call_target="tpu_custom_call" | custom-call | tf_op jit(solution)/shard_map/exchange/pallas_call | solution.py:551
  117.8 2.3 %update.1 = (f32[96,4096]{1,0:T(8,128)}, f32[96,4096]{1,0:T(8,128)}, f32[16,2,128]{2,1,0:T(2,128)}, f32[16,2,128]{2,1,0:T(2,128)}, f32[1,96]{1,0:T(1,128)}, /*in...) custom-call(f32[96,4096]{1,0:T(8,128)S(1)} %get-tuple-element.25.emb_g, ...), custom_call_target="tpu_custom_call" | custom-call | tf_op jit(solution)/shard_map/update/pallas_call | solution.py:562

commit v11 on v10

--- a/solution.py
+++ b/solution.py
@@ -408,10 +408,7 @@
     arrived(old_cols.at[:, c], in_sem.at[3])
     arrived(old_cols.at[:, oc], in_sem.at[4])
     arrived(m_in.at[0:7], last_r.at[0])
-    total = jnp.sum(m_in[...], axis=0)
-    m_sum[...] = total
-    firsts = total[0, 0]
-    r_firsts = [jnp.sum(jnp.where(lane == COLS, firsts[t:t + 1, :], 0.0), axis=1, keepdims=True) / VOCAB for t in range(2)]
+    m_sum[...] = jnp.sum(m_in[...], axis=0)
     chip = 4 * model + data // 2
 
     @pl.when(c == 1)
@@ -422,7 +419,7 @@
             u_first = jnp.zeros((1, COLS), jnp.float32)
             for core in range(2):
                 col_new = BETA_TWO * old_cols[t, core] + (1.0 - BETA_TWO) * (m_sum[1, core, t:t + 1, :COLS] / VOCAB)
-                weight = r_firsts[t] / col_new
+                weight = 1.0 / col_new
                 u_first = u_first + m_sum[0, core, t:t + 1, :COLS] * weight
                 weights.append(jnp.sum(jnp.where(diag[:, :COLS], weight, 0.0), axis=1, keepdims=True))
             u_firsts.append(0.25 * jnp.sum(u_first, axis=1, keepdims=True))
@@ -437,9 +434,9 @@
                         g = in2[2 * q + i, t, core]
                         part = part + (g * g) * r[2 * t + i:2 * t + i + 1, :]
                 acc = acc + part * weights[2 * t + core]
-            r_mean = 0.0625 * r_firsts[t] + 0.25 * total_of((row_new[0] + row_new[1])[2 * t:2 * t + 2, :]) / VOCAB
-            p_col = 0.25 * jnp.sum(jnp.where(lane == COLS + 1, m_sum[0, 0, t:t + 1, :], 0.0), axis=1, keepdims=True)
-            for i, value in enumerate((u_firsts[t] + total_of(acc), p_col, r_mean)):
+            r_early, p_col = [jnp.sum(jnp.where(lane == COLS + i, m_sum[0, 0, t:t + 1, :], 0.0), axis=1, keepdims=True) for i in range(2)]
+            r_mean = (0.0625 * r_early + 0.25 * total_of((row_new[0] + row_new[1])[2 * t:2 * t + 2, :])) / VOCAB
+            for i, value in enumerate((u_firsts[t] + total_of(acc), 0.25 * p_col, r_mean)):
                 message = jnp.where(lane == 3 * t + i, value, message)
         s_own[...] = message
         s_in[chip] = message
@@ -494,7 +491,7 @@
     count = float(VOCAB * EMBED)
     for t in range(2):
         u_sq, p_sq, r_mean = [jnp.sum(jnp.where(lane == 3 * t + i, message, 0.0), axis=1, keepdims=True) for i in range(3)]
-        u_rms = jnp.sqrt(u_sq * (r_mean / r_firsts[t]) / count)
+        u_rms = jnp.sqrt(u_sq * r_mean / count)
         p_rms = jnp.sqrt(p_sq / count)
         step = LEARN_RATE * jnp.maximum(SCALE_FLOOR, p_rms) / jnp.maximum(1.0, u_rms / CLIP_LIMIT)
         scale_out[t] = jnp.broadcast_to(factor_cols[t] * (step * jnp.sqrt(r_mean)), (COLS, LANES))

time: 120 us -> 120 us (level)
  no operation moved by 1% of the time
where the time goes in v11:
time: 120 us
  Pallas kernels  119 us (99%)
    pallas_call x1, Pallas kernels, local_step(): pl.pallas_call(exchange_kernel, out_shape=tuple(kept), in_specs=[hbm] * 8...  117 us

profile of v11, /device:TPU:0, one launch (start us, length us, event | category | flops | bytes accessed | tf_op | source)
XLA Modules:
  0.0 120.1 jit_solution(8893576208364863201)
XLA Ops:
  0.6 117.1 %exchange.1 = (f32[96,4096]{1,0:T(8,128)S(1)}, f32[96,4096]{1,0:T(8,128)S(1)}, f32[96,4096]{1,0:T(8,128)S(1)}, f32[96,4096]{1,0:T(8,128)S(1)}, f32[16,2,128]{2,1...) custom-call(f32[4096,768]{1,0:T(8,128)} %bitcast.13, ...), custom_call_target="tpu_custom_call" | custom-call | tf_op jit(solution)/shard_map/exchange/pallas_call | solution.py:548
  117.7 2.3 %update.1 = (f32[96,4096]{1,0:T(8,128)}, f32[96,4096]{1,0:T(8,128)}, f32[16,2,128]{2,1,0:T(2,128)}, f32[16,2,128]{2,1,0:T(2,128)}, f32[1,96]{1,0:T(1,128)}, /*in...) custom-call(f32[96,4096]{1,0:T(8,128)S(1)} %get-tuple-element.25.emb_g, ...), custom_call_target="tpu_custom_call" | custom-call | tf_op jit(solution)/shard_map/update/pallas_call | solution.py:559

commit v12 on v11

--- a/solution.py
+++ b/solution.py
@@ -27,7 +27,9 @@
 AHEAD = 2
 RING = 6
 SHORT = 4
-PARTS = 8
+SWAPS = 5
+RELAY = 5
+PARTS = 16
 MESH = pl.DeviceIdType.MESH
 PLANE = ((0, 1), (1, 0), (1, 1))
 
@@ -35,8 +37,8 @@
 def exchange_kernel(emb_ref, head_ref, emb_p_ref, head_p_ref, emb_r_ref, head_r_ref, emb_c_ref, head_c_ref,
                     stage_e, stage_h, par_e, par_h, emb_rows_out, head_rows_out, emb_cols_out, head_cols_out, scale_out,
                     both_e, sum_e, both_h, in1, in2, peer,
-                    rows, old_rows, old_cols, rp_own, rp_in, col_acc, t_acc, rsum, psum, m_own, m_in, m_sum, s_own, s_in,
-                    s0e_r, s0h_r, s1_r, s2_r, swap_r, rp_r, fw_r, send, last_r, in_sem, token):
+                    rows, old_rows, old_cols, rp_own, rp_sum, rp_in, col_acc, t_acc, rsum, psum, m_own, m_in, m_sum, s_own, s_in,
+                    s0e_r, s0h_r, s1_r, s2_r, swap_r, rp_r, ry_r, fw_r, send, last_r, in_sem, token):
     model = lax.axis_index("model")
     data = lax.axis_index("data")
     c = data % 2
@@ -103,15 +105,18 @@
         return remote(in1.at[k, 1, oy], in2.at[k, 1], send.at[3], s2_r.at[k % RING], y_peer)
 
     def swap(q):
-        return [remote(in2.at[pl.ds(2 * q, 2), t, oc], peer.at[q, t], send.at[4], swap_r.at[q % SHORT], core_peer)
+        return [remote(in2.at[pl.ds(2 * q, 2), t, oc], peer.at[q, t], send.at[4], swap_r.at[q % SWAPS], core_peer)
                 for t in range(2)]
 
     def row_msg(q, i):
         fy, fx = PLANE[i]
-        return remote(rp_own.at[q], rp_in.at[q, i], send.at[5], rp_r.at[q % SHORT], plane_id(fy, fx, 0))
+        return remote(rp_own.at[q], rp_in.at[3 * q + i], send.at[5], rp_r.at[q % SHORT], plane_id(fy, fx, 0))
+
+    def sum_msg(q):
+        return remote(rp_sum.at[q], rp_in.at[3 * q + 1], send.at[5], ry_r.at[q % SHORT], y_peer)
 
     def row_fwd(q):
-        return remote(rows.at[c * PAIRS + q], rows.at[c * PAIRS + q], send.at[6], fw_r.at[q % SHORT], core_peer)
+        return remote(rows.at[c * PAIRS + q], rows.at[c * PAIRS + q], send.at[6], fw_r.at[q % SWAPS], core_peer)
 
     small_loads = [pltpu.make_async_copy(src, dst, in_sem.at[i]) for i, (src, dst) in (
         (0, (emb_p_ref, par_e)), (1, (head_p_ref, par_h)), (2, (emb_r_ref, old_rows.at[0])), (2, (head_r_ref, old_rows.at[1])),
@@ -219,17 +224,28 @@
         for cp in swap(q):
             cp.start()
 
-    def new_rows(q):
-        arrived(rp_in.at[q], rp_r.at[q % SHORT])
+    def relay_rows(q):
+        row_msg(q, 0).wait_recv()
+        rp_sum[q] = rp_own[q] + rp_in[3 * q]
+        sum_msg(q).start()
+
+    def new_rows(q, relayed=False):
+        if relayed:
+            sum_msg(q).wait_recv()
+        else:
+            arrived(rp_in.at[pl.ds(3 * q, 3)], rp_r.at[q % SHORT])
         block = c * PAIRS + q
-        row_sq = (rp_own[q] + rp_in[q, 0]) + (rp_in[q, 1] + rp_in[q, 2])
+        if relayed:
+            row_sq = rp_sum[q] + rp_in[3 * q + 1]
+        else:
+            row_sq = (rp_own[q] + rp_in[3 * q]) + (rp_in[3 * q + 1] + rp_in[3 * q + 2])
         old = jnp.concatenate([old_rows[0, block], old_rows[1, block]], axis=0)
         row_new = BETA_TWO * old + (1.0 - BETA_TWO) * (row_sq / EMBED)
         rows[block] = row_new
         return row_new
 
-    def row_stats(q):
-        row_new = new_rows(q)
+    def row_stats(q, relayed=False):
+        row_new = new_rows(q, relayed)
         rsum[...] = rsum[...] + row_new
         inv = 1.0 / row_new
         for t in range(2):
@@ -251,8 +267,8 @@
         scale_rows(c * PAIRS + q, lambda t, i: in2[2 * q + i, t, c])
 
     def scale_peer(q):
-        arrived(rows.at[oc * PAIRS + q], fw_r.at[q % SHORT])
-        arrived(peer.at[q], swap_r.at[q % SHORT])
+        arrived(rows.at[oc * PAIRS + q], fw_r.at[q % SWAPS])
+        arrived(peer.at[q], swap_r.at[q % SWAPS])
         scale_rows(oc * PAIRS + q, lambda t, i: peer[q, t, i])
 
     def param_sq(k):
@@ -341,18 +357,34 @@
         @pl.when((k >= 3) & (k % 2 == 1))
         def _():
             finish(k - 2, pair - 1, 1)
-            send_rows(pair - 1)
+
+            @pl.when(pair - 1 < RELAY)
+            def _():
+                row_msg(pair - 1, 0).start()
+
+            @pl.when(pair - 1 >= RELAY)
+            def _():
+                send_rows(pair - 1)
+
             send_swap(pair - 1)
 
+        @pl.when((k >= 9) & (k % 2 == 1))
+        def _():
+            scale_peer(pair - 4)
+
+        @pl.when((k >= 5) & (k % 2 == 1) & (pair - 2 < RELAY))
+        def _():
+            relay_rows(pair - 2)
+
         @pl.when((k >= 7) & (k % 2 == 1))
         def _():
-            scale_peer(pair - 3)
-
-        @pl.when((k >= 5) & (k % 2 == 1))
-        def _():
-            row_stats(pair - 2)
-            row_fwd(pair - 2).start()
-            scale_own(pair - 2)
+            row_stats(pair - 3, True)
+            row_fwd(pair - 3).start()
+            scale_own(pair - 3)
+
+    row_stats(PAIRS - 3)
+    row_fwd(PAIRS - 3).start()
+    scale_own(PAIRS - 3)
 
     lane = lax.broadcasted_iota(jnp.int32, (1, LANES), 1)
     diag = lax.broadcasted_iota(jnp.int32, (COLS, LANES), 0) == lax.broadcasted_iota(jnp.int32, (COLS, LANES), 1)
@@ -463,7 +495,7 @@
         c_out[...] = col_new
         factor_cols.append(jnp.sum(jnp.where(diag[:, :COLS], lax.rsqrt(col_new), 0.0), axis=1, keepdims=True))
 
-    @pl.loop(PAIRS - 3, PAIRS)
+    @pl.loop(PAIRS - 4, PAIRS)
     def _(q):
         scale_peer(q)
 
@@ -474,7 +506,7 @@
     arrived(in1, send.at[2])
     arrived(in2, send.at[3])
     arrived(peer, send.at[4])
-    arrived(rp_in, send.at[5])
+    arrived(rp_in.at[0:2 * RELAY + 3 * (PAIRS - RELAY)], send.at[5])
     arrived(rows.at[0:PAIRS], send.at[6])
     arrived(m_in.at[0:7], send.at[7])
     arrived(old_cols.at[:, c], send.at[8])
@@ -537,11 +569,11 @@
     shapes = [(2, ROWS // 2, EMBED), (n, 2, 2, 2, COLS, LANES), (2, n, 2, 2, 2, COLS, LANES)]
     shapes += [(n, 2, 2, 2, COLS, LANES), (n, 2, 2, COLS, LANES), (PAIRS, 2, 2, COLS, LANES)]
     shapes += [(BLOCKS, 4, LANES), (2, *rows_shape), (2, 2, 1, COLS)]
-    shapes += [(PAIRS, 4, LANES), (PAIRS, 3, 4, LANES)]
+    shapes += [(PAIRS, 4, LANES), (PAIRS, 4, LANES), (3 * PAIRS, 4, LANES)]
     shapes += [(2, 2, COLS, LANES)] * 2 + [(4, LANES), (2, LANES)]
     shapes += [(2, 2, 2, LANES), (8, 2, 2, 2, LANES), (2, 2, 2, LANES), (1, LANES), (32, 1, LANES)]
     scratch = [pltpu.VMEM(shape, f32) for shape in shapes]
-    scratch += [dma((len(GROUPS) + 1,))] * 2 + [dma((RING,))] * 2 + [dma((SHORT,))] * 3
+    scratch += [dma((len(GROUPS) + 1,))] * 2 + [dma((RING,))] * 2 + [dma((SWAPS,))] + [dma((SHORT,))] * 2 + [dma((SWAPS,))]
     scratch += [dma((10,)), dma((2,)), dma((5,)), pltpu.SemaphoreType.REGULAR((2,))]
     kept = [pltpu.VMEM((COLS, ROWS), f32)] * 4 + [pltpu.VMEM(rows_shape, f32)] * 2 + [pltpu.VMEM((1, COLS), f32)] * 2
     kept.append(pltpu.VMEM((2, COLS, LANES), f32))

time: 120 us -> 120 us (level)
  no operation moved by 1% of the time
where the time goes in v12:
time: 120 us
  Pallas kernels  119 us (99%)
    pallas_call x1, Pallas kernels, local_step(): pl.pallas_call(exchange_kernel, out_shape=tuple(kept), in_specs=[hbm] * 8...  117 us

profile of v12, /device:TPU:0, one launch (start us, length us, event | category | flops | bytes accessed | tf_op | source)
XLA Modules:
  0.0 119.9 jit_solution(6731690928270569935)
XLA Ops:
  0.6 116.9 %exchange.1 = (f32[96,4096]{1,0:T(8,128)S(1)}, f32[96,4096]{1,0:T(8,128)S(1)}, f32[96,4096]{1,0:T(8,128)S(1)}, f32[96,4096]{1,0:T(8,128)S(1)}, f32[16,2,128]{2,1...) custom-call(f32[4096,768]{1,0:T(8,128)} %bitcast.13, ...), custom_call_target="tpu_custom_call" | custom-call | tf_op jit(solution)/shard_map/exchange/pallas_call | solution.py:580
  117.6 2.3 %update.1 = (f32[96,4096]{1,0:T(8,128)}, f32[96,4096]{1,0:T(8,128)}, f32[16,2,128]{2,1,0:T(2,128)}, f32[16,2,128]{2,1,0:T(2,128)}, f32[1,96]{1,0:T(1,128)}, /*in...) custom-call(f32[96,4096]{1,0:T(8,128)S(1)} %get-tuple-element.25.emb_g, ...), custom_call_target="tpu_custom_call" | custom-call | tf_op jit(solution)/shard_map/update/pallas_call | solution.py:591

commit v13 on v12

--- a/solution.py
+++ b/solution.py
@@ -29,7 +29,7 @@
 SHORT = 4
 SWAPS = 5
 RELAY = 5
-PARTS = 16
+PARTS = 32
 MESH = pl.DeviceIdType.MESH
 PLANE = ((0, 1), (1, 0), (1, 1))
 
@@ -121,7 +121,7 @@
     small_loads = [pltpu.make_async_copy(src, dst, in_sem.at[i]) for i, (src, dst) in (
         (0, (emb_p_ref, par_e)), (1, (head_p_ref, par_h)), (2, (emb_r_ref, old_rows.at[0])), (2, (head_r_ref, old_rows.at[1])),
         (3, (emb_c_ref, old_cols.at[0, c])), (3, (head_c_ref, old_cols.at[1, c])))]
-    old_cols_out = [remote(src, old_cols.at[t, c], send.at[8], in_sem.at[4], core_peer)
+    old_cols_out = [remote(src, old_cols.at[t, c], send.at[8], in_sem.at[3], core_peer)
                     for t, src in enumerate((emb_c_ref, head_c_ref))]
 
     barrier = pltpu.get_barrier_semaphore()
@@ -437,8 +437,7 @@
         send_weighted()
 
     m_in[2 * model + c] = m_own[...]
-    arrived(old_cols.at[:, c], in_sem.at[3])
-    arrived(old_cols.at[:, oc], in_sem.at[4])
+    arrived(old_cols, in_sem.at[3])
     arrived(m_in.at[0:7], last_r.at[0])
     m_sum[...] = jnp.sum(m_in[...], axis=0)
     chip = 4 * model + data // 2
@@ -545,7 +544,7 @@
     for i in range(PARTS):
         part = slice(i * size, (i + 1) * size)
         for t, (p, g, new, half) in enumerate(tables):
-            value = p[:, part] - g[:, part] * scale[t, :, 0:1]
+            value = p[:, part] - g[:, part] * jnp.concatenate([scale[t]] * (size // LANES), axis=1)
             new_buf[t, :, part] = value
             half_buf[t, :, part] = value.astype(jnp.bfloat16)
             pltpu.make_async_copy(new_buf.at[t, :, part], new.at[:, part], big_sem.at[0]).start()
@@ -574,7 +573,7 @@
     shapes += [(2, 2, 2, LANES), (8, 2, 2, 2, LANES), (2, 2, 2, LANES), (1, LANES), (32, 1, LANES)]
     scratch = [pltpu.VMEM(shape, f32) for shape in shapes]
     scratch += [dma((len(GROUPS) + 1,))] * 2 + [dma((RING,))] * 2 + [dma((SWAPS,))] + [dma((SHORT,))] * 2 + [dma((SWAPS,))]
-    scratch += [dma((10,)), dma((2,)), dma((5,)), pltpu.SemaphoreType.REGULAR((2,))]
+    scratch += [dma((10,)), dma((2,)), dma((4,)), pltpu.SemaphoreType.REGULAR((2,))]
     kept = [pltpu.VMEM((COLS, ROWS), f32)] * 4 + [pltpu.VMEM(rows_shape, f32)] * 2 + [pltpu.VMEM((1, COLS), f32)] * 2
     kept.append(pltpu.VMEM((2, COLS, LANES), f32))
     state = pl.pallas_call(

time: 120 us -> 120 us (level)
  no operation moved by 1% of the time
where the time goes in v13:
time: 120 us
  Pallas kernels  119 us (99%)
    pallas_call x1, Pallas kernels, local_step(): pl.pallas_call(exchange_kernel, out_shape=tuple(kept), in_specs=[hbm] * 8...  117 us

profile of v13, /device:TPU:0, one launch (start us, length us, event | category | flops | bytes accessed | tf_op | source)
XLA Modules:
  0.0 119.8 jit_solution(9050233305722282659)
XLA Ops:
  0.6 116.9 %exchange.1 = (f32[96,4096]{1,0:T(8,128)S(1)}, f32[96,4096]{1,0:T(8,128)S(1)}, f32[96,4096]{1,0:T(8,128)S(1)}, f32[96,4096]{1,0:T(8,128)S(1)}, f32[16,2,128]{2,1...) custom-call(f32[4096,768]{1,0:T(8,128)} %bitcast.13, ...), custom_call_target="tpu_custom_call" | custom-call | tf_op jit(solution)/shard_map/exchange/pallas_call | solution.py:579
  117.6 2.2 %update.1 = (f32[96,4096]{1,0:T(8,128)}, f32[96,4096]{1,0:T(8,128)}, f32[16,2,128]{2,1,0:T(2,128)}, f32[16,2,128]{2,1,0:T(2,128)}, f32[1,96]{1,0:T(1,128)}, /*in...) custom-call(f32[96,4096]{1,0:T(8,128)S(1)} %get-tuple-element.25.emb_g, ...), custom_call_target="tpu_custom_call" | custom-call | tf_op jit(solution)/shard_map/update/pallas_call | solution.py:590
